TPU v7x, 256 devices: a whole 4x4x8 slice. The times are simulated.
256 devices in a mesh: seq: 32 (over y, z), batch: 8 (over x, core).
Axes of the slice: x: 4, y: 4, z: 8, core: 2. Of those that a mesh axis runs over, the one named last changes fastest.
Arguments:
- conv_input: bfloat16 [32768, 8192], P(('batch', 'seq')), parts along dimension 0, may hold values from -6 to 6
- gate_input: bfloat16 [32768, 8192], P(('batch', 'seq')), parts along dimension 0, may hold values from -6 to 6
- conv_weight: bfloat16 [4, 8192], P(None, 'seq'), may hold values from -3 to 3
- conv_bias: bfloat16 [8192], P('seq'), may hold values from -3 to 3
- x_weight: bfloat16 [8192, 288], P('seq'), may hold values from -0.0625 to 0.0625
- dt_gain: float32 [256], replicated, may hold values from 0.5 to 1.5
- dt_weight: bfloat16 [256, 8192], P(None, 'seq'), may hold values from -0.375 to 0.375
- dt_bias: float32 [8192], P('seq'), may hold values from -6.9 to -2.3
- a_log: float32 [16, 8192], P(None, 'seq'), may hold values from 0 to 2.77
- skip: float32 [8192], P('seq'), may hold values from 0.5 to 1.5
Outputs:
- mixed: bfloat16 [32768, 8192], P(('batch', 'seq')), parts along dimension 0
There are 8 independent parts, one for each index of `batch`. A program takes and returns all parts, laid end to end along the dimension named above; an argument that names none is the same for every part. Nothing has to cross between parts.
All inputs are finite; a program needn't handle non-finite values.
Results may differ from a plain program's by a relative error of at most 0.0085.
Values may be sent and summed in bfloat16 or wider, within the bound.
No kernel may reach another device: no remote copies, remote signals or barrier semaphores. Data moves between devices by JAX's collectives and lax.ppermute only.
A program may use at most 128 MiB of HBM per device.

v0:
```python
import jax
import jax.numpy as jnp
from jax import lax
from jax.sharding import PartitionSpec as P


def passed_along(value, axis, steps):
    count = lax.axis_size(axis)
    initial, last = (max(0, -steps), min(count, count - steps))
    return lax.ppermute(value, axis, [(source, source + steps) for source in range(initial, last)])


def from_everyone(x, axis):
    copies = jnp.broadcast_to(x, (lax.axis_size(axis), *x.shape))
    return lax.all_to_all(copies, axis, split_axis=0, concat_axis=0, tiled=True)


def joined_along(parts, dim):
    parts = jnp.moveaxis(parts, 0, dim)
    dims = parts.shape
    return parts.reshape(*dims[:dim], dims[dim] * dims[dim + 1], *dims[dim + 2 :])


def gather_directly(x, axis, dim):
    parts = from_everyone(x, axis)
    return joined_along(parts, dim)


def causal_conv(prefix, inputs, weight, bias):
    rows = inputs.shape[0]
    width = weight.shape[0]
    padded = jnp.concatenate([prefix, inputs.astype(jnp.float32)], 0)
    total = bias.astype(jnp.float32)[None, :]
    for tap in range(width):
        total = total + weight[tap].astype(jnp.float32)[None, :] * padded[tap : tap + rows]
    return jax.nn.silu(total).astype(jnp.bfloat16)


def link_blocks(earlier, later):
    return (earlier[0] * later[0], later[0] * earlier[1] + later[1])


def selective_scan(step, xfloat, bmat, cmat, rate):
    span = 16
    length, chans = step.shape
    states = rate.shape[0]
    blocks = length // span
    step_rows = step.reshape(blocks, span * chans)
    drive_rows = (step * xfloat).reshape(blocks, span * chans)
    b_rows = bmat.reshape(blocks, span * states)
    c_rows = cmat.reshape(blocks, span * states)
    state = jnp.zeros((blocks, states, chans), jnp.float32)
    running = jnp.zeros((blocks, chans), jnp.float32)
    local_parts = []
    elapsed = []
    for place in range(span):
        step_now = step_rows[:, place * chans : (place + 1) * chans]
        drive_now = drive_rows[:, place * chans : (place + 1) * chans]
        b_now = b_rows[:, place * states : (place + 1) * states]
        c_now = c_rows[:, place * states : (place + 1) * states]
        state = (
            jnp.exp(step_now[:, None, :] * rate[None]) * state
            + b_now[:, :, None] * drive_now[:, None, :]
        )
        local_parts.append(jnp.sum(c_now[:, :, None] * state, axis=1))
        running = running + step_now
        elapsed.append(running)
    totals = jnp.exp(running[:, None, :] * rate[None])
    _, through = lax.associative_scan(link_blocks, (totals, state), axis=0)
    starts = jnp.concatenate([jnp.zeros((1, states, chans), jnp.float32), through[: blocks - 1]], 0)
    pieces = []
    for place in range(span):
        c_now = c_rows[:, place * states : (place + 1) * states]
        carried = jnp.sum(
            c_now[:, :, None] * jnp.exp(elapsed[place][:, None, :] * rate[None]) * starts, axis=1
        )
        pieces.append(local_parts[place] + carried)
    return jnp.concatenate(pieces, 1).reshape(length, chans)


def local(
    conv_input,
    gate_input,
    conv_weight,
    conv_bias,
    x_weight,
    dt_gain,
    dt_weight,
    dt_bias,
    a_log,
    skip,
):
    width = conv_weight.shape[0]
    rank = dt_weight.shape[0]
    states = a_log.shape[0]
    prior = passed_along(conv_input[conv_input.shape[0] - (width - 1) :], "seq", 1)
    params = gather_directly(jnp.concatenate([conv_weight, conv_bias[None, :]], 0), "seq", 1)
    outgoing = causal_conv(prior.astype(jnp.float32), conv_input, params[:width], params[width])
    local_proj = jnp.dot(
        outgoing,
        lax.all_gather(x_weight, "seq", axis=0, tiled=True),
        preferred_element_type=jnp.float32,
    )
    arrived, gate_part = (
        lax.all_to_all(outgoing, "seq", split_axis=1, concat_axis=0, tiled=True),
        lax.all_to_all(gate_input, "seq", split_axis=1, concat_axis=0, tiled=True),
    )
    proj = lax.all_gather(local_proj, "seq", axis=0, tiled=True)
    dt_low = proj[:, :rank]
    bmat = proj[:, rank : rank + states]
    cmat = proj[:, rank + states :]
    normed = (
        dt_low
        * lax.rsqrt(jnp.mean(dt_low * dt_low, axis=1, keepdims=True) + 1e-06)
        * dt_gain[None, :]
    ).astype(jnp.bfloat16)
    step = jax.nn.softplus(
        jnp.dot(normed, dt_weight, preferred_element_type=jnp.float32) + dt_bias[None, :]
    )
    rate = -jnp.exp(a_log)
    xfloat = arrived.astype(jnp.float32)
    scanned = selective_scan(step, xfloat, bmat, cmat, rate)
    y_out = (scanned + skip[None, :] * xfloat).astype(jnp.bfloat16)
    held = lax.optimization_barrier(y_out)
    gated = (held.astype(jnp.float32) * jax.nn.silu(gate_part.astype(jnp.float32))).astype(
        jnp.bfloat16
    )
    return lax.all_to_all(gated, "seq", split_axis=0, concat_axis=1, tiled=True)


def solution(mesh):
    return jax.shard_map(
        local,
        mesh=mesh,
        in_specs=(
            P(("batch", "seq"), None),
            P(("batch", "seq"), None),
            P(None, "seq"),
            P("seq"),
            P("seq", None),
            P(),
            P(None, "seq"),
            P("seq"),
            P(None, "seq"),
            P("seq"),
        ),
        out_specs=P(("batch", "seq"), None),
        check_vma=False,
    )
```

profile of v0, /device:TPU:32, one launch (start us, length us, event | category | flops | bytes accessed | tf_op | source)
XLA Modules:
  0.0 660.3 jit_solution(11097169348318939079)
XLA Ops:
  9.3 11.4 %all-to-all-start = ((bf16[32,5,256]{2,1,0:T(8,128)(2,1)}), bf16[32,5,256]{2,1,0:T(8,128)(2,1)S(1)}, u32[]{:S(2)}, u32[]{:S(2)}) async-start(bf16[32,5,256]{2,1,0:T(8,128)(2,1)} %broadcast_in_dim.7), calls=%async_computation | async-start | bytes 262144 | tf_op jit(solution)/shard_map/all_to_all | solution.py:15
  30.5 7.6 %multiply_convert_fusion.1 = bf16[128,8192]{1,0:T(8,128)(2,1)S(1)} fusion(f32[128,8192]{1,0:T(8,128)} %convert_element_type.94, f32[3,8192]{1,0:T(4,128)S(1)} %convert_element_type.93, f32[8192]{0:T(1024)S(1)} %bitcast.55, f32[8192]{0:T(1024)S(1)} %bitcast.56, f32[8192]{0:T(1024)S(1)} %bitcast.57, f32[8192]{0:T(1024)S(1)} %bitcast.58, f32[8192]{0:T(1024)S(1)} %bitcast.54), kind=kLoop, calls=%fused_computation.78 | loop fusion | flops 16777216 | bytes 6553600 | tf_op jit(solution)/shard_map/convert_element_type | solution.py:36
  38.2 59.4 %all-gather.3.cloned.1.call-done = bf16[8192,288]{0,1:T(8,128)(2,1)} async-done(((bf16[256,288]{0,1:T(8,128)(2,1)}), bf16[8192,288]{0,1:T(8,128)(2,1)}) %all-gather.3.cloned.1.call-update) | async-done | bytes 4718608 | tf_op jit(solution)/shard_map/all_gather | solution.py:101
  103.5 9.4 %all-to-all-start.1 = ((bf16[128,32,256]{2,0,1:T(8,128)(2,1)}), bf16[128,32,256]{2,0,1:T(8,128)(2,1)S(1)}, u32[]{:S(2)}, u32[]{:S(2)}) async-start(bf16[128,32,256]{2,0,1:T(8,128)(2,1)} %bitcast.50), calls=%async_computation.1 | async-start | bytes 4194304 | tf_op jit(solution)/shard_map/all_to_all | solution.py:105
  116.2 88.2 %all-gather.5.cloned.1.call-done = f32[4096,288]{0,1:T(8,128)} async-done(((f32[128,288]{0,1:T(8,128)}), f32[4096,288]{0,1:T(8,128)}) %all-gather.5.cloned.1.call-update) | async-done | bytes 4718608 | tf_op jit(solution)/shard_map/all_gather | solution.py:108
  206.9 9.4 %all-to-all-start.2 = ((bf16[128,32,256]{2,0,1:T(8,128)(2,1)}), bf16[128,32,256]{2,0,1:T(8,128)(2,1)}, u32[]{:S(2)}, u32[]{:S(2)}) async-start(bf16[128,32,256]{2,0,1:T(8,128)(2,1)} %bitcast.49), calls=%async_computation.2 | async-start | bytes 4194304 | tf_op jit(solution)/shard_map/all_to_all | solution.py:106
  216.4 8.7 %bitcast_multiply_fusion.2 = (f32[4096,256]{1,0:T(8,128)}, f32[4096,256]{1,0:T(8,128)}) fusion(bf16[128,32,256]{2,0,1:T(8,128)(2,1)S(1)} %all-to-all-done.1, f32[256]{0:T(256)S(1)} %copy-done.131, bf16[256,256]{1,0:T(8,128)(2,1)S(1)} %copy-done, f32[4096,288]{0,1:T(8,128)} %all-gather.5.cloned.1.call-done, f32[256]{0:T(256)S(1)} %copy-done.132, ...), kind=kOutput, calls=%fused_computation.23 | convolution fusion | flops 549453824 | bytes 14829568 | tf_op jit(solution)/shard_map/dot_general | solution.py:118
  254.2 20.0 %multiply_reduce_fusion.1 = (f32[256,256]{1,0:T(8,128)}, f32[256,16,256]{2,1,0:T(8,128)S(1)}, f32[256,16,256]{2,1,0:T(8,128)S(1)}, f32[256,16,256]{2,1,0:T(8,128)}) fusion(f32[256,16]{1,0:T(8,128)S(1)} %get-tuple-element.99, f32[256,256]{1,0:T(8,128)} %get-tuple-element.77, f32[256,16]{1,0:T(8,128)} %get-tuple-element.117, ...), kind=kLoop, calls=%fused_computation.27 | loop fusion | flops 69140480 | bytes 21528576 | tf_op jit(solution)/shard_map/reduce_sum | solution.py:65
  274.2 6.4 multiply_reduce_fusion.3
  323.2 8.7 %pad.59 = f32[32,16,256]{2,1,0:T(8,128)} pad(f32[16,16,256]{2,1,0:T(8,128)} %add.351, f32[]{:T(128)} %constant.5.clone.1), padding=1_0_1x0_0_0x0_0_0 | pad | bytes 786436 | tf_op jit(solution)/shard_map/pad | solution.py:69
  336.3 11.6 %pad.61 = f32[64,16,256]{2,1,0:T(8,128)S(1)} pad(f32[32,16,256]{2,1,0:T(8,128)} %add.353, f32[]{:T(128)} %constant.5.clone.1), padding=1_0_1x0_0_0x0_0_0 | pad | bytes 1572868 | tf_op jit(solution)/shard_map/pad | solution.py:69
  349.8 15.6 %pad.60 = f32[64,16,256]{2,1,0:T(8,128)} pad(f32[32,16,256]{2,1,0:T(8,128)} %pad_maximum_fusion.3, f32[]{:T(128)} %constant.5.clone.1), padding=0_1_1x0_0_0x0_0_0 | pad | bytes 1572868 | tf_op jit(solution)/shard_map/pad | solution.py:69
  369.8 23.1 %pad.62 = f32[128,16,256]{2,1,0:T(8,128)S(1)} pad(f32[64,16,256]{2,1,0:T(8,128)} %pad_maximum_fusion.2, f32[]{:T(128)} %constant.5.clone.1), padding=0_1_1x0_0_0x0_0_0 | pad | bytes 3145732 | tf_op jit(solution)/shard_map/pad | solution.py:69
  392.9 20.5 %pad.63 = f32[128,16,256]{2,1,0:T(8,128)} pad(f32[64,16,256]{2,1,0:T(8,128)S(1)} %copy-done.14, f32[]{:T(128)} %constant.5.clone.1), padding=1_0_1x0_0_0x0_0_0 | pad | bytes 3145732 | tf_op jit(solution)/shard_map/pad | solution.py:69
  422.5 9.2 %multiply_reduce_fusion.17 = f32[256,256]{1,0:T(8,128)} fusion(f32[256,16]{1,0:T(8,128)S(1)} %copy-done.103, f32[256,256]{1,0:T(8,128)S(1)} %copy-done.93, f32[256,16]{1,0:T(8,128)S(1)} %copy-done.128, f32[256,256]{1,0:T(8,128)S(1)} %copy-done.102, f32[16,256]{1,0:T(8,128)S(1)} %exponential_negate_fusion, f32[256,256]{1,0:T(8,128)S(1)} %copy-done.92, ...), kind=kLoop, calls=%fused_computation.43 | loop fusion | flops 35586048 | bytes 4620288 | tf_op jit(solution)/shard_map/reduce_sum | solution.py:65
  431.7 40.5 %pad.161 = f32[256,16,256]{2,1,0:T(8,128)} pad(f32[128,16,256]{2,1,0:T(8,128)S(1)} %copy-done.11, f32[]{:T(128)} %constant.5.clone.1), padding=1_0_1x0_0_0x0_0_0 | pad | bytes 6291460
  473.9 40.5 %pad.87 = f32[255,16,256]{2,1,0:T(8,128)} pad(f32[128,16,256]{2,1,0:T(8,128)S(1)} %pad_maximum_fusion.1, f32[]{:T(128)} %constant.5.clone.1), padding=0_0_1x0_0_0x0_0_0 | pad | bytes 6275076 | tf_op jit(solution)/shard_map/slice | solution.py:70
  514.5 8.7 %multiply_reduce_fusion.19 = f32[256,256]{1,0:T(8,128)S(1)} fusion(f32[256,16]{1,0:T(8,128)S(1)} %copy-done.105, f32[256,256]{1,0:T(8,128)} %get-tuple-element.86, f32[256,16]{1,0:T(8,128)} %get-tuple-element.126, f32[256,256]{1,0:T(8,128)} %get-tuple-element.87, f32[256,16]{1,0:T(8,128)} %get-tuple-element.127, f32[256,256]{1,0:T(8,128)} %get-tuple-element.65, ...), kind=kLoop, calls=%fused_computation.45 | loop fusion | flops 31391744 | bytes 4079616 | tf_op jit(solution)/shard_map/reduce_sum | solution.py:65
  531.2 9.1 %multiply_reduce_fusion.29 = (f32[256,256]{1,0:T(8,128)S(1)}, f32[256,256]{1,0:T(8,128)S(1)}, f32[256,256]{1,0:T(8,128)S(1)}, f32[256,256]{1,0:T(8,128)S(1)}, f32[256,256]{1,0:T(8,128)S(1)}, /*index=5*/f32[256,256]{1,0:T(8,128)S(1)}) fusion(f32[256,16]{1,0:T(8,128)S(1)} %copy-done.113, f32[256,256]{1,0:T(8,128)S(1)} %copy-done.87, ...), kind=kLoop, calls=%fused_computation.55 | loop fusion | flops 27918336 | bytes 7716864 | tf_op jit(solution)/shard_map/reduce_sum | solution.py:65
  541.1 7.6 %multiply_reduce_fusion.23 = (f32[256,256]{1,0:T(8,128)S(1)}, f32[256,256]{1,0:T(8,128)S(1)}, f32[256,256]{1,0:T(8,128)S(1)}) fusion(f32[256,16]{1,0:T(8,128)S(1)} %copy-done.110, f32[256,256]{1,0:T(8,128)S(1)} %copy-done.81, f32[256,16]{1,0:T(8,128)S(1)} %copy-done.117, f32[256,256]{1,0:T(8,128)S(1)} %copy-done.84, f32[256,16]{1,0:T(8,128)S(1)} %copy-done.119, ...), kind=kLoop, calls=%fused_computation.49 | loop fusion | flops 27066368 | bytes 3555328 | tf_op jit(solution)/shard_map/reduce_sum | solution.py:65
  548.9 8.8 %multiply_reduce_fusion = (f32[256,256]{1,0:T(8,128)S(1)}, f32[256,256]{1,0:T(8,128)S(1)}, f32[256,256]{1,0:T(8,128)S(1)}, f32[256,256]{1,0:T(8,128)S(1)}, f32[256,256]{1,0:T(8,128)S(1)}, /*index=5*/f32[256,256]{1,0:T(8,128)S(1)}) fusion(f32[256,16]{1,0:T(8,128)S(1)} %copy-done.108, f32[16,256]{1,0:T(8,128)S(1)} %exponential_negate_fusion, ...), kind=kLoop, calls=%fused_computation.26 | loop fusion | flops 24772608 | bytes 7438336 | tf_op jit(solution)/shard_map/reduce_sum | solution.py:74
  561.7 8.8 %multiply_reduce_fusion.2 = (f32[256,256]{1,0:T(8,128)S(1)}, f32[256,256]{1,0:T(8,128)S(1)}, f32[256,256]{1,0:T(8,128)S(1)}, f32[256,256]{1,0:T(8,128)S(1)}, f32[256,256]{1,0:T(8,128)S(1)}, /*index=5*/f32[256,256]{1,0:T(8,128)S(1)}) fusion(f32[256,256]{1,0:T(8,128)S(1)} %copy-done.57, f32[256,16]{1,0:T(8,128)S(1)} %copy-done.50, ...), kind=kLoop, calls=%fused_computation.28 | loop fusion | flops 24772608 | bytes 7438336 | tf_op jit(solution)/shard_map/reduce_sum | solution.py:74
  572.1 7.2 %multiply_reduce_fusion.9 = (f32[256,256]{1,0:T(8,128)S(1)}, f32[256,256]{1,0:T(8,128)S(1)}, f32[256,256]{1,0:T(8,128)S(1)}, f32[256,256]{1,0:T(8,128)S(1)}) fusion(f32[256,16]{1,0:T(8,128)S(1)} %copy-done.46, f32[256,256]{1,0:T(8,128)S(1)} %copy-done.27, f32[256,16]{1,0:T(8,128)S(1)} %copy-done.40, f32[256,256]{1,0:T(8,128)S(1)} %copy-done.37, ...), kind=kLoop, calls=%fused_computation.35 | loop fusion | flops 20709376 | bytes 6946816 | tf_op jit(solution)/shard_map/reduce_sum | solution.py:65
  596.8 55.1 %all_to_all.50 = bf16[32,128,256]{2,1,0:T(8,128)(2,1)S(1)} all-to-all(bf16[32,128,256]{2,1,0:T(8,128)(2,1)S(1)} %bitcast.48), channel_id=1, replica_groups=mesh['seq'=32,'batch'=8] {'seq'}, dimensions={0} | all-to-all | bytes 4194304 | tf_op jit(solution)/shard_map/all_to_all | solution.py:128
  (364 shorter events, 149.8 us)
Async XLA Ops:
  6.5 209.8 %copy-start = (bf16[256,256]{1,0:T(8,128)(2,1)S(1)}, bf16[256,256]{1,0:T(8,128)(2,1)}, u32[]{:S(2)}) copy-start(bf16[256,256]{1,0:T(8,128)(2,1)} %param.16) | copy-start | bytes 393220
  6.5 91.0 %all-gather.3.cloned.1.call-start = ((), (), s32[]{:S(2)}) async-start(), calls=%async_computation.4 | async-start | bytes 4866048 | tf_op jit(solution)/shard_map/all_gather | solution.py:101
  9.3 21.2 %all-to-all-start = ((bf16[32,5,256]{2,1,0:T(8,128)(2,1)}), bf16[32,5,256]{2,1,0:T(8,128)(2,1)S(1)}, u32[]{:S(2)}, u32[]{:S(2)}) async-start(bf16[32,5,256]{2,1,0:T(8,128)(2,1)} %broadcast_in_dim.7), calls=%async_computation | async-start | bytes 262144 | tf_op jit(solution)/shard_map/all_to_all | solution.py:15
  20.6 183.7 %all-gather.5.cloned.1.call-start = ((), (), s32[]{:S(2)}) async-start(), calls=%async_computation.5 | async-start | bytes 4866048 | tf_op jit(solution)/shard_map/all_gather | solution.py:108
  21.6 7.5 %collective-permute-start = (bf16[3,8192]{1,0:T(4,128)(2,1)S(1)}, bf16[3,8192]{1,0:T(4,128)(2,1)S(1)}, u32[]{:S(2)}, u32[]{:S(2)}) collective-permute-start(bf16[3,8192]{1,0:T(4,128)(2,1)S(1)} %slice.443), channel_id=1, source_target_pairs={{0,8},{8,16},{16,24},{24,32},{32,40},{40,48},{48,56},{56,64},{64,7... | collective-permute-start | bytes 147464 | tf_op jit(solution)/shard_map/ppermute | solution.py:10
  103.5 103.4 %all-to-all-start.1 = ((bf16[128,32,256]{2,0,1:T(8,128)(2,1)}), bf16[128,32,256]{2,0,1:T(8,128)(2,1)S(1)}, u32[]{:S(2)}, u32[]{:S(2)}) async-start(bf16[128,32,256]{2,0,1:T(8,128)(2,1)} %bitcast.50), calls=%async_computation.1 | async-start | bytes 4194304 | tf_op jit(solution)/shard_map/all_to_all | solution.py:105
  116.2 100.2 %copy-start.131 = (f32[256]{0:T(256)S(1)}, f32[256]{0:T(256)}, u32[]{:S(2)}) copy-start(f32[256]{0:T(256)} %param.17) | copy-start | bytes 3076
  116.2 100.2 %copy-start.132 = (f32[256]{0:T(256)S(1)}, f32[256]{0:T(256)}, u32[]{:S(2)}) copy-start(f32[256]{0:T(256)} %param.15) | copy-start | bytes 3076
  206.9 18.2 %copy-start.12 = (bf16[128,32,256]{2,0,1:T(8,128)(2,1)}, bf16[128,32,256]{2,0,1:T(8,128)(2,1)S(1)}, u32[]{:S(2)}) copy-start(bf16[128,32,256]{2,0,1:T(8,128)(2,1)S(1)} %all-to-all-done.1) | copy-start | bytes 6291460
  206.9 387.0 %all-to-all-start.2 = ((bf16[128,32,256]{2,0,1:T(8,128)(2,1)}), bf16[128,32,256]{2,0,1:T(8,128)(2,1)}, u32[]{:S(2)}, u32[]{:S(2)}) async-start(bf16[128,32,256]{2,0,1:T(8,128)(2,1)} %bitcast.49), calls=%async_computation.2 | async-start | bytes 4194304 | tf_op jit(solution)/shard_map/all_to_all | solution.py:106
  234.5 39.7 %copy-start.19 = (f32[256,256]{1,0:T(8,128)}, f32[256,256]{1,0:T(8,128)S(1)}, u32[]{:S(2)}) copy-start(f32[256,256]{1,0:T(8,128)S(1)} %get-tuple-element.41) | copy-start | bytes 786436
  253.3 20.9 %copy-start.107 = (f32[256,16]{1,0:T(8,128)}, f32[256,16]{1,0:T(8,128)S(1)}, u32[]{:S(2)}) copy-start(f32[256,16]{1,0:T(8,128)S(1)} %get-tuple-element.99) | copy-start | bytes 49156
  253.3 20.9 %copy-start.49 = (f32[256,16]{1,0:T(8,128)}, f32[256,16]{1,0:T(8,128)S(1)}, u32[]{:S(2)}) copy-start(f32[256,16]{1,0:T(8,128)S(1)} %get-tuple-element.100) | copy-start | bytes 49156
  253.3 20.9 %copy-start.51 = (f32[256,16]{1,0:T(8,128)}, f32[256,16]{1,0:T(8,128)S(1)}, u32[]{:S(2)}) copy-start(f32[256,16]{1,0:T(8,128)S(1)} %get-tuple-element.101) | copy-start | bytes 49156
  253.3 20.9 %copy-start.53 = (f32[256,16]{1,0:T(8,128)}, f32[256,16]{1,0:T(8,128)S(1)}, u32[]{:S(2)}) copy-start(f32[256,16]{1,0:T(8,128)S(1)} %get-tuple-element.102) | copy-start | bytes 49156
  368.7 24.2 %copy-start.14 = (f32[64,16,256]{2,1,0:T(8,128)S(1)}, f32[64,16,256]{2,1,0:T(8,128)}, u32[]{:S(2)}) copy-start(f32[64,16,256]{2,1,0:T(8,128)} %add.355) | copy-start | bytes 3145732
  472.1 42.3 %copy-start.105 = (f32[256,16]{1,0:T(8,128)S(1)}, f32[256,16]{1,0:T(8,128)}, u32[]{:S(2)}) copy-start(f32[256,16]{1,0:T(8,128)} %get-tuple-element.107) | copy-start | bytes 49156
  548.8 12.7 %copy-start.45 = (f32[256,16]{1,0:T(8,128)S(1)}, f32[256,16]{1,0:T(8,128)}, u32[]{:S(2)}) copy-start(f32[256,16]{1,0:T(8,128)} %get-tuple-element.98) | copy-start | bytes 49156
  548.8 12.7 %copy-start.47 = (f32[256,16]{1,0:T(8,128)S(1)}, f32[256,16]{1,0:T(8,128)}, u32[]{:S(2)}) copy-start(f32[256,16]{1,0:T(8,128)} %get-tuple-element.104) | copy-start | bytes 49156
  548.8 12.7 %copy-start.48 = (f32[256,16]{1,0:T(8,128)S(1)}, f32[256,16]{1,0:T(8,128)}, u32[]{:S(2)}) copy-start(f32[256,16]{1,0:T(8,128)} %get-tuple-element.105) | copy-start | bytes 49156
  548.8 12.7 %copy-start.50 = (f32[256,16]{1,0:T(8,128)S(1)}, f32[256,16]{1,0:T(8,128)}, u32[]{:S(2)}) copy-start(f32[256,16]{1,0:T(8,128)} %copy-done.49) | copy-start | bytes 49156
  548.8 12.7 %copy-start.57 = (f32[256,256]{1,0:T(8,128)S(1)}, f32[256,256]{1,0:T(8,128)}, u32[]{:S(2)}) copy-start(f32[256,256]{1,0:T(8,128)} %get-tuple-element.42) | copy-start | bytes 786436
  548.8 12.7 %copy-start.58 = (f32[256,256]{1,0:T(8,128)S(1)}, f32[256,256]{1,0:T(8,128)}, u32[]{:S(2)}) copy-start(f32[256,256]{1,0:T(8,128)} %get-tuple-element.46) | copy-start | bytes 786436
  596.8 56.6 %copy-start.1 = (bf16[256,256]{1,0:T(8,128)(2,1)S(1)}, bf16[256,256]{1,0:T(8,128)(2,1)}, u32[]{:S(2)}) copy-start(bf16[256,256]{1,0:T(8,128)(2,1)} %param.16) | copy-start | bytes 393220
  (115 other events, 671.9 us)
Sparse Core Ops, SparseCore 0:
  9.8 87.7 all-gather.2
  102.1 102.2 all-gather.4
where the time goes:
time: 667 us; the launch traced here: 660 us
  local copies, waits for them, and re-layouts  226 us (34%)
  other arithmetic  167 us (25%)
  waiting for transfers between devices  150 us (22%)
  blocking collectives  55.1 us (8%)
  starting transfers between devices  33.6 us (5%)
  between operations  15.2 us (2%)
  matrix products  13.1 us (2%)
    pad x12, local copies, waits for them, and re-layouts, selective_scan(): _, through = lax.associative_scan(link_blocks, (totals, state), axis=0)  99.8 us
    all_gather x1, waiting for transfers between devices, local(): proj = lax.all_gather(local_proj, 'seq', axis=0, tiled=True)  88.2 us
    reduce_sum x8, other arithmetic, selective_scan(): local_parts.append(jnp.sum(c_now[:, :, None] * state, axis=1))  74.5 us
    all_gather x1, waiting for transfers between devices, local(): lax.all_gather(x_weight, 'seq', axis=0, tiled=True)  59.4 us
    all_to_all x1, blocking collectives, local(): return lax.all_to_all(gated, 'seq', split_axis=0, concat_axis=1, tiled=True)  55.1 us
    unnamed x267, local copies, waits for them, and re-layouts  46.1 us
    slice x1, local copies, waits for them, and re-layouts, selective_scan(): through[:blocks - 1]  40.5 us
    reduce_sum x2, other arithmetic, selective_scan(): jnp.sum(c_now[:, :, None] * jnp.exp(elapsed[place][:, None, :] * rate[Non...  17.5 us
  transfers between devices with their start and end apart: 6, of which 3 were waited for; matrix products, arithmetic and copies ran while one was open for 59% of the time, Pallas kernels for 0%

commit v1 on v0

v1 whole, which is shorter than its diff:
```python
import jax
import jax.numpy as jnp
from jax import lax
from jax.experimental import pallas as pl
from jax.experimental.pallas import tpu as pltpu
from jax.sharding import Mesh, PartitionSpec as P

F32 = jnp.float32
BF16 = jnp.bfloat16
LOG2E = 1.4426950408889634
SEQ = ("y", "z")
BLK = 1024
SHARD = 256


def silu(v):
    return v / (1.0 + jnp.exp(-v))


def row_of(ref, at):
    return ref[pl.ds(at, 8, stride=0), :]


def two_parts(v):
    high = lax.reduce_precision(v, 8, 7)
    return high.astype(BF16), (v - high).astype(BF16)


def front_kernel(core_ref, ci_ref, prior_ref, own_ref, oth_ref, gain_ref, xc_ref, normed_ref, bc_ref, pad_ref, acc_ref):
    step = pl.program_id(0)
    core = core_ref[0]
    rows = ci_ref.shape[0]
    taps = 4
    pad_ref[0:8, :] = prior_ref[...].astype(F32)
    pad_ref[8 : 8 + rows, :] = ci_ref[...].astype(F32)

    @pl.when(step == 0)
    def _():
        acc_ref[...] = jnp.zeros_like(acc_ref)

    acc = acc_ref[...]
    for s in range(4):
        mine = own_ref[s, 0, 128:136, 0:SHARD].astype(F32)
        other = oth_ref[s, 0, 128:136, 0:SHARD].astype(F32)
        par = jnp.where(core == 0, mine, other)
        lanes = slice(s * SHARD, (s + 1) * SHARD)
        total = jnp.broadcast_to(par[taps : taps + 1, :], (rows, SHARD))
        for k in range(taps):
            total = total + par[k : k + 1, :] * pad_ref[5 + k : 5 + k + rows, lanes]
        xc_ref[:, lanes] = silu(total).astype(BF16)
        at = pl.multiple_of(s * SHARD + core * 128, 128)
        acc = acc + jnp.dot(xc_ref[:, pl.ds(at, 128)], own_ref[s, 0, 0:128, :], preferred_element_type=F32)
        at = pl.multiple_of(s * SHARD + (1 - core) * 128, 128)
        acc = acc + jnp.dot(xc_ref[:, pl.ds(at, 128)], oth_ref[s, 0, 0:128, :], preferred_element_type=F32)
    acc_ref[...] = acc

    @pl.when(step == pl.num_programs(0) - 1)
    def _():
        rank = gain_ref.shape[1]
        low = acc_ref[:, 0:rank]
        scale = lax.rsqrt(jnp.mean(low * low, axis=1, keepdims=True) + 1e-06)
        normed_ref[...] = (low * scale * gain_ref[...]).astype(BF16)
        for m in range(32):
            col = acc_ref[:, rank + m : rank + m + 1]
            bc_ref[m * rows : (m + 1) * rows, :] = jnp.broadcast_to(col, (rows, 128))


def front(core, conv_input, prior, x_own, x_oth, gain):
    rows, inner = conv_input.shape
    wspec = pl.BlockSpec((4, 1, 136, 288), lambda b: (b % 2, b // 2, 0, 0))
    return pl.pallas_call(
        front_kernel,
        grid=(inner // BLK,),
        in_specs=[
            pl.BlockSpec(memory_space=pltpu.SMEM),
            pl.BlockSpec((rows, BLK), lambda b: (0, b)),
            pl.BlockSpec((8, BLK), lambda b: (0, b)),
            wspec,
            wspec,
            pl.BlockSpec((1, 256), lambda b: (0, 0)),
        ],
        out_specs=[
            pl.BlockSpec((rows, BLK), lambda b: (0, b)),
            pl.BlockSpec((rows, 256), lambda b: (0, 0)),
            pl.BlockSpec((32 * rows, 128), lambda b: (0, 0)),
        ],
        out_shape=[
            jax.ShapeDtypeStruct((rows, inner), BF16),
            jax.ShapeDtypeStruct((rows, 256), BF16),
            jax.ShapeDtypeStruct((32 * rows, 128), F32),
        ],
        scratch_shapes=[pltpu.VMEM((rows + 8, BLK), F32), pltpu.VMEM((rows, 288), F32)],
        compiler_params=pltpu.CompilerParams(dimension_semantics=("arbitrary",)),
        name="front",
    )(core, conv_input, prior, x_own, x_oth, gain)


def scan_kernel(core_ref, normed_ref, xc_ref, own_ref, oth_ref, bc_ref, step_ref, y_ref, rate_ref, ends_ref, x_scr, par_scr, h_scr):
    core = core_ref[0]
    rows = normed_ref.shape[0]
    mine_k = normed_ref[:, pl.ds(pl.multiple_of(core * 128, 128), 128)]
    other_k = normed_ref[:, pl.ds(pl.multiple_of((1 - core) * 128, 128), 128)]
    skips = []
    for s in range(4):
        raw = jnp.dot(mine_k, own_ref[s, 0, 0:128, :], preferred_element_type=F32)
        raw = raw + jnp.dot(other_k, oth_ref[s, 0, 0:128, :], preferred_element_type=F32)
        mine = own_ref[s, 0, 128:152, :].astype(F32)
        other = oth_ref[s, 0, 128:152, :].astype(F32)
        mine_log = mine[0:8] + mine[8:16]
        other_log = other[0:8] + other[8:16]
        mine_vec = mine[16:17] + mine[17:18]
        other_vec = other[16:17] + other[17:18]
        bias = jnp.where(core == 0, mine_vec, other_vec)
        skip = jnp.where(core == 0, other_vec, mine_vec)
        raw = raw + bias
        step = jnp.maximum(raw, 0.0) + jnp.log1p(jnp.exp(-jnp.abs(raw)))
        xs = xc_ref[:, s * SHARD : (s + 1) * SHARD].astype(F32)
        for p in range(2):
            j = 2 * s + p
            lanes = slice(p * 128, (p + 1) * 128)
            for i in range(rows // 8):
                step_ref[0, pl.ds(64 * i + j, 8, stride=8), :] = step[8 * i : 8 * i + 8, lanes]
                x_scr[pl.ds(64 * i + j, 8, stride=8), :] = xs[8 * i : 8 * i + 8, lanes]
            at = pl.multiple_of(j * 16 + core * 8, 8)
            par_scr[pl.ds(at, 8), :] = -LOG2E * jnp.exp(mine_log[:, lanes])
            at = pl.multiple_of(j * 16 + (1 - core) * 8, 8)
            par_scr[pl.ds(at, 8), :] = -LOG2E * jnp.exp(other_log[:, lanes])
            skips.append(skip[:, lanes])
    skip = jnp.concatenate(skips, 0)
    for n in range(16):
        rate_ref[0, 8 * n : 8 * n + 8, :] = par_scr[pl.ds(n, 8, stride=16), :]
    rates = [rate_ref[0, 8 * n : 8 * n + 8, :] for n in range(16)]

    def advance(t, carry):
        total, state = carry
        at = pl.multiple_of(t * 8, 8)
        now = step_ref[0, pl.ds(at, 8), :]
        xt = x_scr[pl.ds(at, 8), :]
        drive = now * xt
        even = skip * xt
        odd = None
        fresh = []
        for n in range(16):
            b = row_of(bc_ref, n * rows + t)
            c = row_of(bc_ref, (16 + n) * rows + t)
            h = jnp.exp2(now * rates[n]) * state[n] + b * drive
            fresh.append(h)
            if n % 2:
                odd = c * h if odd is None else odd + c * h
            else:
                even = even + c * h
        y_ref[0, pl.ds(at, 8), :] = even + odd
        return total + now, tuple(fresh)

    zero = jnp.zeros((8, 128), F32)
    total, state = lax.fori_loop(0, rows, advance, (zero, (zero,) * 16))
    for n in range(16):
        h_scr[8 * n : 8 * n + 8, :] = state[n]
    high = total.astype(BF16).astype(F32)
    h_scr[128:136, :] = high
    h_scr[136:144, :] = total - high
    for j in range(8):
        low = h_scr[pl.ds(j, 8, stride=8), :]
        up = h_scr[pl.ds(64 + j, 8, stride=8), :]
        ends_ref[j // 2, (j % 2) * 16 : (j % 2) * 16 + 16, :] = jnp.concatenate([low, up], 0).astype(BF16)
    for jj in range(4):
        sums = [h_scr[128 + 2 * jj : 130 + 2 * jj, :], h_scr[136 + 2 * jj : 138 + 2 * jj, :], jnp.zeros((4, 128), F32)]
        ends_ref[jj, 32:40, :] = jnp.concatenate(sums, 0).astype(BF16)


def scan(core, normed, xc, d_own, d_oth, bc):
    rows, inner = xc.shape
    blocks = inner // BLK
    wspec = pl.BlockSpec((4, 1, 152, 256), lambda b: (b % 2, b // 2, 0, 0))
    return pl.pallas_call(
        scan_kernel,
        grid=(blocks,),
        in_specs=[
            pl.BlockSpec(memory_space=pltpu.SMEM),
            pl.BlockSpec((rows, 256), lambda b: (0, 0)),
            pl.BlockSpec((rows, BLK), lambda b: (0, b)),
            wspec,
            wspec,
            pl.BlockSpec((32 * rows, 128), lambda b: (0, 0)),
        ],
        out_specs=[
            pl.BlockSpec((1, 8 * rows, 128), lambda b: (b, 0, 0)),
            pl.BlockSpec((1, 8 * rows, 128), lambda b: (b, 0, 0)),
            pl.BlockSpec((1, 128, 128), lambda b: (b, 0, 0)),
            pl.BlockSpec((4, 40, 128), lambda b: (b, 0, 0)),
        ],
        out_shape=[
            jax.ShapeDtypeStruct((blocks, 8 * rows, 128), F32),
            jax.ShapeDtypeStruct((blocks, 8 * rows, 128), F32),
            jax.ShapeDtypeStruct((blocks, 128, 128), F32),
            jax.ShapeDtypeStruct((4 * blocks, 40, 128), BF16),
        ],
        scratch_shapes=[
            pltpu.VMEM((8 * rows, 128), F32),
            pltpu.VMEM((128, 128), F32),
            pltpu.VMEM((144, 128), F32),
        ],
        compiler_params=pltpu.CompilerParams(dimension_semantics=("arbitrary",)),
        name="scan",
    )(core, normed, xc, d_own, d_oth, bc)


def link_kernel(ends_ref, log_ref, start_ref):
    count = ends_ref.shape[0]
    rate = -LOG2E * jnp.exp(log_ref[...])
    rate = jnp.concatenate([rate[:, 0:128], rate[:, 128:256]], 0)
    state = jnp.zeros((32, 128), F32)
    for s in range(count):
        start_ref[s] = state.astype(BF16)
        sums = ends_ref[s, 32:40, :].astype(F32)
        sums = sums[0:2] + sums[2:4]
        spread = jnp.concatenate([jnp.broadcast_to(sums[0:1], (16, 128)), jnp.broadcast_to(sums[1:2], (16, 128))], 0)
        state = jnp.exp2(rate * spread) * state + ends_ref[s, 0:32, :].astype(F32)


def link(ends, a_log):
    return pl.pallas_call(
        link_kernel,
        out_shape=jax.ShapeDtypeStruct((ends.shape[0], 32, 128), BF16),
        name="link",
    )(ends, a_log)


def close_kernel(step_ref, y_ref, rate_ref, start_ref, c_ref, gate_ref, out_ref, s_scr, y_scr):
    rows = gate_ref.shape[0]
    for j in range(8):
        s_scr[16 * j : 16 * j + 16, :] = start_ref[j // 2, (j % 2) * 16 : (j % 2) * 16 + 16, :].astype(F32)
    starts = [s_scr[pl.ds(n, 8, stride=16), :] for n in range(16)]
    rates = [rate_ref[0, 8 * n : 8 * n + 8, :] for n in range(16)]

    def advance(t, total):
        at = pl.multiple_of(t * 8, 8)
        total = total + step_ref[0, pl.ds(at, 8), :]
        even = y_ref[0, pl.ds(at, 8), :]
        odd = None
        for n in range(16):
            c = row_of(c_ref, n * rows + t)
            part = c * starts[n] * jnp.exp2(total * rates[n])
            if n % 2:
                odd = part if odd is None else odd + part
            else:
                even = even + part
        y_scr[pl.ds(at, 8), :] = even + odd
        return total

    lax.fori_loop(0, rows, advance, jnp.zeros((8, 128), F32))
    for j in range(8):
        for i in range(rows // 16):
            low = y_scr[pl.ds(128 * i + j, 8, stride=8), :]
            up = y_scr[pl.ds(128 * i + 64 + j, 8, stride=8), :]
            y = jnp.concatenate([low, up], 0).astype(BF16).astype(F32)
            gate = gate_ref[16 * i : 16 * i + 16, j * 128 : (j + 1) * 128].astype(F32)
            out_ref[16 * i : 16 * i + 16, j * 128 : (j + 1) * 128] = (y * silu(gate)).astype(BF16)


def close(step, y, rate, start, bc, gate):
    rows, inner = gate.shape
    return pl.pallas_call(
        close_kernel,
        grid=(inner // BLK,),
        in_specs=[
            pl.BlockSpec((1, 8 * rows, 128), lambda b: (b, 0, 0)),
            pl.BlockSpec((1, 8 * rows, 128), lambda b: (b, 0, 0)),
            pl.BlockSpec((1, 128, 128), lambda b: (b, 0, 0)),
            pl.BlockSpec((4, 32, 128), lambda b: (b, 0, 0)),
            pl.BlockSpec((16 * rows, 128), lambda b: (1, 0)),
            pl.BlockSpec((rows, BLK), lambda b: (0, b)),
        ],
        out_specs=pl.BlockSpec((rows, BLK), lambda b: (0, b)),
        out_shape=jax.ShapeDtypeStruct((rows, inner), BF16),
        scratch_shapes=[pltpu.VMEM((128, 128), F32), pltpu.VMEM((8 * rows, 128), F32)],
        compiler_params=pltpu.CompilerParams(dimension_semantics=("arbitrary",)),
        name="close",
    )(step, y, rate, start, bc, gate)


def from_everyone(x, axis):
    copies = jnp.broadcast_to(x, (lax.axis_size(axis), *x.shape))
    return lax.all_to_all(copies, axis, split_axis=0, concat_axis=0, tiled=True)


def pack_x(core, x_weight, conv_weight, conv_bias):
    half = lax.dynamic_slice_in_dim(x_weight, core * 128, 128, 0)
    extra = jnp.concatenate([conv_weight, conv_bias[None, :], jnp.zeros((3, SHARD), BF16)], 0)
    return jnp.concatenate([half, jnp.pad(extra, ((0, 0), (0, 32)))], 0)


def pack_d(core, dt_weight, dt_bias, a_log, skip):
    half = lax.dynamic_slice_in_dim(dt_weight, core * 128, 128, 0)
    logs = lax.dynamic_slice_in_dim(a_log, core * 8, 8, 0)
    vec = jnp.where(core == 0, dt_bias, skip)[None, :]
    pieces = [half, *two_parts(logs), *two_parts(vec), jnp.zeros((6, SHARD), BF16)]
    return jnp.concatenate(pieces, 0)


def local(conv_input, gate_input, conv_weight, conv_bias, x_weight, dt_gain, dt_weight, dt_bias, a_log, skip):
    core = lax.axis_index("core")
    count = lax.axis_size(SEQ)
    swap = [(0, 1), (1, 0)]
    x_part = from_everyone(pack_x(core, x_weight, conv_weight, conv_bias), "y")
    x_own = lax.all_gather(x_part, "z", axis=0)
    d_part = from_everyone(pack_d(core, dt_weight, dt_bias, a_log, skip), "y")
    d_own = lax.all_gather(d_part, "z", axis=0)
    x_oth = lax.ppermute(x_own, "core", swap)
    d_oth = lax.ppermute(d_own, "core", swap)
    prior = lax.ppermute(conv_input[conv_input.shape[0] - 8 :], SEQ, [(i, i + 1) for i in range(count - 1)])
    which = core.reshape(1).astype(jnp.int32)
    xc, normed, bc = front(which, conv_input, prior, x_own, x_oth, dt_gain[None, :])
    step, y, rate, ends = scan(which, normed, xc, d_own, d_oth, bc)
    ends = lax.all_to_all(ends, SEQ, split_axis=0, concat_axis=0, tiled=True)
    ends = ends.reshape(count, 40, 128)
    start = lax.all_to_all(link(ends, a_log), SEQ, split_axis=0, concat_axis=0, tiled=True)
    return close(step, y, rate, start, bc, gate_input)


def solution(mesh):
    inner = Mesh(mesh.devices.reshape(4, 8, 4, 2), ("y", "z", "x", "core"))
    tokens = P(("x", "core", "y", "z"), None)
    return jax.shard_map(
        local,
        mesh=inner,
        in_specs=(tokens, tokens, P(None, SEQ), P(SEQ), P(SEQ, None), P(), P(None, SEQ), P(SEQ), P(None, SEQ), P(SEQ)),
        out_specs=tokens,
        check_vma=False,
    )
```

time: 667 us -> 244 us (0.37)
  local copies, waits for them, and re-layouts: 226 us -> 4.55 us
  other arithmetic: 167 us -> 0.8 us
  Pallas kernels: 0 us -> 75.8 us
  waiting for transfers between devices: 150 us -> 83.4 us
  starting transfers between devices: 33.6 us -> 3.2 us
  matrix products: 13.1 us -> 0 us
    pad x12 -> x0, local copies, waits for them, and re-layouts: 99.8 us -> none  [selective_scan(): _, through = lax.associative_scan(link_blocks, (totals, state), axis=0)]
    reduce_sum x11 -> x0, other arithmetic: 94.6 us -> none  [the longest x8 74.5 us: selective_scan(): local_parts.append(jnp.sum(c_now[:, :, None] * state, axis=1))]
    pallas_call x0 -> x4, Pallas kernels: none -> 75.8 us  [the longest x1 35.3 us: scan(): pl.pallas_call(scan_kernel, grid=(blocks,), in_specs=[pl.BlockSpec(memory...]
    all_gather x2, waiting for transfers between devices: 148 us -> 78.7 us  [the longest x1 42.4 us: local(): d_own = lax.all_gather(d_part, 'z', axis=0)]
    slice x15 -> x1, local copies, waits for them, and re-layouts: 56.2 us -> 0.91 us  [local(): conv_input[conv_input.shape[0] - 8:]]
    unnamed x267 -> x15, local copies, waits for them, and re-layouts: 46.1 us -> 2.53 us
    all_to_all x3 -> x0, starting transfers between devices: 30.2 us -> none  [the longest x1 11.4 us: from_everyone(): return lax.all_to_all(copies, axis, split_axis=0, concat_axis=0, tiled=True)]
    add x15 -> x0, other arithmetic: 29.9 us -> none  [the longest x8 13.2 us: selective_scan(): _, through = lax.associative_scan(link_blocks, (totals, state), axis=0)]
  transfers between devices with their start and end apart: 6 -> 5, of which waited for: 3 -> 3; matrix products, arithmetic and copies ran while one was open for 59% -> 0% of each run, Pallas kernels for 0% -> 5%
where the time goes in v1:
time: 244 us; the launch traced here: 243 us
  waiting for transfers between devices  83.4 us (34%)
  Pallas kernels  75.8 us (31%)
  blocking collectives  61.4 us (25%)
  between operations  13.6 us (6%)
  local copies, waits for them, and re-layouts  4.55 us (2%)
  starting transfers between devices  3.2 us (1%)
    all_gather x1, waiting for transfers between devices, local(): d_own = lax.all_gather(d_part, 'z', axis=0)  42.4 us
    all_gather x1, waiting for transfers between devices, local(): x_own = lax.all_gather(x_part, 'z', axis=0)  36.3 us
    pallas_call x1, Pallas kernels, scan(): pl.pallas_call(scan_kernel, grid=(blocks,), in_specs=[pl.BlockSpec(memory...  35.3 us
    pallas_call x1, Pallas kernels, close(): pl.pallas_call(close_kernel, grid=(inner // BLK,), in_specs=[pl.BlockSpec...  26.8 us
    all_to_all x2, blocking collectives, from_everyone(): return lax.all_to_all(copies, axis, split_axis=0, concat_axis=0, tiled=True)  22.7 us
    all_to_all x1, blocking collectives, local(): ends = lax.all_to_all(ends, SEQ, split_axis=0, concat_axis=0, tiled=True)  22.5 us
    all_to_all x1, blocking collectives, local(): lax.all_to_all(link(ends, a_log), SEQ, split_axis=0, concat_axis=0, tiled...  16.2 us
    pallas_call x1, Pallas kernels, front(): pl.pallas_call(front_kernel, grid=(inner // BLK,), in_specs=[pl.BlockSpec...  11.9 us
  transfers between devices with their start and end apart: 5, of which 3 were waited for; matrix products, arithmetic and copies ran while one was open for 0% of the time, Pallas kernels for 5%

profile of v1, /device:TPU:32, one launch (start us, length us, event | category | flops | bytes accessed | tf_op | source)
XLA Modules:
  0.0 242.8 jit_solution(16764825931408646812)
XLA Ops:
  6.5 0.0 all-gather.5.cloned.1.call-start
  6.6 0.8 broadcast_in_dim.19
  7.4 0.1 pad.9.clone
  7.5 0.8 maximum_maximum_fusion
  8.2 0.1 copy.18
  8.4 0.1 copy.17
  8.6 12.7 %all_to_all.20 = bf16[4,136,288]{2,1,0:T(8,128)(2,1)} all-to-all(bf16[4,136,288]{2,1,0:T(8,128)(2,1)S(1)} %broadcast_in_dim.21), channel_id=1, replica_groups=mesh['y'=4,'z'=8,'x'=4,'core'=2] {'y'}, dimensions={0} | all-to-all | bytes 626688 | tf_op jit(solution)/shard_map/all_to_all | solution.py:284
  21.3 0.0 all-gather.5.cloned.1.call-update
  21.3 0.0 all-gather.7.cloned.1.call-start
  21.5 10.0 %all_to_all.21 = bf16[4,152,256]{2,1,0:T(8,128)(2,1)} all-to-all(bf16[4,152,256]{2,1,0:T(8,128)(2,1)S(1)} %broadcast_in_dim.24), channel_id=1, replica_groups=mesh['y'=4,'z'=8,'x'=4,'core'=2] {'y'}, dimensions={0} | all-to-all | bytes 622592 | tf_op jit(solution)/shard_map/all_to_all | solution.py:284
  31.5 0.0 all-gather.7.cloned.1.call-update
  31.6 36.3 %all-gather.5.cloned.1.call-done = bf16[32,136,288]{2,1,0:T(8,128)(2,1)} async-done(((bf16[4,136,288]{2,1,0:T(8,128)(2,1)}), bf16[32,136,288]{2,1,0:T(8,128)(2,1)}) %all-gather.5.cloned.1.call-update) | async-done | bytes 2506768 | tf_op jit(solution)/shard_map/all_gather | solution.py:306
  67.9 42.4 %all-gather.7.cloned.1.call-done = bf16[32,152,256]{2,1,0:T(8,128)(2,1)} async-done(((bf16[4,152,256]{2,1,0:T(8,128)(2,1)}), bf16[32,152,256]{2,1,0:T(8,128)(2,1)}) %all-gather.7.cloned.1.call-update) | async-done | bytes 2490384 | tf_op jit(solution)/shard_map/all_gather | solution.py:308
  110.3 0.9 slice.3
  111.2 3.1 %collective-permute-start = (bf16[8,8192]{1,0:T(8,128)(2,1)S(1)}, bf16[8,8192]{1,0:T(8,128)(2,1)S(1)}, u32[]{:S(2)}, u32[]{:S(2)}) collective-permute-start(bf16[8,8192]{1,0:T(8,128)(2,1)S(1)} %slice.3), channel_id=1, source_target_pairs={{0,8},{8,16},{16,24},{24,32},{32,40},{40,48},{48,56},{56,64},{64,7... | collective-permute-start | bytes 393224 | tf_op jit(solution)/shard_map/ppermute | solution.py:311
  114.3 4.7 %collective-permute-done.prior_ref = bf16[8,8192]{1,0:T(8,128)(2,1)S(1)} collective-permute-done((bf16[8,8192]{1,0:T(8,128)(2,1)S(1)}, bf16[8,8192]{1,0:T(8,128)(2,1)S(1)}, u32[]{:S(2)}, u32[]{:S(2)}) %collective-permute-start) | collective-permute-done | bytes 131104 | tf_op jit(solution)/shard_map/ppermute | solution.py:311
  119.0 0.6 copy-done.2
  119.7 1.8 copy-done.1
  121.4 11.9 %front.1 = (bf16[128,8192]{1,0:T(8,128)(2,1)}, bf16[128,256]{1,0:T(8,128)(2,1)}, f32[4096,128]{1,0:T(8,128)}) custom-call(s32[1]{0:T(128)} %bitcast.core_ref, bf16[128,8192]{1,0:T(8,128)(2,1)} %ci_ref.1, bf16[8,8192]{1,0:T(8,128)(2,1)} %copy-done.2, bf16[8,4,136,288]{3,2,1,0:T(8,128)(2,1)} %bitcast.5, bf16[8,4,136,288]{3,2,1,0:T(8,128)(2,1)} %copy-done.1, ...), custom_call_target="tpu_custom_call" | custom-call | tf_op jit(solution)/shard_map/front/pallas_call | solution.py:71
  133.3 35.3 %scan.1 = (f32[8,1024,128]{2,1,0:T(8,128)}, f32[8,1024,128]{2,1,0:T(8,128)}, f32[8,128,128]{2,1,0:T(8,128)}, bf16[32,40,128]{2,1,0:T(8,128)(2,1)}) custom-call(s32[1]{0:T(128)} %bitcast.core_ref, bf16[128,256]{1,0:T(8,128)(2,1)} %get-tuple-element.12.normed_ref, bf16[128,8192]{1,0:T(8,128)(2,1)} %get-tuple-element.13.xc_ref, ...), custom_call_target="tpu_custom_call" | custom-call | tf_op jit(solution)/shard_map/scan/pallas_call | solution.py:175
  168.7 22.5 %all_to_all.22.ends_ref = bf16[32,40,128]{2,1,0:T(8,128)(2,1)} all-to-all(bf16[32,40,128]{2,1,0:T(8,128)(2,1)} %get-tuple-element.18), channel_id=1, replica_groups=mesh['y'=4,'z'=8,'x'=4,'core'=2] {'y','z'}, dimensions={0} | all-to-all | bytes 655360 | tf_op jit(solution)/shard_map/all_to_all | solution.py:315
  191.2 1.8 link.1
  193.0 16.2 %all_to_all.23.start_ref = bf16[32,32,128]{2,1,0:T(8,128)(2,1)} all-to-all(bf16[32,32,128]{2,1,0:T(8,128)(2,1)} %link.1), channel_id=1, replica_groups=mesh['y'=4,'z'=8,'x'=4,'core'=2] {'y','z'}, dimensions={0} | all-to-all | bytes 524288 | tf_op jit(solution)/shard_map/all_to_all | solution.py:317
  209.1 26.8 %close.1 = bf16[128,8192]{1,0:T(8,128)(2,1)} custom-call(f32[8,1024,128]{2,1,0:T(8,128)} %get-tuple-element.15.step_ref, f32[8,1024,128]{2,1,0:T(8,128)} %get-tuple-element.16.y_ref, f32[8,128,128]{2,1,0:T(8,128)} %get-tuple-element.17.rate_ref, bf16[32,32,128]{2,1,0:T(8,128)(2,1)} %all_to_all.23.start_ref, f32[4096,128]{1,0:T(8,128)} %get-tuple-element.14.bc_ref.c_ref, ...), custom_call_target="tpu_custom_call" | custom-call | tf_op jit(solution)/shard_map/close/pallas_call | solution.py:263
  (28 shorter events, 0.2 us)
Async XLA Ops:
  6.5 1.8 copy-start
  6.5 14.8 %copy-start.6 = (f32[256]{0:T(256)S(1)}, f32[256]{0:T(256)}, u32[]{:S(2)}) copy-start(f32[256]{0:T(256)} %param.19) | copy-start | bytes 3076
  6.5 14.8 %copy-start.5 = (f32[256]{0:T(256)S(1)}, f32[256]{0:T(256)}, u32[]{:S(2)}) copy-start(f32[256]{0:T(256)} %param.17) | copy-start | bytes 3076
  6.5 14.9 %copy-start.3 = (f32[16,256]{1,0:T(8,128)S(1)}, f32[16,256]{1,0:T(8,128)}, u32[]{:S(2)}) copy-start(f32[16,256]{1,0:T(8,128)} %log_ref.1) | copy-start | bytes 49156
  6.5 14.9 %copy-start.4 = (bf16[256,256]{1,0:T(8,128)(2,1)S(1)}, bf16[256,256]{1,0:T(8,128)(2,1)}, u32[]{:S(2)}) copy-start(bf16[256,256]{1,0:T(8,128)(2,1)} %param.16) | copy-start | bytes 393220
  6.5 61.4 %all-gather.5.cloned.1.call-start = ((), (), s32[]{:S(2)}) async-start(), calls=%async_computation.4 | async-start | bytes 3760128 | tf_op jit(solution)/shard_map/all_gather | solution.py:306
  21.3 89.0 %all-gather.7.cloned.1.call-start = ((), (), s32[]{:S(2)}) async-start(), calls=%async_computation.5 | async-start | bytes 2801664 | tf_op jit(solution)/shard_map/all_gather | solution.py:308
  67.9 51.1 %collective-permute-start.1 = (bf16[8,4,136,288]{3,2,1,0:T(8,128)(2,1)}, bf16[8,4,136,288]{3,2,1,0:T(8,128)(2,1)S(1)}, u32[]{:S(2)}, u32[]{:S(2)}) collective-permute-start(bf16[8,4,136,288]{3,2,1,0:T(8,128)(2,1)} %bitcast.4), channel_id=1, source_target_pairs={{0,1},{1,0},{2,3},{3,2},{4,5},{5,4},{6,7},{7,6},{8,9},{9,8},{10,11... | collective-permute-start | bytes 7520264 | tf_op jit(solution)/shard_map/ppermute | solution.py:309
  110.3 23.0 %collective-permute-start.2 = (bf16[8,4,152,256]{3,2,1,0:T(8,128)(2,1)}, bf16[8,4,152,256]{3,2,1,0:T(8,128)(2,1)}, u32[]{:S(2)}, u32[]{:S(2)}) collective-permute-start(bf16[8,4,152,256]{3,2,1,0:T(8,128)(2,1)} %bitcast.6), channel_id=1, source_target_pairs={{0,1},{1,0},{2,3},{3,2},{4,5},{5,4},{6,7},{7,6},{8,9},{9,8},{10,11... | collective-permute-start | bytes 7471112 | tf_op jit(solution)/shard_map/ppermute | solution.py:310
  111.2 7.8 %collective-permute-start = (bf16[8,8192]{1,0:T(8,128)(2,1)S(1)}, bf16[8,8192]{1,0:T(8,128)(2,1)S(1)}, u32[]{:S(2)}, u32[]{:S(2)}) collective-permute-start(bf16[8,8192]{1,0:T(8,128)(2,1)S(1)} %slice.3), channel_id=1, source_target_pairs={{0,8},{8,16},{16,24},{24,32},{32,40},{40,48},{48,56},{56,64},{64,7... | collective-permute-start | bytes 393224 | tf_op jit(solution)/shard_map/ppermute | solution.py:311
  119.0 0.6 copy-start.2
  119.7 1.8 copy-start.1
Sparse Core Ops, SparseCore 0:
  21.4 46.4 all-gather.4
  69.7 40.5 all-gather.6

commit v2 on v1

--- a/solution.py
+++ b/solution.py
@@ -26,32 +26,53 @@
     return high.astype(BF16), (v - high).astype(BF16)
 
 
-def front_kernel(core_ref, ci_ref, prior_ref, own_ref, oth_ref, gain_ref, xc_ref, normed_ref, bc_ref, pad_ref, acc_ref):
-    step = pl.program_id(0)
-    core = core_ref[0]
+def conv_kernel(ci_ref, prior_ref, par_ref, xc_ref, pad_ref):
     rows = ci_ref.shape[0]
     taps = 4
     pad_ref[0:8, :] = prior_ref[...].astype(F32)
     pad_ref[8 : 8 + rows, :] = ci_ref[...].astype(F32)
-
-    @pl.when(step == 0)
-    def _():
-        acc_ref[...] = jnp.zeros_like(acc_ref)
-
-    acc = acc_ref[...]
     for s in range(4):
-        mine = own_ref[s, 0, 128:136, 0:SHARD].astype(F32)
-        other = oth_ref[s, 0, 128:136, 0:SHARD].astype(F32)
-        par = jnp.where(core == 0, mine, other)
+        par = par_ref[s, 0].astype(F32)
         lanes = slice(s * SHARD, (s + 1) * SHARD)
         total = jnp.broadcast_to(par[taps : taps + 1, :], (rows, SHARD))
         for k in range(taps):
             total = total + par[k : k + 1, :] * pad_ref[5 + k : 5 + k + rows, lanes]
         xc_ref[:, lanes] = silu(total).astype(BF16)
+
+
+def conv(conv_input, prior, params):
+    rows, inner = conv_input.shape
+    return pl.pallas_call(
+        conv_kernel,
+        grid=(inner // BLK,),
+        in_specs=[
+            pl.BlockSpec((rows, BLK), lambda b: (0, b)),
+            pl.BlockSpec((8, BLK), lambda b: (0, b)),
+            pl.BlockSpec((4, 1, 8, SHARD), lambda b: (b % 2, b // 2, 0, 0)),
+        ],
+        out_specs=pl.BlockSpec((rows, BLK), lambda b: (0, b)),
+        out_shape=jax.ShapeDtypeStruct((rows, inner), BF16),
+        scratch_shapes=[pltpu.VMEM((rows + 8, BLK), F32)],
+        compiler_params=pltpu.CompilerParams(dimension_semantics=("arbitrary",)),
+        name="conv",
+    )(conv_input, prior, params)
+
+
+def front_kernel(core_ref, xc_ref, own_ref, oth_ref, gain_ref, normed_ref, bc_ref, acc_ref):
+    step = pl.program_id(0)
+    core = core_ref[0]
+    rows = xc_ref.shape[0]
+
+    @pl.when(step == 0)
+    def _():
+        acc_ref[...] = jnp.zeros_like(acc_ref)
+
+    acc = acc_ref[...]
+    for s in range(4):
         at = pl.multiple_of(s * SHARD + core * 128, 128)
-        acc = acc + jnp.dot(xc_ref[:, pl.ds(at, 128)], own_ref[s, 0, 0:128, :], preferred_element_type=F32)
+        acc = acc + jnp.dot(xc_ref[:, pl.ds(at, 128)], own_ref[s, 0], preferred_element_type=F32)
         at = pl.multiple_of(s * SHARD + (1 - core) * 128, 128)
-        acc = acc + jnp.dot(xc_ref[:, pl.ds(at, 128)], oth_ref[s, 0, 0:128, :], preferred_element_type=F32)
+        acc = acc + jnp.dot(xc_ref[:, pl.ds(at, 128)], oth_ref[s, 0], preferred_element_type=F32)
     acc_ref[...] = acc
 
     @pl.when(step == pl.num_programs(0) - 1)
@@ -65,47 +86,44 @@
             bc_ref[m * rows : (m + 1) * rows, :] = jnp.broadcast_to(col, (rows, 128))
 
 
-def front(core, conv_input, prior, x_own, x_oth, gain):
-    rows, inner = conv_input.shape
-    wspec = pl.BlockSpec((4, 1, 136, 288), lambda b: (b % 2, b // 2, 0, 0))
+def front(core, xc, x_own, x_oth, gain):
+    rows, inner = xc.shape
+    wspec = pl.BlockSpec((4, 1, 128, 288), lambda b: (b % 2, b // 2, 0, 0))
     return pl.pallas_call(
         front_kernel,
         grid=(inner // BLK,),
         in_specs=[
             pl.BlockSpec(memory_space=pltpu.SMEM),
             pl.BlockSpec((rows, BLK), lambda b: (0, b)),
-            pl.BlockSpec((8, BLK), lambda b: (0, b)),
             wspec,
             wspec,
             pl.BlockSpec((1, 256), lambda b: (0, 0)),
         ],
         out_specs=[
-            pl.BlockSpec((rows, BLK), lambda b: (0, b)),
             pl.BlockSpec((rows, 256), lambda b: (0, 0)),
             pl.BlockSpec((32 * rows, 128), lambda b: (0, 0)),
         ],
         out_shape=[
-            jax.ShapeDtypeStruct((rows, inner), BF16),
             jax.ShapeDtypeStruct((rows, 256), BF16),
             jax.ShapeDtypeStruct((32 * rows, 128), F32),
         ],
-        scratch_shapes=[pltpu.VMEM((rows + 8, BLK), F32), pltpu.VMEM((rows, 288), F32)],
+        scratch_shapes=[pltpu.VMEM((rows, 288), F32)],
         compiler_params=pltpu.CompilerParams(dimension_semantics=("arbitrary",)),
         name="front",
-    )(core, conv_input, prior, x_own, x_oth, gain)
-
-
-def scan_kernel(core_ref, normed_ref, xc_ref, own_ref, oth_ref, bc_ref, step_ref, y_ref, rate_ref, ends_ref, x_scr, par_scr, h_scr):
-    core = core_ref[0]
+    )(core, xc, x_own, x_oth, gain)
+
+
+def scan_kernel(where_ref, normed_ref, xc_ref, own_ref, oth_ref, bc_ref, step_ref, y_ref, rate_ref, ends_ref, x_scr, par_scr, h_scr):
+    core = where_ref[0]
     rows = normed_ref.shape[0]
     mine_k = normed_ref[:, pl.ds(pl.multiple_of(core * 128, 128), 128)]
     other_k = normed_ref[:, pl.ds(pl.multiple_of((1 - core) * 128, 128), 128)]
     skips = []
     for s in range(4):
-        raw = jnp.dot(mine_k, own_ref[s, 0, 0:128, :], preferred_element_type=F32)
-        raw = raw + jnp.dot(other_k, oth_ref[s, 0, 0:128, :], preferred_element_type=F32)
-        mine = own_ref[s, 0, 128:152, :].astype(F32)
-        other = oth_ref[s, 0, 128:152, :].astype(F32)
+        raw = jnp.dot(mine_k, own_ref[0, s, 0:128, :], preferred_element_type=F32)
+        raw = raw + jnp.dot(other_k, oth_ref[0, s, 0:128, :], preferred_element_type=F32)
+        mine = own_ref[0, s, 128:152, :].astype(F32)
+        other = oth_ref[0, s, 128:152, :].astype(F32)
         mine_log = mine[0:8] + mine[8:16]
         other_log = other[0:8] + other[8:16]
         mine_vec = mine[16:17] + mine[17:18]
@@ -153,7 +171,7 @@
         return total + now, tuple(fresh)
 
     zero = jnp.zeros((8, 128), F32)
-    total, state = lax.fori_loop(0, rows, advance, (zero, (zero,) * 16))
+    total, state = lax.fori_loop(0, rows, advance, (zero, (zero,) * 16), unroll=4)
     for n in range(16):
         h_scr[8 * n : 8 * n + 8, :] = state[n]
     high = total.astype(BF16).astype(F32)
@@ -168,41 +186,44 @@
         ends_ref[jj, 32:40, :] = jnp.concatenate(sums, 0).astype(BF16)
 
 
-def scan(core, normed, xc, d_own, d_oth, bc):
+def scan(where, normed, xc, d_own, d_oth, bc):
     rows, inner = xc.shape
     blocks = inner // BLK
-    wspec = pl.BlockSpec((4, 1, 152, 256), lambda b: (b % 2, b // 2, 0, 0))
-    return pl.pallas_call(
-        scan_kernel,
+    wspec = pl.BlockSpec((1, 4, 152, 256), lambda b, where: ((b // 2 + 4 - where[1]) % 4, b % 2, 0, 0))
+    grid_spec = pltpu.PrefetchScalarGridSpec(
+        num_scalar_prefetch=1,
         grid=(blocks,),
         in_specs=[
-            pl.BlockSpec(memory_space=pltpu.SMEM),
-            pl.BlockSpec((rows, 256), lambda b: (0, 0)),
-            pl.BlockSpec((rows, BLK), lambda b: (0, b)),
+            pl.BlockSpec((rows, 256), lambda b, where: (0, 0)),
+            pl.BlockSpec((rows, BLK), lambda b, where: (0, b)),
             wspec,
             wspec,
-            pl.BlockSpec((32 * rows, 128), lambda b: (0, 0)),
+            pl.BlockSpec((32 * rows, 128), lambda b, where: (0, 0)),
         ],
         out_specs=[
-            pl.BlockSpec((1, 8 * rows, 128), lambda b: (b, 0, 0)),
-            pl.BlockSpec((1, 8 * rows, 128), lambda b: (b, 0, 0)),
-            pl.BlockSpec((1, 128, 128), lambda b: (b, 0, 0)),
-            pl.BlockSpec((4, 40, 128), lambda b: (b, 0, 0)),
-        ],
+            pl.BlockSpec((1, 8 * rows, 128), lambda b, where: (b, 0, 0)),
+            pl.BlockSpec((1, 8 * rows, 128), lambda b, where: (b, 0, 0)),
+            pl.BlockSpec((1, 128, 128), lambda b, where: (b, 0, 0)),
+            pl.BlockSpec((4, 40, 128), lambda b, where: (b, 0, 0)),
+        ],
+        scratch_shapes=[
+            pltpu.VMEM((8 * rows, 128), F32),
+            pltpu.VMEM((128, 128), F32),
+            pltpu.VMEM((144, 128), F32),
+        ],
+    )
+    return pl.pallas_call(
+        scan_kernel,
+        grid_spec=grid_spec,
         out_shape=[
             jax.ShapeDtypeStruct((blocks, 8 * rows, 128), F32),
             jax.ShapeDtypeStruct((blocks, 8 * rows, 128), F32),
             jax.ShapeDtypeStruct((blocks, 128, 128), F32),
             jax.ShapeDtypeStruct((4 * blocks, 40, 128), BF16),
         ],
-        scratch_shapes=[
-            pltpu.VMEM((8 * rows, 128), F32),
-            pltpu.VMEM((128, 128), F32),
-            pltpu.VMEM((144, 128), F32),
-        ],
         compiler_params=pltpu.CompilerParams(dimension_semantics=("arbitrary",)),
         name="scan",
-    )(core, normed, xc, d_own, d_oth, bc)
+    )(where, normed, xc, d_own, d_oth, bc)
 
 
 def link_kernel(ends_ref, log_ref, start_ref):
@@ -248,7 +269,7 @@
         y_scr[pl.ds(at, 8), :] = even + odd
         return total
 
-    lax.fori_loop(0, rows, advance, jnp.zeros((8, 128), F32))
+    lax.fori_loop(0, rows, advance, jnp.zeros((8, 128), F32), unroll=4)
     for j in range(8):
         for i in range(rows // 16):
             low = y_scr[pl.ds(128 * i + j, 8, stride=8), :]
@@ -298,22 +319,34 @@
     return jnp.concatenate(pieces, 0)
 
 
+def around(block, axis):
+    up = [(i, (i + 1) % 4) for i in range(4)]
+    down = [(i, (i - 1) % 4) for i in range(4)]
+    previous = lax.ppermute(block, axis, up)
+    following = lax.ppermute(block, axis, down)
+    half = block.shape[0] // 2
+    opposite = [lax.ppermute(previous[:half], axis, up), lax.ppermute(following[half:], axis, down)]
+    return jnp.concatenate([block, following, *opposite, previous], 0).reshape(4, *block.shape)
+
+
 def local(conv_input, gate_input, conv_weight, conv_bias, x_weight, dt_gain, dt_weight, dt_bias, a_log, skip):
     core = lax.axis_index("core")
     count = lax.axis_size(SEQ)
     swap = [(0, 1), (1, 0)]
+    prior = lax.ppermute(conv_input[conv_input.shape[0] - 8 :], SEQ, [(i, i + 1) for i in range(count - 1)])
     x_part = from_everyone(pack_x(core, x_weight, conv_weight, conv_bias), "y")
-    x_own = lax.all_gather(x_part, "z", axis=0)
-    d_part = from_everyone(pack_d(core, dt_weight, dt_bias, a_log, skip), "y")
-    d_own = lax.all_gather(d_part, "z", axis=0)
+    x_own = lax.all_gather(x_part[:, :128], "z", axis=0)
+    params = x_part[:, 128:136, :SHARD].reshape(32, SHARD)
+    d_part = from_everyone(jnp.concatenate([pack_d(core, dt_weight, dt_bias, a_log, skip), params], 0), "z")
+    d_part = d_part.reshape(8, 184, SHARD)
+    xc = conv(conv_input, prior, d_part[:, 152:].reshape(8, 4, 8, SHARD))
+    d_own = around(d_part[:, :152], "y")
+    d_oth = lax.ppermute(d_own, "core", swap)
     x_oth = lax.ppermute(x_own, "core", swap)
-    d_oth = lax.ppermute(d_own, "core", swap)
-    prior = lax.ppermute(conv_input[conv_input.shape[0] - 8 :], SEQ, [(i, i + 1) for i in range(count - 1)])
-    which = core.reshape(1).astype(jnp.int32)
-    xc, normed, bc = front(which, conv_input, prior, x_own, x_oth, dt_gain[None, :])
-    step, y, rate, ends = scan(which, normed, xc, d_own, d_oth, bc)
+    where = jnp.stack([core, lax.axis_index("y")]).astype(jnp.int32)
+    normed, bc = front(where, xc, x_own, x_oth, dt_gain[None, :])
+    step, y, rate, ends = scan(where, normed, xc, d_own, d_oth, bc)
     ends = lax.all_to_all(ends, SEQ, split_axis=0, concat_axis=0, tiled=True)
-    ends = ends.reshape(count, 40, 128)
     start = lax.all_to_all(link(ends, a_log), SEQ, split_axis=0, concat_axis=0, tiled=True)
     return close(step, y, rate, start, bc, gate_input)
 

time: 244 us -> 211 us (0.86)
  waiting for transfers between devices: 83.4 us -> 20.3 us
  blocking collectives: 61.4 us -> 84.5 us
  local copies, waits for them, and re-layouts: 4.55 us -> 14.5 us
  Pallas kernels: 75.8 us -> 66.4 us
  starting transfers between devices: 3.2 us -> 9.49 us
    all_gather x2 -> x1, waiting for transfers between devices: 78.7 us -> 0.02 us  [local(): x_own = lax.all_gather(x_part[:, :128], 'z', axis=0)]
    all_to_all x2, blocking collectives: 22.7 us -> 47.5 us  [from_everyone(): return lax.all_to_all(copies, axis, split_axis=0, concat_axis=0, tiled=True)]
    ppermute x0 -> x4, waiting for transfers between devices: none -> 16.3 us  [the longest x1 11.5 us: around(): previous = lax.ppermute(block, axis, up)]
    pallas_call x1, Pallas kernels: 26.8 us -> 18.7 us  [close(): pl.pallas_call(close_kernel, grid=(inner // BLK,), in_specs=[pl.BlockSpec...]
    ppermute x0 -> x4, starting transfers between devices: none -> 6.68 us  [the longest x1 3.29 us: around(): lax.ppermute(following[half:], axis, down)]
    ppermute x0 -> x1, local copies, waits for them, and re-layouts: none -> 4.49 us  [local(): x_oth = lax.ppermute(x_own, 'core', swap)]
    all_gather x0 -> x1, local copies, waits for them, and re-layouts: none -> 4.48 us  [local(): x_own = lax.all_gather(x_part[:, :128], 'z', axis=0)]
    pallas_call x1, Pallas kernels: 11.9 us -> 9.12 us  [front(): pl.pallas_call(front_kernel, grid=(inner // BLK,), in_specs=[pl.BlockSpec...]
  transfers between devices with their start and end apart: 5 -> 8, of which waited for: 3 -> 3; matrix products, arithmetic and copies ran while one was open for 0% -> 6% of each run, Pallas kernels for 5% -> 8%
where the time goes in v2:
time: 211 us; the launch traced here: 210 us
  blocking collectives  84.5 us (40%)
  Pallas kernels  66.4 us (31%)
  waiting for transfers between devices  20.3 us (10%)
  local copies, waits for them, and re-layouts  14.5 us (7%)
  between operations  13.6 us (6%)
  starting transfers between devices  9.49 us (4%)
    all_to_all x2, blocking collectives, from_everyone(): return lax.all_to_all(copies, axis, split_axis=0, concat_axis=0, tiled=True)  47.5 us
    pallas_call x1, Pallas kernels, scan(): pl.pallas_call(scan_kernel, grid_spec=grid_spec, out_shape=[jax.ShapeDtyp...  29.2 us
    all_to_all x1, blocking collectives, local(): ends = lax.all_to_all(ends, SEQ, split_axis=0, concat_axis=0, tiled=True)  21.1 us
    pallas_call x1, Pallas kernels, close(): pl.pallas_call(close_kernel, grid=(inner // BLK,), in_specs=[pl.BlockSpec...  18.7 us
    all_to_all x1, blocking collectives, local(): lax.all_to_all(link(ends, a_log), SEQ, split_axis=0, concat_axis=0, tiled...  15.9 us
    ppermute x1, waiting for transfers between devices, around(): previous = lax.ppermute(block, axis, up)  11.5 us
    pallas_call x1, Pallas kernels, front(): pl.pallas_call(front_kernel, grid=(inner // BLK,), in_specs=[pl.BlockSpec...  9.12 us
    pallas_call x1, Pallas kernels, conv(): pl.pallas_call(conv_kernel, grid=(inner // BLK,), in_specs=[pl.BlockSpec(...  7.6 us
  transfers between devices with their start and end apart: 8, of which 3 were waited for; matrix products, arithmetic and copies ran while one was open for 6% of the time, Pallas kernels for 8%

profile of v2, /device:TPU:32, one launch (start us, length us, event | category | flops | bytes accessed | tf_op | source)
XLA Modules:
  0.0 210.2 jit_solution(1639550758023465648)
XLA Ops:
  6.6 0.8 broadcast_in_dim.20
  7.5 0.8 maximum_maximum_fusion
  8.6 12.6 %all_to_all.20 = bf16[4,136,288]{2,1,0:T(8,128)(2,1)S(1)} all-to-all(bf16[4,136,288]{2,1,0:T(8,128)(2,1)S(1)} %broadcast_in_dim.22), channel_id=1, replica_groups=mesh['y'=4,'z'=8,'x'=4,'core'=2] {'y'}, dimensions={0} | all-to-all | bytes 626688 | tf_op jit(solution)/shard_map/all_to_all | solution.py:305
  21.2 0.9 copy.22
  22.4 34.9 %all_to_all.21 = bf16[8,184,256]{2,1,0:T(8,128)(2,1)S(1)} all-to-all(bf16[8,184,256]{2,1,0:T(8,128)(2,1)S(1)} %broadcast_in_dim.23), channel_id=1, replica_groups=mesh['y'=4,'z'=8,'x'=4,'core'=2] {'z'}, dimensions={0} | all-to-all | bytes 1507328 | tf_op jit(solution)/shard_map/all_to_all | solution.py:305
  57.6 3.1 %collective-permute-start.2 = (bf16[8,152,256]{2,1,0:T(8,128)(2,1)S(1)}, bf16[8,152,256]{2,1,0:T(8,128)(2,1)S(1)}, u32[]{:S(2)}, u32[]{:S(2)}) collective-permute-start(bf16[8,152,256]{2,1,0:T(8,128)(2,1)S(1)} %get-tuple-element.17), channel_id=1, source_target_pairs={{0,192},{64,0},{128,64},{192,128},{1,193},{65,1},{129,65},{193,129... | collective-permute-start | bytes 1867784 | tf_op jit(solution)/shard_map/ppermute | solution.py:326
  60.7 11.5 %collective-permute-done.3 = bf16[8,152,256]{2,1,0:T(8,128)(2,1)S(1)} collective-permute-done((bf16[8,152,256]{2,1,0:T(8,128)(2,1)S(1)}, bf16[8,152,256]{2,1,0:T(8,128)(2,1)S(1)}, u32[]{:S(2)}, u32[]{:S(2)}) %collective-permute-start.3) | collective-permute-done | bytes 622624 | tf_op jit(solution)/shard_map/ppermute | solution.py:325
  72.4 3.3 %collective-permute-start.5 = (bf16[4,152,256]{2,1,0:T(8,128)(2,1)S(1)}, bf16[4,152,256]{2,1,0:T(8,128)(2,1)S(1)}, u32[]{:S(2)}, u32[]{:S(2)}) collective-permute-start(bf16[4,152,256]{2,1,0:T(8,128)(2,1)S(1)} %slice.33), channel_id=1, source_target_pairs={{0,192},{64,0},{128,64},{192,128},{1,193},{65,1},{129,65},{193,129... | collective-permute-start | bytes 933896 | tf_op jit(solution)/shard_map/ppermute | solution.py:328
  75.7 4.7 %collective-permute-done.4 = bf16[4,152,256]{2,1,0:T(8,128)(2,1)S(1)} collective-permute-done((bf16[4,152,256]{2,1,0:T(8,128)(2,1)S(1)}, bf16[4,152,256]{2,1,0:T(8,128)(2,1)S(1)}, u32[]{:S(2)}, u32[]{:S(2)}) %collective-permute-start.4) | collective-permute-done | bytes 311328 | tf_op jit(solution)/shard_map/ppermute | solution.py:328
  81.2 1.7 slice.21
  82.9 2.2 %collective-permute-start = (bf16[8,8192]{1,0:T(8,128)(2,1)}, bf16[8,8192]{1,0:T(8,128)(2,1)S(1)}, u32[]{:S(2)}, u32[]{:S(2)}) collective-permute-start(bf16[8,8192]{1,0:T(8,128)(2,1)} %slice.21), channel_id=1, source_target_pairs={{0,8},{8,16},{16,24},{24,32},{32,40},{40,48},{48,56},{56,64},{64,7... | collective-permute-start | bytes 393224 | tf_op jit(solution)/shard_map/ppermute | solution.py:336
  85.1 0.6 pad_add_fusion.core_ref.where_ref
  85.7 0.7 slice_bitcast_fusion.par_ref
  86.4 4.0 %collective-permute-done.prior_ref = bf16[8,8192]{1,0:T(8,128)(2,1)S(1)} collective-permute-done((bf16[8,8192]{1,0:T(8,128)(2,1)}, bf16[8,8192]{1,0:T(8,128)(2,1)S(1)}, u32[]{:S(2)}, u32[]{:S(2)}) %collective-permute-start) | collective-permute-done | bytes 131104 | tf_op jit(solution)/shard_map/ppermute | solution.py:336
  90.4 0.7 copy-done.2
  91.0 7.6 %conv.1.xc_ref = bf16[128,8192]{1,0:T(8,128)(2,1)} custom-call(bf16[128,8192]{1,0:T(8,128)(2,1)} %ci_ref.1, bf16[8,8192]{1,0:T(8,128)(2,1)} %copy-done.2, bf16[8,4,8,256]{3,2,1,0:T(8,128)(2,1)} %slice_bitcast_fusion.par_ref), custom_call_target="tpu_custom_call" | custom-call | tf_op jit(solution)/shard_map/conv/pallas_call | solution.py:45
  98.6 4.5 %copy.23 = bf16[32,128,288]{2,1,0:T(8,128)(2,1)} copy(bf16[32,128,288]{1,2,0:T(8,128)(2,1)} %all-gather.3.cloned.1.call-done) | data formatting | bytes 4718592 | tf_op jit(solution)/shard_map/all_gather | solution.py:338
  103.1 4.5 %copy.25.oth_ref = bf16[8,4,128,288]{3,2,1,0:T(8,128)(2,1)} copy(bf16[8,4,128,288]{2,3,1,0:T(8,128)(2,1)} %collective-permute-done.1) | data formatting | bytes 4718592 | tf_op jit(solution)/shard_map/ppermute | solution.py:345
  107.6 9.1 %front.1 = (bf16[128,256]{1,0:T(8,128)(2,1)}, f32[4096,128]{1,0:T(8,128)}) custom-call(s32[2]{0:T(128)} %pad_add_fusion.core_ref.where_ref, bf16[128,8192]{1,0:T(8,128)(2,1)} %conv.1.xc_ref, bf16[8,4,128,288]{3,2,1,0:T(8,128)(2,1)} %bitcast.10, bf16[8,4,128,288]{3,2,1,0:T(8,128)(2,1)} %copy.25.oth_ref, f32[1,256]{1,0:T(1,128)} %bitcast.14), custom_call_target="tpu_custom_call" | custom-call | tf_op jit(solution)/shard_map/front/pallas_call | solution.py:92
  116.7 29.2 %scan.1 = (f32[8,1024,128]{2,1,0:T(8,128)}, f32[8,1024,128]{2,1,0:T(8,128)}, f32[8,128,128]{2,1,0:T(8,128)}, bf16[32,40,128]{2,1,0:T(8,128)(2,1)}) custom-call(s32[2]{0:T(128)} %pad_add_fusion.core_ref.where_ref, bf16[128,256]{1,0:T(8,128)(2,1)} %get-tuple-element.11.normed_ref, bf16[128,8192]{1,0:T(8,128)(2,1)} %conv.1.xc_ref, ...), custom_call_target="tpu_custom_call" | custom-call | tf_op jit(solution)/shard_map/scan/pallas_call | solution.py:215
  145.9 21.1 %all_to_all.22.ends_ref = bf16[32,40,128]{2,1,0:T(8,128)(2,1)} all-to-all(bf16[32,40,128]{2,1,0:T(8,128)(2,1)} %get-tuple-element.16), channel_id=1, replica_groups=mesh['y'=4,'z'=8,'x'=4,'core'=2] {'y','z'}, dimensions={0} | all-to-all | bytes 655360 | tf_op jit(solution)/shard_map/all_to_all | solution.py:349
  167.0 1.8 link.1
  168.8 15.9 %all_to_all.23.start_ref = bf16[32,32,128]{2,1,0:T(8,128)(2,1)} all-to-all(bf16[32,32,128]{2,1,0:T(8,128)(2,1)} %link.1), channel_id=1, replica_groups=mesh['y'=4,'z'=8,'x'=4,'core'=2] {'y','z'}, dimensions={0} | all-to-all | bytes 524288 | tf_op jit(solution)/shard_map/all_to_all | solution.py:350
  184.7 18.7 %close.1 = bf16[128,8192]{1,0:T(8,128)(2,1)} custom-call(f32[8,1024,128]{2,1,0:T(8,128)} %get-tuple-element.13.step_ref, f32[8,1024,128]{2,1,0:T(8,128)} %get-tuple-element.14.y_ref, f32[8,128,128]{2,1,0:T(8,128)} %get-tuple-element.15.rate_ref, bf16[32,32,128]{2,1,0:T(8,128)(2,1)} %all_to_all.23.start_ref, f32[4096,128]{1,0:T(8,128)} %get-tuple-element.12.bc_ref.c_ref, ...), custom_call_target="tpu_custom_call" | custom-call | tf_op jit(solution)/shard_map/close/pallas_call | solution.py:284
  (48 shorter events, 1.8 us)
Async XLA Ops:
  6.5 1.8 copy-start
  6.5 15.6 %copy-start.6 = (f32[256]{0:T(256)S(1)}, f32[256]{0:T(256)}, u32[]{:S(2)}) copy-start(f32[256]{0:T(256)} %param.19) | copy-start | bytes 3076
  6.5 15.6 %copy-start.5 = (f32[256]{0:T(256)S(1)}, f32[256]{0:T(256)}, u32[]{:S(2)}) copy-start(f32[256]{0:T(256)} %param.17) | copy-start | bytes 3076
  6.5 15.7 %copy-start.3 = (f32[16,256]{1,0:T(8,128)S(1)}, f32[16,256]{1,0:T(8,128)}, u32[]{:S(2)}) copy-start(f32[16,256]{1,0:T(8,128)} %log_ref.1) | copy-start | bytes 49156
  6.5 15.7 %copy-start.4 = (bf16[256,256]{1,0:T(8,128)(2,1)S(1)}, bf16[256,256]{1,0:T(8,128)(2,1)}, u32[]{:S(2)}) copy-start(bf16[256,256]{1,0:T(8,128)(2,1)} %param.16) | copy-start | bytes 393220
  6.5 74.2 %all-gather.3.cloned.1.call-start = ((), (), s32[]{:S(2)}) async-start(), calls=%async_computation.4 | async-start | bytes 2654208 | tf_op jit(solution)/shard_map/all_gather | solution.py:338
  57.4 14.9 %collective-permute-start.3 = (bf16[8,152,256]{2,1,0:T(8,128)(2,1)S(1)}, bf16[8,152,256]{2,1,0:T(8,128)(2,1)S(1)}, u32[]{:S(2)}, u32[]{:S(2)}) collective-permute-start(bf16[8,152,256]{2,1,0:T(8,128)(2,1)S(1)} %get-tuple-element.17), channel_id=1, source_target_pairs={{0,64},{64,128},{128,192},{192,0},{1,65},{65,129},{129,193},{193,1... | collective-permute-start | bytes 1867784 | tf_op jit(solution)/shard_map/ppermute | solution.py:325
  57.6 14.8 %collective-permute-start.2 = (bf16[8,152,256]{2,1,0:T(8,128)(2,1)S(1)}, bf16[8,152,256]{2,1,0:T(8,128)(2,1)S(1)}, u32[]{:S(2)}, u32[]{:S(2)}) collective-permute-start(bf16[8,152,256]{2,1,0:T(8,128)(2,1)S(1)} %get-tuple-element.17), channel_id=1, source_target_pairs={{0,192},{64,0},{128,64},{192,128},{1,193},{65,1},{129,65},{193,129... | collective-permute-start | bytes 1867784 | tf_op jit(solution)/shard_map/ppermute | solution.py:326
  72.3 8.2 %collective-permute-start.4 = (bf16[4,152,256]{2,1,0:T(8,128)(2,1)S(1)}, bf16[4,152,256]{2,1,0:T(8,128)(2,1)S(1)}, u32[]{:S(2)}, u32[]{:S(2)}) collective-permute-start(bf16[4,152,256]{2,1,0:T(8,128)(2,1)S(1)} %slice.32), channel_id=1, source_target_pairs={{0,64},{64,128},{128,192},{192,0},{1,65},{65,129},{129,193},{193,1... | collective-permute-start | bytes 933896 | tf_op jit(solution)/shard_map/ppermute | solution.py:328
  72.4 8.1 %collective-permute-start.5 = (bf16[4,152,256]{2,1,0:T(8,128)(2,1)S(1)}, bf16[4,152,256]{2,1,0:T(8,128)(2,1)S(1)}, u32[]{:S(2)}, u32[]{:S(2)}) collective-permute-start(bf16[4,152,256]{2,1,0:T(8,128)(2,1)S(1)} %slice.33), channel_id=1, source_target_pairs={{0,192},{64,0},{128,64},{192,128},{1,193},{65,1},{129,65},{193,129... | collective-permute-start | bytes 933896 | tf_op jit(solution)/shard_map/ppermute | solution.py:328
  80.6 18.1 %copy-start.1 = (bf16[32,152,256]{2,1,0:T(8,128)(2,1)}, bf16[32,152,256]{2,1,0:T(8,128)(2,1)S(1)}, u32[]{:S(2)}) copy-start(bf16[32,152,256]{2,1,0:T(8,128)(2,1)S(1)} %constant_dynamic-update-slice_fusion) | copy-start | bytes 7471108
  80.6 36.1 %collective-permute-start.6 = (bf16[4,8,152,256]{3,2,1,0:T(8,128)(2,1)S(1)}, bf16[4,8,152,256]{3,2,1,0:T(8,128)(2,1)}, u32[]{:S(2)}, u32[]{:S(2)}) collective-permute-start(bf16[4,8,152,256]{3,2,1,0:T(8,128)(2,1)S(1)} %bitcast.11), channel_id=1, source_target_pairs={{0,1},{1,0},{2,3},{3,2},{4,5},{5,4},{6,7},{7,6},{8,9},{9,8},{10,11... | collective-permute-start | bytes 7471112 | tf_op jit(solution)/shard_map/ppermute | solution.py:344
  80.7 22.4 %collective-permute-start.1 = (bf16[8,4,128,288]{2,3,1,0:T(8,128)(2,1)}, bf16[8,4,128,288]{2,3,1,0:T(8,128)(2,1)}, u32[]{:S(2)}, u32[]{:S(2)}) collective-permute-start(bf16[8,4,128,288]{2,3,1,0:T(8,128)(2,1)} %bitcast.13), channel_id=1, source_target_pairs={{0,1},{1,0},{2,3},{3,2},{4,5},{5,4},{6,7},{7,6},{8,9},{9,8},{10,11... | collective-permute-start | bytes 7077896 | tf_op jit(solution)/shard_map/ppermute | solution.py:345
  82.9 7.5 %collective-permute-start = (bf16[8,8192]{1,0:T(8,128)(2,1)}, bf16[8,8192]{1,0:T(8,128)(2,1)S(1)}, u32[]{:S(2)}, u32[]{:S(2)}) collective-permute-start(bf16[8,8192]{1,0:T(8,128)(2,1)} %slice.21), channel_id=1, source_target_pairs={{0,8},{8,16},{16,24},{24,32},{32,40},{40,48},{48,56},{56,64},{64,7... | collective-permute-start | bytes 393224 | tf_op jit(solution)/shard_map/ppermute | solution.py:336
  90.4 0.7 copy-start.2
Sparse Core Ops, SparseCore 0:
  22.3 51.0 all-gather.2

commit v3 on v2

--- a/solution.py
+++ b/solution.py
@@ -32,7 +32,7 @@
     pad_ref[0:8, :] = prior_ref[...].astype(F32)
     pad_ref[8 : 8 + rows, :] = ci_ref[...].astype(F32)
     for s in range(4):
-        par = par_ref[s, 0].astype(F32)
+        par = par_ref[0, s].astype(F32)
         lanes = slice(s * SHARD, (s + 1) * SHARD)
         total = jnp.broadcast_to(par[taps : taps + 1, :], (rows, SHARD))
         for k in range(taps):
@@ -48,7 +48,7 @@
         in_specs=[
             pl.BlockSpec((rows, BLK), lambda b: (0, b)),
             pl.BlockSpec((8, BLK), lambda b: (0, b)),
-            pl.BlockSpec((4, 1, 8, SHARD), lambda b: (b % 2, b // 2, 0, 0)),
+            pl.BlockSpec((1, 4, 8, SHARD), lambda b: (b // 2, b % 2, 0, 0)),
         ],
         out_specs=pl.BlockSpec((rows, BLK), lambda b: (0, b)),
         out_shape=jax.ShapeDtypeStruct((rows, inner), BF16),
@@ -58,6 +58,10 @@
     )(conv_input, prior, params)
 
 
+def times_rows(left, right):
+    return lax.dot_general(left, right, (((1,), (1,)), ((), ())), preferred_element_type=F32)
+
+
 def front_kernel(core_ref, xc_ref, own_ref, oth_ref, gain_ref, normed_ref, bc_ref, acc_ref):
     step = pl.program_id(0)
     core = core_ref[0]
@@ -70,9 +74,9 @@
     acc = acc_ref[...]
     for s in range(4):
         at = pl.multiple_of(s * SHARD + core * 128, 128)
-        acc = acc + jnp.dot(xc_ref[:, pl.ds(at, 128)], own_ref[s, 0], preferred_element_type=F32)
+        acc = acc + times_rows(xc_ref[:, pl.ds(at, 128)], own_ref[s, 0])
         at = pl.multiple_of(s * SHARD + (1 - core) * 128, 128)
-        acc = acc + jnp.dot(xc_ref[:, pl.ds(at, 128)], oth_ref[s, 0], preferred_element_type=F32)
+        acc = acc + times_rows(xc_ref[:, pl.ds(at, 128)], oth_ref[s, 0])
     acc_ref[...] = acc
 
     @pl.when(step == pl.num_programs(0) - 1)
@@ -88,7 +92,7 @@
 
 def front(core, xc, x_own, x_oth, gain):
     rows, inner = xc.shape
-    wspec = pl.BlockSpec((4, 1, 128, 288), lambda b: (b % 2, b // 2, 0, 0))
+    wspec = pl.BlockSpec((4, 1, 288, 128), lambda b: (b % 2, b // 2, 0, 0))
     return pl.pallas_call(
         front_kernel,
         grid=(inner // BLK,),
@@ -189,7 +193,7 @@
 def scan(where, normed, xc, d_own, d_oth, bc):
     rows, inner = xc.shape
     blocks = inner // BLK
-    wspec = pl.BlockSpec((1, 4, 152, 256), lambda b, where: ((b // 2 + 4 - where[1]) % 4, b % 2, 0, 0))
+    wspec = pl.BlockSpec((1, 4, 152, 256), lambda b, where: (b // 2, b % 2, 0, 0))
     grid_spec = pltpu.PrefetchScalarGridSpec(
         num_scalar_prefetch=1,
         grid=(blocks,),
@@ -305,28 +309,40 @@
     return lax.all_to_all(copies, axis, split_axis=0, concat_axis=0, tiled=True)
 
 
-def pack_x(core, x_weight, conv_weight, conv_bias):
-    half = lax.dynamic_slice_in_dim(x_weight, core * 128, 128, 0)
-    extra = jnp.concatenate([conv_weight, conv_bias[None, :], jnp.zeros((3, SHARD), BF16)], 0)
-    return jnp.concatenate([half, jnp.pad(extra, ((0, 0), (0, 32)))], 0)
-
-
-def pack_d(core, dt_weight, dt_bias, a_log, skip):
+def pack_x(core, x_weight):
+    return lax.dynamic_slice_in_dim(x_weight.T, core * 128, 128, 1)
+
+
+def pack_d(core, dt_weight, dt_bias, a_log, skip, conv_weight, conv_bias):
     half = lax.dynamic_slice_in_dim(dt_weight, core * 128, 128, 0)
     logs = lax.dynamic_slice_in_dim(a_log, core * 8, 8, 0)
     vec = jnp.where(core == 0, dt_bias, skip)[None, :]
     pieces = [half, *two_parts(logs), *two_parts(vec), jnp.zeros((6, SHARD), BF16)]
+    pieces += [conv_weight, conv_bias[None, :], jnp.zeros((3, SHARD), BF16)]
     return jnp.concatenate(pieces, 0)
 
 
-def around(block, axis):
-    up = [(i, (i + 1) % 4) for i in range(4)]
-    down = [(i, (i - 1) % 4) for i in range(4)]
-    previous = lax.ppermute(block, axis, up)
-    following = lax.ppermute(block, axis, down)
-    half = block.shape[0] // 2
-    opposite = [lax.ppermute(previous[:half], axis, up), lax.ppermute(following[half:], axis, down)]
-    return jnp.concatenate([block, following, *opposite, previous], 0).reshape(4, *block.shape)
+def shifted(block, axis, by):
+    count = lax.axis_size(axis)
+    return lax.ppermute(block, axis, [(i, (i + by) % count) for i in range(count)])
+
+
+def placed(blocks, at, axis):
+    count = lax.axis_size(axis)
+    here = lax.axis_index(axis)
+    first = blocks[0]
+    out = jnp.zeros((count, *first.shape), first.dtype)
+    for block, (by, row) in zip(blocks, at):
+        out = lax.dynamic_update_slice(out, block[None], ((here + by) % count, row) + (0,) * (first.ndim - 1))
+    return out
+
+
+def together(*values):
+    return lax.optimization_barrier(values)
+
+
+def straight(block, axis):
+    return [block] + [shifted(block, axis, k) for k in (1, 2, 3)], [(0, 0), (-1, 0), (-2, 0), (-3, 0)]
 
 
 def local(conv_input, gate_input, conv_weight, conv_bias, x_weight, dt_gain, dt_weight, dt_bias, a_log, skip):
@@ -334,16 +350,28 @@
     count = lax.axis_size(SEQ)
     swap = [(0, 1), (1, 0)]
     prior = lax.ppermute(conv_input[conv_input.shape[0] - 8 :], SEQ, [(i, i + 1) for i in range(count - 1)])
-    x_part = from_everyone(pack_x(core, x_weight, conv_weight, conv_bias), "y")
-    x_own = lax.all_gather(x_part[:, :128], "z", axis=0)
-    params = x_part[:, 128:136, :SHARD].reshape(32, SHARD)
-    d_part = from_everyone(jnp.concatenate([pack_d(core, dt_weight, dt_bias, a_log, skip), params], 0), "z")
-    d_part = d_part.reshape(8, 184, SHARD)
-    xc = conv(conv_input, prior, d_part[:, 152:].reshape(8, 4, 8, SHARD))
-    d_own = around(d_part[:, :152], "y")
+    x_pieces, x_at = straight(pack_x(core, x_weight), "y")
+    d_part = from_everyone(pack_d(core, dt_weight, dt_bias, a_log, skip, conv_weight, conv_bias), "z")
+    x0 = placed(x_pieces, x_at, "y")
+    x1 = shifted(x0, "z", 1), shifted(x0, "z", -1)
+    *x1, d_part, prior = together(*x1, d_part, prior)
+    d_part = d_part.reshape(8, 160, SHARD)
+    d0 = d_part[:, :152]
+    d1 = shifted(d0, "y", 1), shifted(d0, "y", -1)
+    params = placed(*straight(d_part[:, 152:], "y"), "y")
+    x2 = shifted(x1[0], "z", 1), shifted(x1[1], "z", -1)
+    *x2, params = together(*x2, params)
+    x3 = shifted(x2[0], "z", 1), shifted(x2[1], "z", -1)
+    xc = conv(conv_input, prior, params)
+    *x3, xc, up, down = together(*x3, xc, *d1)
+    d1 = up, down
+    x4 = shifted(x3[0][:2], "z", 1), shifted(x3[1][2:], "z", -1)
+    d2 = shifted(d1[0][:4], "y", 1), shifted(d1[1][4:], "y", -1)
+    x_own = placed([x0, *x1, *x2, *x3, *x4], [(0, 0), (-1, 0), (1, 0), (-2, 0), (2, 0), (-3, 0), (3, 0), (4, 0), (4, 2)], "z")
+    x_oth = lax.ppermute(x_own, "core", swap)
+    d_own = placed([d0, *d1, *d2], [(0, 0), (-1, 0), (1, 0), (2, 0), (2, 4)], "y")
     d_oth = lax.ppermute(d_own, "core", swap)
-    x_oth = lax.ppermute(x_own, "core", swap)
-    where = jnp.stack([core, lax.axis_index("y")]).astype(jnp.int32)
+    where = jnp.stack([core, core]).astype(jnp.int32)
     normed, bc = front(where, xc, x_own, x_oth, dt_gain[None, :])
     step, y, rate, ends = scan(where, normed, xc, d_own, d_oth, bc)
     ends = lax.all_to_all(ends, SEQ, split_axis=0, concat_axis=0, tiled=True)

time: 211 us -> 188 us (0.89)
  blocking collectives: 84.5 us -> 37.6 us
  starting transfers between devices: 9.49 us -> 41 us
  between operations: 13.6 us -> 0.42 us
  local copies, waits for them, and re-layouts: 14.5 us -> 22.8 us
  waiting for transfers between devices: 20.3 us -> 16.6 us
    all_to_all x2 -> x0, blocking collectives: 47.5 us -> none  [from_everyone(): return lax.all_to_all(copies, axis, split_axis=0, concat_axis=0, tiled=True)]
    ppermute x4 -> x18, starting transfers between devices: 6.68 us -> 28.7 us  [shifted(): lax.ppermute(block, axis, [(i, (i + by) % count) for i in range(count)])]
    dynamic_update_slice x0 -> x22, local copies, waits for them, and re-layouts: none -> 13.8 us  [placed(): lax.dynamic_update_slice(out, block[None], ((here + by) % count, row) + (...]
    ppermute x4 -> x18, waiting for transfers between devices: 16.3 us -> 4.47 us  [shifted(): lax.ppermute(block, axis, [(i, (i + by) % count) for i in range(count)])]
    all_to_all x0 -> x1, starting transfers between devices: none -> 8.57 us  [from_everyone(): return lax.all_to_all(copies, axis, split_axis=0, concat_axis=0, tiled=True)]
    ppermute x1, waiting for transfers between devices: 0.01 us -> 6.38 us  [local(): x_oth = lax.ppermute(x_own, 'core', swap)]
    ppermute x1 -> x0, local copies, waits for them, and re-layouts: 4.49 us -> none  [local(): x_oth = lax.ppermute(x_own, 'core', swap)]
    all_gather x1 -> x0, local copies, waits for them, and re-layouts: 4.48 us -> none  [local(): x_own = lax.all_gather(x_part[:, :128], 'z', axis=0)]
  transfers between devices with their start and end apart: 8 -> 22, of which waited for: 3 -> 5; matrix products, arithmetic and copies ran while one was open for 6% -> 10% of each run, Pallas kernels for 8% -> 9%
where the time goes in v3:
time: 188 us; the launch traced here: 187 us
  Pallas kernels  66.1 us (35%)
  starting transfers between devices  41 us (22%)
  blocking collectives  37.6 us (20%)
  local copies, waits for them, and re-layouts  22.8 us (12%)
  waiting for transfers between devices  16.6 us (9%)
  other arithmetic  2.09 us (1%)
    pallas_call x1, Pallas kernels, scan(): pl.pallas_call(scan_kernel, grid_spec=grid_spec, out_shape=[jax.ShapeDtyp...  29.2 us
    ppermute x18, starting transfers between devices, shifted(): lax.ppermute(block, axis, [(i, (i + by) % count) for i in range(count)])  28.7 us
    all_to_all x1, blocking collectives, local(): ends = lax.all_to_all(ends, SEQ, split_axis=0, concat_axis=0, tiled=True)  20.8 us
    pallas_call x1, Pallas kernels, close(): pl.pallas_call(close_kernel, grid=(inner // BLK,), in_specs=[pl.BlockSpec...  18.7 us
    all_to_all x1, blocking collectives, local(): lax.all_to_all(link(ends, a_log), SEQ, split_axis=0, concat_axis=0, tiled...  16.8 us
    dynamic_update_slice x22, local copies, waits for them, and re-layouts, placed(): lax.dynamic_update_slice(out, block[None], ((here + by) % count, row) + (...  13.8 us
    pallas_call x1, Pallas kernels, front(): pl.pallas_call(front_kernel, grid=(inner // BLK,), in_specs=[pl.BlockSpec...  8.86 us
    all_to_all x1, starting transfers between devices, from_everyone(): return lax.all_to_all(copies, axis, split_axis=0, concat_axis=0, tiled=True)  8.57 us
  transfers between devices with their start and end apart: 22, of which 5 were waited for; matrix products, arithmetic and copies ran while one was open for 10% of the time, Pallas kernels for 9%

profile of v3, /device:TPU:32, one launch (start us, length us, event | category | flops | bytes accessed | tf_op | source)
XLA Modules:
  0.0 186.7 jit_solution(16598472716671684585)
XLA Ops:
  3.8 8.6 %all-to-all-start = ((bf16[8,160,256]{2,1,0:T(8,128)(2,1)}), bf16[8,160,256]{2,1,0:T(8,128)(2,1)S(1)}, u32[]{:S(2)}, u32[]{:S(2)}) async-start(bf16[8,160,256]{2,1,0:T(8,128)(2,1)} %broadcast_in_dim.102), calls=%async_computation | async-start | bytes 1310720 | tf_op jit(solution)/shard_map/all_to_all | solution.py:309
  12.3 3.3 %collective-permute-start.1 = (bf16[288,128]{1,0:T(8,128)(2,1)S(1)}, bf16[288,128]{1,0:T(8,128)(2,1)S(1)}, u32[]{:S(2)}, u32[]{:S(2)}) collective-permute-start(bf16[288,128]{1,0:T(8,128)(2,1)S(1)} %dynamic-slice_bitcast_fusion), channel_id=1, source_target_pairs={{0,128},{64,192},{128,0},{192,64},{1,129},{65,193},{129,1},{193,65... | collective-permute-start | bytes 221192 | tf_op jit(solution)/shard_map/ppermute | solution.py:327
  16.3 2.6 %collective-permute-start.2 = (bf16[288,128]{1,0:T(8,128)(2,1)S(1)}, bf16[288,128]{1,0:T(8,128)(2,1)S(1)}, u32[]{:S(2)}, u32[]{:S(2)}) collective-permute-start(bf16[288,128]{1,0:T(8,128)(2,1)S(1)} %dynamic-slice_bitcast_fusion), channel_id=1, source_target_pairs={{0,192},{64,0},{128,64},{192,128},{1,193},{65,1},{129,65},{193,129... | collective-permute-start | bytes 221192 | tf_op jit(solution)/shard_map/ppermute | solution.py:327
  18.9 2.3 %collective-permute-done = bf16[288,128]{1,0:T(8,128)(2,1)S(1)} collective-permute-done((bf16[288,128]{1,0:T(8,128)(2,1)S(1)}, bf16[288,128]{1,0:T(8,128)(2,1)S(1)}, u32[]{:S(2)}, u32[]{:S(2)}) %collective-permute-start) | collective-permute-done | bytes 73760 | tf_op jit(solution)/shard_map/ppermute | solution.py:327
  21.4 2.0 %collective-permute-start.3 = (bf16[4,288,128]{2,1,0:T(8,128)(2,1)S(1)}, bf16[4,288,128]{2,1,0:T(8,128)(2,1)}, u32[]{:S(2)}, u32[]{:S(2)}) collective-permute-start(bf16[4,288,128]{2,1,0:T(8,128)(2,1)S(1)} %bitcast_dynamic-update-slice_fusion.15), channel_id=1, source_target_pairs={{0,8},{8,16},{16,24},{24,32},{32,40},{40,48},{48,56},{56,0},{1,9},... | collective-permute-start | bytes 884744 | tf_op jit(solution)/shard_map/ppermute | solution.py:327
  24.3 3.4 %collective-permute-start.5 = (bf16[8,8192]{1,0:T(8,128)(2,1)S(1)}, bf16[8,8192]{1,0:T(8,128)(2,1)S(1)}, u32[]{:S(2)}, u32[]{:S(2)}) collective-permute-start(bf16[8,8192]{1,0:T(8,128)(2,1)S(1)} %slice.21), channel_id=1, source_target_pairs={{0,8},{8,16},{16,24},{24,32},{32,40},{40,48},{48,56},{56,64},{64,7... | collective-permute-start | bytes 393224 | tf_op jit(solution)/shard_map/ppermute | solution.py:352
  27.8 1.8 broadcast_in_dim.108
  30.4 5.8 %collective-permute-done.5.prior_ref = bf16[8,8192]{1,0:T(8,128)(2,1)S(1)} collective-permute-done((bf16[8,8192]{1,0:T(8,128)(2,1)S(1)}, bf16[8,8192]{1,0:T(8,128)(2,1)S(1)}, u32[]{:S(2)}, u32[]{:S(2)}) %collective-permute-start.5) | collective-permute-done | bytes 131104 | tf_op jit(solution)/shard_map/ppermute | solution.py:352
  36.2 3.3 %collective-permute-start.9 = (bf16[8,8,256]{2,1,0:T(8,128)(2,1)S(1)}, bf16[8,8,256]{2,1,0:T(8,128)(2,1)S(1)}, u32[]{:S(2)}, u32[]{:S(2)}) collective-permute-start(bf16[8,8,256]{2,1,0:T(8,128)(2,1)S(1)} %slice.22), channel_id=1, source_target_pairs={{0,128},{64,192},{128,0},{192,64},{1,129},{65,193},{129,1},{193,65... | collective-permute-start | bytes 98312 | tf_op jit(solution)/shard_map/ppermute | solution.py:327
  40.2 2.6 %collective-permute-start.10 = (bf16[8,8,256]{2,1,0:T(8,128)(2,1)S(1)}, bf16[8,8,256]{2,1,0:T(8,128)(2,1)S(1)}, u32[]{:S(2)}, u32[]{:S(2)}) collective-permute-start(bf16[8,8,256]{2,1,0:T(8,128)(2,1)S(1)} %slice.22), channel_id=1, source_target_pairs={{0,192},{64,0},{128,64},{192,128},{1,193},{65,1},{129,65},{193,129... | collective-permute-start | bytes 98312 | tf_op jit(solution)/shard_map/ppermute | solution.py:327
  45.7 1.7 bitcast_dynamic-update-slice_fusion.10
  50.1 2.1 %collective-permute-start.13 = (bf16[8,152,256]{2,1,0:T(8,128)(2,1)}, bf16[8,152,256]{2,1,0:T(8,128)(2,1)}, u32[]{:S(2)}, u32[]{:S(2)}) collective-permute-start(bf16[8,152,256]{2,1,0:T(8,128)(2,1)} %slice.23), channel_id=1, source_target_pairs={{0,64},{64,128},{128,192},{192,0},{1,65},{65,129},{129,193},{193,1... | collective-permute-start | bytes 1867784 | tf_op jit(solution)/shard_map/ppermute | solution.py:327
  52.3 1.9 %collective-permute-start.11 = (bf16[4,288,128]{2,1,0:T(8,128)(2,1)}, bf16[4,288,128]{2,1,0:T(8,128)(2,1)}, u32[]{:S(2)}, u32[]{:S(2)}) collective-permute-start(bf16[4,288,128]{2,1,0:T(8,128)(2,1)} %collective-permute-done.6), channel_id=1, source_target_pairs={{0,8},{8,16},{16,24},{24,32},{32,40},{40,48},{48,56},{56,0},{1,9},... | collective-permute-start | bytes 884744 | tf_op jit(solution)/shard_map/ppermute | solution.py:327
  55.8 1.7 bitcast_dynamic-update-slice_fusion.8
  57.5 7.6 %conv.1.xc_ref = bf16[128,8192]{1,0:T(8,128)(2,1)} custom-call(bf16[128,8192]{1,0:T(8,128)(2,1)} %ci_ref.1, bf16[8,8192]{1,0:T(8,128)(2,1)} %copy-done.4, bf16[4,8,8,256]{3,2,1,0:T(8,128)(2,1)} %copy-done.2), custom_call_target="tpu_custom_call" | custom-call | tf_op jit(solution)/shard_map/conv/pallas_call | solution.py:45
  68.7 3.0 %collective-permute-start.16 = (bf16[2,288,128]{2,1,0:T(8,128)(2,1)S(1)}, bf16[2,288,128]{2,1,0:T(8,128)(2,1)S(1)}, u32[]{:S(2)}, u32[]{:S(2)}) collective-permute-start(bf16[2,288,128]{2,1,0:T(8,128)(2,1)S(1)} %slice.25), channel_id=1, source_target_pairs={{0,56},{8,0},{16,8},{24,16},{32,24},{40,32},{48,40},{56,48},{1,57}... | collective-permute-start | bytes 442376 | tf_op jit(solution)/shard_map/ppermute | solution.py:327
  80.1 2.1 %collective-permute-done.18 = bf16[4,152,256]{2,1,0:T(8,128)(2,1)S(1)} collective-permute-done((bf16[4,152,256]{2,1,0:T(8,128)(2,1)S(1)}, bf16[4,152,256]{2,1,0:T(8,128)(2,1)S(1)}, u32[]{:S(2)}, u32[]{:S(2)}) %collective-permute-start.18) | collective-permute-done | bytes 311328 | tf_op jit(solution)/shard_map/ppermute | solution.py:327
  84.2 6.4 %collective-permute-done.17.oth_ref = bf16[8,4,288,128]{3,2,1,0:T(8,128)(2,1)} collective-permute-done((bf16[8,4,288,128]{3,2,1,0:T(8,128)(2,1)}, bf16[8,4,288,128]{3,2,1,0:T(8,128)(2,1)}, u32[]{:S(2)}, u32[]{:S(2)}) %collective-permute-start.17) | collective-permute-done | bytes 2359328 | tf_op jit(solution)/shard_map/ppermute | solution.py:371
  90.5 8.9 %front.1 = (bf16[128,256]{1,0:T(8,128)(2,1)}, f32[4096,128]{1,0:T(8,128)}) custom-call(s32[2]{0:T(128)} %pad_add_fusion.core_ref.where_ref, bf16[128,8192]{1,0:T(8,128)(2,1)} %conv.1.xc_ref, bf16[8,4,288,128]{3,2,1,0:T(8,128)(2,1)} %bitcast_dynamic-update-slice_fusion.12.own_ref, bf16[8,4,288,128]{3,2,1,0:T(8,128)(2,1)} %collective-permute-done.17.oth_ref, ...), custom_call_target="tpu_custom_call" | custom-call | tf_op jit(solution)/shard_map/front/pallas_call | solution.py:96
  99.4 29.2 %scan.1 = (f32[8,1024,128]{2,1,0:T(8,128)}, f32[8,1024,128]{2,1,0:T(8,128)}, f32[8,128,128]{2,1,0:T(8,128)}, bf16[32,40,128]{2,1,0:T(8,128)(2,1)}) custom-call(s32[2]{0:T(128)} %pad_add_fusion.core_ref.where_ref, bf16[128,256]{1,0:T(8,128)(2,1)} %get-tuple-element.33.normed_ref, bf16[128,8192]{1,0:T(8,128)(2,1)} %conv.1.xc_ref, ...), custom_call_target="tpu_custom_call" | custom-call | tf_op jit(solution)/shard_map/scan/pallas_call | solution.py:219
  128.6 20.8 %all_to_all.15.ends_ref = bf16[32,40,128]{2,1,0:T(8,128)(2,1)} all-to-all(bf16[32,40,128]{2,1,0:T(8,128)(2,1)} %get-tuple-element.40), channel_id=1, replica_groups=mesh['y'=4,'z'=8,'x'=4,'core'=2] {'y','z'}, dimensions={0} | all-to-all | bytes 655360 | tf_op jit(solution)/shard_map/all_to_all | solution.py:377
  149.4 1.8 link.1
  151.2 16.8 %all_to_all.16.start_ref = bf16[32,32,128]{2,1,0:T(8,128)(2,1)} all-to-all(bf16[32,32,128]{2,1,0:T(8,128)(2,1)} %link.1), channel_id=1, replica_groups=mesh['y'=4,'z'=8,'x'=4,'core'=2] {'y','z'}, dimensions={0} | all-to-all | bytes 524288 | tf_op jit(solution)/shard_map/all_to_all | solution.py:378
  168.0 18.7 %close.1 = bf16[128,8192]{1,0:T(8,128)(2,1)} custom-call(f32[8,1024,128]{2,1,0:T(8,128)} %get-tuple-element.37.step_ref, f32[8,1024,128]{2,1,0:T(8,128)} %get-tuple-element.38.y_ref, f32[8,128,128]{2,1,0:T(8,128)} %get-tuple-element.39.rate_ref, bf16[32,32,128]{2,1,0:T(8,128)(2,1)} %all_to_all.16.start_ref, f32[4096,128]{1,0:T(8,128)} %get-tuple-element.36.bc_ref.c_ref, ...), custom_call_target="tpu_custom_call" | custom-call | tf_op jit(solution)/shard_map/close/pallas_call | solution.py:288
  (82 shorter events, 28.2 us)
Async XLA Ops:
  3.8 32.4 %all-to-all-start = ((bf16[8,160,256]{2,1,0:T(8,128)(2,1)}), bf16[8,160,256]{2,1,0:T(8,128)(2,1)S(1)}, u32[]{:S(2)}, u32[]{:S(2)}) async-start(bf16[8,160,256]{2,1,0:T(8,128)(2,1)} %broadcast_in_dim.102), calls=%async_computation | async-start | bytes 1310720 | tf_op jit(solution)/shard_map/all_to_all | solution.py:309
  12.3 8.9 %collective-permute-start.1 = (bf16[288,128]{1,0:T(8,128)(2,1)S(1)}, bf16[288,128]{1,0:T(8,128)(2,1)S(1)}, u32[]{:S(2)}, u32[]{:S(2)}) collective-permute-start(bf16[288,128]{1,0:T(8,128)(2,1)S(1)} %dynamic-slice_bitcast_fusion), channel_id=1, source_target_pairs={{0,128},{64,192},{128,0},{192,64},{1,129},{65,193},{129,1},{193,65... | collective-permute-start | bytes 221192 | tf_op jit(solution)/shard_map/ppermute | solution.py:327
  15.6 5.6 %collective-permute-start = (bf16[288,128]{1,0:T(8,128)(2,1)S(1)}, bf16[288,128]{1,0:T(8,128)(2,1)S(1)}, u32[]{:S(2)}, u32[]{:S(2)}) collective-permute-start(bf16[288,128]{1,0:T(8,128)(2,1)S(1)} %dynamic-slice_bitcast_fusion), channel_id=1, source_target_pairs={{0,64},{64,128},{128,192},{192,0},{1,65},{65,129},{129,193},{193,1... | collective-permute-start | bytes 221192 | tf_op jit(solution)/shard_map/ppermute | solution.py:327
  16.3 4.9 %collective-permute-start.2 = (bf16[288,128]{1,0:T(8,128)(2,1)S(1)}, bf16[288,128]{1,0:T(8,128)(2,1)S(1)}, u32[]{:S(2)}, u32[]{:S(2)}) collective-permute-start(bf16[288,128]{1,0:T(8,128)(2,1)S(1)} %dynamic-slice_bitcast_fusion), channel_id=1, source_target_pairs={{0,192},{64,0},{128,64},{192,128},{1,193},{65,1},{129,65},{193,129... | collective-permute-start | bytes 221192 | tf_op jit(solution)/shard_map/ppermute | solution.py:327
  21.3 14.9 %collective-permute-start.4 = (bf16[4,288,128]{2,1,0:T(8,128)(2,1)S(1)}, bf16[4,288,128]{2,1,0:T(8,128)(2,1)}, u32[]{:S(2)}, u32[]{:S(2)}) collective-permute-start(bf16[4,288,128]{2,1,0:T(8,128)(2,1)S(1)} %bitcast_dynamic-update-slice_fusion.15), channel_id=1, source_target_pairs={{0,56},{8,0},{16,8},{24,16},{32,24},{40,32},{48,40},{56,48},{1,57}... | collective-permute-start | bytes 884744 | tf_op jit(solution)/shard_map/ppermute | solution.py:327
  21.4 14.8 %collective-permute-start.3 = (bf16[4,288,128]{2,1,0:T(8,128)(2,1)S(1)}, bf16[4,288,128]{2,1,0:T(8,128)(2,1)}, u32[]{:S(2)}, u32[]{:S(2)}) collective-permute-start(bf16[4,288,128]{2,1,0:T(8,128)(2,1)S(1)} %bitcast_dynamic-update-slice_fusion.15), channel_id=1, source_target_pairs={{0,8},{8,16},{16,24},{24,32},{32,40},{40,48},{48,56},{56,0},{1,9},... | collective-permute-start | bytes 884744 | tf_op jit(solution)/shard_map/ppermute | solution.py:327
  24.3 11.9 %collective-permute-start.5 = (bf16[8,8192]{1,0:T(8,128)(2,1)S(1)}, bf16[8,8192]{1,0:T(8,128)(2,1)S(1)}, u32[]{:S(2)}, u32[]{:S(2)}) collective-permute-start(bf16[8,8192]{1,0:T(8,128)(2,1)S(1)} %slice.21), channel_id=1, source_target_pairs={{0,8},{8,16},{16,24},{24,32},{32,40},{40,48},{48,56},{56,64},{64,7... | collective-permute-start | bytes 393224 | tf_op jit(solution)/shard_map/ppermute | solution.py:352
  36.2 13.0 %copy-start.4 = (bf16[8,8192]{1,0:T(8,128)(2,1)}, bf16[8,8192]{1,0:T(8,128)(2,1)S(1)}, u32[]{:S(2)}) copy-start(bf16[8,8192]{1,0:T(8,128)(2,1)S(1)} %collective-permute-done.5.prior_ref) | copy-start | bytes 393220
  36.2 13.9 %collective-permute-start.9 = (bf16[8,8,256]{2,1,0:T(8,128)(2,1)S(1)}, bf16[8,8,256]{2,1,0:T(8,128)(2,1)S(1)}, u32[]{:S(2)}, u32[]{:S(2)}) collective-permute-start(bf16[8,8,256]{2,1,0:T(8,128)(2,1)S(1)} %slice.22), channel_id=1, source_target_pairs={{0,128},{64,192},{128,0},{192,64},{1,129},{65,193},{129,1},{193,65... | collective-permute-start | bytes 98312 | tf_op jit(solution)/shard_map/ppermute | solution.py:327
  39.5 10.6 %collective-permute-start.8 = (bf16[8,8,256]{2,1,0:T(8,128)(2,1)S(1)}, bf16[8,8,256]{2,1,0:T(8,128)(2,1)S(1)}, u32[]{:S(2)}, u32[]{:S(2)}) collective-permute-start(bf16[8,8,256]{2,1,0:T(8,128)(2,1)S(1)} %slice.22), channel_id=1, source_target_pairs={{0,64},{64,128},{128,192},{192,0},{1,65},{65,129},{129,193},{193,1... | collective-permute-start | bytes 98312 | tf_op jit(solution)/shard_map/ppermute | solution.py:327
  40.2 12.0 %collective-permute-start.10 = (bf16[8,8,256]{2,1,0:T(8,128)(2,1)S(1)}, bf16[8,8,256]{2,1,0:T(8,128)(2,1)S(1)}, u32[]{:S(2)}, u32[]{:S(2)}) collective-permute-start(bf16[8,8,256]{2,1,0:T(8,128)(2,1)S(1)} %slice.22), channel_id=1, source_target_pairs={{0,192},{64,0},{128,64},{192,128},{1,193},{65,1},{129,65},{193,129... | collective-permute-start | bytes 98312 | tf_op jit(solution)/shard_map/ppermute | solution.py:327
  42.7 9.5 %collective-permute-start.6 = (bf16[4,288,128]{2,1,0:T(8,128)(2,1)}, bf16[4,288,128]{2,1,0:T(8,128)(2,1)}, u32[]{:S(2)}, u32[]{:S(2)}) collective-permute-start(bf16[4,288,128]{2,1,0:T(8,128)(2,1)} %collective-permute-done.3), channel_id=1, source_target_pairs={{0,8},{8,16},{16,24},{24,32},{32,40},{40,48},{48,56},{56,0},{1,9},... | collective-permute-start | bytes 884744 | tf_op jit(solution)/shard_map/ppermute | solution.py:327
  44.2 8.1 %collective-permute-start.7 = (bf16[4,288,128]{2,1,0:T(8,128)(2,1)}, bf16[4,288,128]{2,1,0:T(8,128)(2,1)}, u32[]{:S(2)}, u32[]{:S(2)}) collective-permute-start(bf16[4,288,128]{2,1,0:T(8,128)(2,1)} %collective-permute-done.4), channel_id=1, source_target_pairs={{0,56},{8,0},{16,8},{24,16},{32,24},{40,32},{48,40},{56,48},{1,57}... | collective-permute-start | bytes 884744 | tf_op jit(solution)/shard_map/ppermute | solution.py:327
  50.1 16.8 %collective-permute-start.14 = (bf16[8,152,256]{2,1,0:T(8,128)(2,1)}, bf16[8,152,256]{2,1,0:T(8,128)(2,1)S(1)}, u32[]{:S(2)}, u32[]{:S(2)}) collective-permute-start(bf16[8,152,256]{2,1,0:T(8,128)(2,1)} %slice.23), channel_id=1, source_target_pairs={{0,192},{64,0},{128,64},{192,128},{1,193},{65,1},{129,65},{193,129... | collective-permute-start | bytes 1867784 | tf_op jit(solution)/shard_map/ppermute | solution.py:327
  50.1 16.7 %collective-permute-start.13 = (bf16[8,152,256]{2,1,0:T(8,128)(2,1)}, bf16[8,152,256]{2,1,0:T(8,128)(2,1)}, u32[]{:S(2)}, u32[]{:S(2)}) collective-permute-start(bf16[8,152,256]{2,1,0:T(8,128)(2,1)} %slice.23), channel_id=1, source_target_pairs={{0,64},{64,128},{128,192},{192,0},{1,65},{65,129},{129,193},{193,1... | collective-permute-start | bytes 1867784 | tf_op jit(solution)/shard_map/ppermute | solution.py:327
  52.3 14.5 %collective-permute-start.11 = (bf16[4,288,128]{2,1,0:T(8,128)(2,1)}, bf16[4,288,128]{2,1,0:T(8,128)(2,1)}, u32[]{:S(2)}, u32[]{:S(2)}) collective-permute-start(bf16[4,288,128]{2,1,0:T(8,128)(2,1)} %collective-permute-done.6), channel_id=1, source_target_pairs={{0,8},{8,16},{16,24},{24,32},{32,40},{40,48},{48,56},{56,0},{1,9},... | collective-permute-start | bytes 884744 | tf_op jit(solution)/shard_map/ppermute | solution.py:327
  54.2 12.6 %collective-permute-start.12 = (bf16[4,288,128]{2,1,0:T(8,128)(2,1)}, bf16[4,288,128]{2,1,0:T(8,128)(2,1)}, u32[]{:S(2)}, u32[]{:S(2)}) collective-permute-start(bf16[4,288,128]{2,1,0:T(8,128)(2,1)} %collective-permute-done.7), channel_id=1, source_target_pairs={{0,56},{8,0},{16,8},{24,16},{32,24},{40,32},{48,40},{56,48},{1,57}... | collective-permute-start | bytes 884744 | tf_op jit(solution)/shard_map/ppermute | solution.py:327
  68.7 13.7 %collective-permute-start.16 = (bf16[2,288,128]{2,1,0:T(8,128)(2,1)S(1)}, bf16[2,288,128]{2,1,0:T(8,128)(2,1)S(1)}, u32[]{:S(2)}, u32[]{:S(2)}) collective-permute-start(bf16[2,288,128]{2,1,0:T(8,128)(2,1)S(1)} %slice.25), channel_id=1, source_target_pairs={{0,56},{8,0},{16,8},{24,16},{32,24},{40,32},{48,40},{56,48},{1,57}... | collective-permute-start | bytes 442376 | tf_op jit(solution)/shard_map/ppermute | solution.py:327
  71.7 7.7 %collective-permute-start.15 = (bf16[2,288,128]{2,1,0:T(8,128)(2,1)S(1)}, bf16[2,288,128]{2,1,0:T(8,128)(2,1)S(1)}, u32[]{:S(2)}, u32[]{:S(2)}) collective-permute-start(bf16[2,288,128]{2,1,0:T(8,128)(2,1)S(1)} %slice.24), channel_id=1, source_target_pairs={{0,8},{8,16},{16,24},{24,32},{32,40},{40,48},{48,56},{56,0},{1,9},... | collective-permute-start | bytes 442376 | tf_op jit(solution)/shard_map/ppermute | solution.py:327
  72.7 9.4 %collective-permute-start.19 = (bf16[4,152,256]{2,1,0:T(8,128)(2,1)S(1)}, bf16[4,152,256]{2,1,0:T(8,128)(2,1)S(1)}, u32[]{:S(2)}, u32[]{:S(2)}) collective-permute-start(bf16[4,152,256]{2,1,0:T(8,128)(2,1)S(1)} %slice.27), channel_id=1, source_target_pairs={{0,192},{64,0},{128,64},{192,128},{1,193},{65,1},{129,65},{193,129... | collective-permute-start | bytes 933896 | tf_op jit(solution)/shard_map/ppermute | solution.py:327
  74.0 8.1 %collective-permute-start.18 = (bf16[4,152,256]{2,1,0:T(8,128)(2,1)S(1)}, bf16[4,152,256]{2,1,0:T(8,128)(2,1)S(1)}, u32[]{:S(2)}, u32[]{:S(2)}) collective-permute-start(bf16[4,152,256]{2,1,0:T(8,128)(2,1)S(1)} %slice.26), channel_id=1, source_target_pairs={{0,64},{64,128},{128,192},{192,0},{1,65},{65,129},{129,193},{193,1... | collective-permute-start | bytes 933896 | tf_op jit(solution)/shard_map/ppermute | solution.py:327
  82.2 17.2 %copy-start.1 = (bf16[4,8,152,256]{3,2,1,0:T(8,128)(2,1)}, bf16[4,8,152,256]{3,2,1,0:T(8,128)(2,1)S(1)}, u32[]{:S(2)}) copy-start(bf16[4,8,152,256]{3,2,1,0:T(8,128)(2,1)S(1)} %bitcast_dynamic-update-slice_fusion.3.own_ref) | copy-start | bytes 7471108
  82.2 17.2 %collective-permute-start.20 = (bf16[4,8,152,256]{3,2,1,0:T(8,128)(2,1)S(1)}, bf16[4,8,152,256]{3,2,1,0:T(8,128)(2,1)}, u32[]{:S(2)}, u32[]{:S(2)}) collective-permute-start(bf16[4,8,152,256]{3,2,1,0:T(8,128)(2,1)S(1)} %bitcast_dynamic-update-slice_fusion.3.own_ref), channel_id=1, source_target_pairs={{0,1},{1,0},{2,3},{3,2},{4,5},{5,4},{6,7},{7,6},{8,9},{9,8},{10,11... | collective-permute-start | bytes 7471112 | tf_op jit(solution)/shard_map/ppermute | solution.py:373
  83.2 7.3 %collective-permute-start.17 = (bf16[8,4,288,128]{3,2,1,0:T(8,128)(2,1)}, bf16[8,4,288,128]{3,2,1,0:T(8,128)(2,1)}, u32[]{:S(2)}, u32[]{:S(2)}) collective-permute-start(bf16[8,4,288,128]{3,2,1,0:T(8,128)(2,1)} %bitcast_dynamic-update-slice_fusion.12.own_ref), channel_id=1, source_target_pairs={{0,1},{1,0},{2,3},{3,2},{4,5},{5,4},{6,7},{7,6},{8,9},{9,8},{10,11... | collective-permute-start | bytes 7077896 | tf_op jit(solution)/shard_map/ppermute | solution.py:371
  (3 other events, 19.8 us)

commit v4 on v3

--- a/solution.py
+++ b/solution.py
@@ -32,7 +32,7 @@
     pad_ref[0:8, :] = prior_ref[...].astype(F32)
     pad_ref[8 : 8 + rows, :] = ci_ref[...].astype(F32)
     for s in range(4):
-        par = par_ref[0, s].astype(F32)
+        par = jnp.concatenate([par_ref[s, 0:8, :], par_ref[s, 8:16, :]], 1).astype(F32)
         lanes = slice(s * SHARD, (s + 1) * SHARD)
         total = jnp.broadcast_to(par[taps : taps + 1, :], (rows, SHARD))
         for k in range(taps):
@@ -48,7 +48,7 @@
         in_specs=[
             pl.BlockSpec((rows, BLK), lambda b: (0, b)),
             pl.BlockSpec((8, BLK), lambda b: (0, b)),
-            pl.BlockSpec((1, 4, 8, SHARD), lambda b: (b // 2, b % 2, 0, 0)),
+            pl.BlockSpec((4, 16, 128), lambda b: (b, 0, 0)),
         ],
         out_specs=pl.BlockSpec((rows, BLK), lambda b: (0, b)),
         out_shape=jax.ShapeDtypeStruct((rows, inner), BF16),
@@ -63,56 +63,44 @@
 
 
 def front_kernel(core_ref, xc_ref, own_ref, oth_ref, gain_ref, normed_ref, bc_ref, acc_ref):
-    step = pl.program_id(0)
     core = core_ref[0]
     rows = xc_ref.shape[0]
-
-    @pl.when(step == 0)
-    def _():
-        acc_ref[...] = jnp.zeros_like(acc_ref)
-
-    acc = acc_ref[...]
-    for s in range(4):
-        at = pl.multiple_of(s * SHARD + core * 128, 128)
-        acc = acc + times_rows(xc_ref[:, pl.ds(at, 128)], own_ref[s, 0])
-        at = pl.multiple_of(s * SHARD + (1 - core) * 128, 128)
-        acc = acc + times_rows(xc_ref[:, pl.ds(at, 128)], oth_ref[s, 0])
-    acc_ref[...] = acc
-
-    @pl.when(step == pl.num_programs(0) - 1)
-    def _():
-        rank = gain_ref.shape[1]
-        low = acc_ref[:, 0:rank]
-        scale = lax.rsqrt(jnp.mean(low * low, axis=1, keepdims=True) + 1e-06)
-        normed_ref[...] = (low * scale * gain_ref[...]).astype(BF16)
-        for m in range(32):
-            col = acc_ref[:, rank + m : rank + m + 1]
-            bc_ref[m * rows : (m + 1) * rows, :] = jnp.broadcast_to(col, (rows, 128))
+    rank = gain_ref.shape[1]
+    acc_ref[...] = jnp.zeros_like(acc_ref)
+
+    def add_shards(group, _):
+        acc = acc_ref[...]
+        for k in range(4):
+            s = group * 4 + k
+            mine = pl.multiple_of(s * SHARD + core * 128, 128)
+            other = pl.multiple_of(s * SHARD + (1 - core) * 128, 128)
+            left = jnp.concatenate([xc_ref[:, pl.ds(mine, 128)], xc_ref[:, pl.ds(other, 128)]], 1)
+            right = [jnp.concatenate([ref[q, s] for q in range(4)], 0) for ref in (own_ref, oth_ref)]
+            acc = acc + times_rows(left, jnp.concatenate(right, 1))
+        acc_ref[...] = acc
+        return 0
+
+    lax.fori_loop(0, own_ref.shape[1] // 4, add_shards, 0)
+    low = acc_ref[:, 0:rank]
+    scale = lax.rsqrt(jnp.mean(low * low, axis=1, keepdims=True) + 1e-06)
+    normed_ref[...] = (low * scale * gain_ref[...]).astype(BF16)
+    for m in range(32):
+        col = acc_ref[:, rank + m : rank + m + 1]
+        bc_ref[m * rows : (m + 1) * rows, :] = jnp.broadcast_to(col, (rows, 128))
 
 
 def front(core, xc, x_own, x_oth, gain):
-    rows, inner = xc.shape
-    wspec = pl.BlockSpec((4, 1, 288, 128), lambda b: (b % 2, b // 2, 0, 0))
+    rows = xc.shape[0]
+    vmem = pl.BlockSpec(memory_space=pltpu.VMEM)
     return pl.pallas_call(
         front_kernel,
-        grid=(inner // BLK,),
-        in_specs=[
-            pl.BlockSpec(memory_space=pltpu.SMEM),
-            pl.BlockSpec((rows, BLK), lambda b: (0, b)),
-            wspec,
-            wspec,
-            pl.BlockSpec((1, 256), lambda b: (0, 0)),
-        ],
-        out_specs=[
-            pl.BlockSpec((rows, 256), lambda b: (0, 0)),
-            pl.BlockSpec((32 * rows, 128), lambda b: (0, 0)),
-        ],
+        in_specs=[pl.BlockSpec(memory_space=pltpu.SMEM), vmem, vmem, vmem, vmem],
+        out_specs=[vmem, vmem],
         out_shape=[
             jax.ShapeDtypeStruct((rows, 256), BF16),
             jax.ShapeDtypeStruct((32 * rows, 128), F32),
         ],
-        scratch_shapes=[pltpu.VMEM((rows, 288), F32)],
-        compiler_params=pltpu.CompilerParams(dimension_semantics=("arbitrary",)),
+        scratch_shapes=[pltpu.VMEM((rows, 320), F32)],
         name="front",
     )(core, xc, x_own, x_oth, gain)
 
@@ -309,16 +297,18 @@
     return lax.all_to_all(copies, axis, split_axis=0, concat_axis=0, tiled=True)
 
 
-def pack_x(core, x_weight):
-    return lax.dynamic_slice_in_dim(x_weight.T, core * 128, 128, 1)
-
-
-def pack_d(core, dt_weight, dt_bias, a_log, skip, conv_weight, conv_bias):
+def pack_x(core, quarter, x_weight, conv_weight, conv_bias):
+    half = lax.dynamic_slice_in_dim(x_weight.T, core * 128, 128, 1)
+    part = lax.dynamic_slice_in_dim(jnp.pad(half, ((0, 32), (0, 0))), quarter * 80, 80, 0)
+    taps = jnp.concatenate([conv_weight, conv_bias[None, :], jnp.zeros((3, SHARD), BF16)], 0)
+    return jnp.concatenate([part, taps[:, :128], taps[:, 128:]], 0)
+
+
+def pack_d(core, dt_weight, dt_bias, a_log, skip):
     half = lax.dynamic_slice_in_dim(dt_weight, core * 128, 128, 0)
     logs = lax.dynamic_slice_in_dim(a_log, core * 8, 8, 0)
     vec = jnp.where(core == 0, dt_bias, skip)[None, :]
     pieces = [half, *two_parts(logs), *two_parts(vec), jnp.zeros((6, SHARD), BF16)]
-    pieces += [conv_weight, conv_bias[None, :], jnp.zeros((3, SHARD), BF16)]
     return jnp.concatenate(pieces, 0)
 
 
@@ -341,8 +331,22 @@
     return lax.optimization_barrier(values)
 
 
-def straight(block, axis):
-    return [block] + [shifted(block, axis, k) for k in (1, 2, 3)], [(0, 0), (-1, 0), (-2, 0), (-3, 0)]
+def around_eight(block, axis):
+    near = {k: shifted(block, axis, -k) for k in (1, -1, 2, -2)}
+    near = dict(zip(near, together(*near.values())))
+    far = {3: shifted(near[2], axis, -1), -3: shifted(near[-2], axis, 1), 4: shifted(near[-2], axis, 2)}
+    blocks = {0: block, **near, **far}
+    return placed(list(blocks.values()), [(k, 0) for k in blocks], axis)
+
+
+def halves_on(up, down, axis):
+    half = up.shape[0] // 2
+    return shifted(up[:half], axis, 1), shifted(down[half:], axis, -1)
+
+
+def around_four(block, first, second, axis):
+    half = block.shape[0] // 2
+    return placed([block, *first, *second], [(0, 0), (-1, 0), (1, 0), (2, 0), (2, half)], axis)
 
 
 def local(conv_input, gate_input, conv_weight, conv_bias, x_weight, dt_gain, dt_weight, dt_bias, a_log, skip):
@@ -350,28 +354,22 @@
     count = lax.axis_size(SEQ)
     swap = [(0, 1), (1, 0)]
     prior = lax.ppermute(conv_input[conv_input.shape[0] - 8 :], SEQ, [(i, i + 1) for i in range(count - 1)])
-    x_pieces, x_at = straight(pack_x(core, x_weight), "y")
-    d_part = from_everyone(pack_d(core, dt_weight, dt_bias, a_log, skip, conv_weight, conv_bias), "z")
-    x0 = placed(x_pieces, x_at, "y")
-    x1 = shifted(x0, "z", 1), shifted(x0, "z", -1)
-    *x1, d_part, prior = together(*x1, d_part, prior)
-    d_part = d_part.reshape(8, 160, SHARD)
-    d0 = d_part[:, :152]
+    x_part = from_everyone(pack_x(core, lax.axis_index("x"), x_weight, conv_weight, conv_bias)[None], SEQ)
+    d0 = around_eight(pack_d(core, dt_weight, dt_bias, a_log, skip), "z")
+    x_part, d0, prior = together(x_part, d0, prior)
+    x_part = x_part.reshape(count, 96, 128)
+    x0 = x_part[:, :80]
+    x1 = shifted(x0, "x", 1), shifted(x0, "x", -1)
     d1 = shifted(d0, "y", 1), shifted(d0, "y", -1)
-    params = placed(*straight(d_part[:, 152:], "y"), "y")
-    x2 = shifted(x1[0], "z", 1), shifted(x1[1], "z", -1)
-    *x2, params = together(*x2, params)
-    x3 = shifted(x2[0], "z", 1), shifted(x2[1], "z", -1)
-    xc = conv(conv_input, prior, params)
-    *x3, xc, up, down = together(*x3, xc, *d1)
-    d1 = up, down
-    x4 = shifted(x3[0][:2], "z", 1), shifted(x3[1][2:], "z", -1)
-    d2 = shifted(d1[0][:4], "y", 1), shifted(d1[1][4:], "y", -1)
-    x_own = placed([x0, *x1, *x2, *x3, *x4], [(0, 0), (-1, 0), (1, 0), (-2, 0), (2, 0), (-3, 0), (3, 0), (4, 0), (4, 2)], "z")
+    xc = conv(conv_input, prior, x_part[:, 80:])
+    *x1, xc = together(*x1, xc)
+    x2 = halves_on(*x1, "x")
+    d2 = halves_on(*d1, "y")
+    x_own = around_four(x0, x1, x2, "x")
     x_oth = lax.ppermute(x_own, "core", swap)
-    d_own = placed([d0, *d1, *d2], [(0, 0), (-1, 0), (1, 0), (2, 0), (2, 4)], "y")
+    d_own = around_four(d0, d1, d2, "y")
     d_oth = lax.ppermute(d_own, "core", swap)
-    where = jnp.stack([core, core]).astype(jnp.int32)
+    where = core.reshape(1).astype(jnp.int32)
     normed, bc = front(where, xc, x_own, x_oth, dt_gain[None, :])
     step, y, rate, ends = scan(where, normed, xc, d_own, d_oth, bc)
     ends = lax.all_to_all(ends, SEQ, split_axis=0, concat_axis=0, tiled=True)

time: 188 us -> 197 us (1.048)
  local copies, waits for them, and re-layouts: 22.8 us -> 28.8 us
  waiting for transfers between devices: 16.6 us -> 21.3 us
  blocking collectives: 37.6 us -> 40.4 us
  starting transfers between devices: 41 us -> 38.6 us
    ppermute x18 -> x15, waiting for transfers between devices: 4.47 us -> 16.9 us  [shifted(): lax.ppermute(block, axis, [(i, (i + by) % count) for i in range(count)])]
    ppermute x1, waiting for transfers between devices: 5.76 us -> 0.01 us  [local(): lax.ppermute(conv_input[conv_input.shape[0] - 8:], SEQ, [(i, i + 1) for i...]
    ppermute x18 -> x15, starting transfers between devices: 28.7 us -> 24.5 us  [shifted(): lax.ppermute(block, axis, [(i, (i + by) % count) for i in range(count)])]
    all_to_all x1, blocking collectives: 20.8 us -> 23.6 us  [local(): ends = lax.all_to_all(ends, SEQ, split_axis=0, concat_axis=0, tiled=True)]
    ppermute x1, waiting for transfers between devices: 6.38 us -> 3.63 us  [local(): x_oth = lax.ppermute(x_own, 'core', swap)]
    all_to_all x1, starting transfers between devices: 8.57 us -> 10.9 us  [from_everyone(): return lax.all_to_all(copies, axis, split_axis=0, concat_axis=0, tiled=True)]
    slice x6 -> x7, local copies, waits for them, and re-layouts: 3.73 us -> 5.55 us  [the longest x4 3.97 us: halves_on(): return (shifted(up[:half], axis, 1), shifted(down[half:], axis, -1))]
    dynamic_update_slice x22 -> x18, local copies, waits for them, and re-layouts: 13.8 us -> 15.2 us  [placed(): lax.dynamic_update_slice(out, block[None], ((here + by) % count, row) + (...]
  transfers between devices with their start and end apart: 22 -> 19, of which waited for: 5 -> 6; matrix products, arithmetic and copies ran while one was open for 10% -> 14% of each run, Pallas kernels for 9% -> 8%
where the time goes in v4:
time: 197 us; the launch traced here: 196 us
  Pallas kernels  64.8 us (33%)
  blocking collectives  40.4 us (21%)
  starting transfers between devices  38.6 us (20%)
  local copies, waits for them, and re-layouts  28.8 us (15%)
  waiting for transfers between devices  21.3 us (11%)
  other arithmetic  2.19 us (1%)
    pallas_call x1, Pallas kernels, scan(): pl.pallas_call(scan_kernel, grid_spec=grid_spec, out_shape=[jax.ShapeDtyp...  28.5 us
    ppermute x15, starting transfers between devices, shifted(): lax.ppermute(block, axis, [(i, (i + by) % count) for i in range(count)])  24.5 us
    all_to_all x1, blocking collectives, local(): ends = lax.all_to_all(ends, SEQ, split_axis=0, concat_axis=0, tiled=True)  23.6 us
    pallas_call x1, Pallas kernels, close(): pl.pallas_call(close_kernel, grid=(inner // BLK,), in_specs=[pl.BlockSpec...  18.7 us
    ppermute x15, waiting for transfers between devices, shifted(): lax.ppermute(block, axis, [(i, (i + by) % count) for i in range(count)])  16.9 us
    all_to_all x1, blocking collectives, local(): lax.all_to_all(link(ends, a_log), SEQ, split_axis=0, concat_axis=0, tiled...  16.8 us
    dynamic_update_slice x18, local copies, waits for them, and re-layouts, placed(): lax.dynamic_update_slice(out, block[None], ((here + by) % count, row) + (...  15.2 us
    all_to_all x1, starting transfers between devices, from_everyone(): return lax.all_to_all(copies, axis, split_axis=0, concat_axis=0, tiled=True)  10.9 us
  transfers between devices with their start and end apart: 19, of which 6 were waited for; matrix products, arithmetic and copies ran while one was open for 14% of the time, Pallas kernels for 8%

profile of v4, /device:TPU:32, one launch (start us, length us, event | category | flops | bytes accessed | tf_op | source)
XLA Modules:
  0.0 196.3 jit_solution(11450692681443711251)
XLA Ops:
  2.3 3.3 %collective-permute-start.3 = (bf16[152,256]{1,0:T(8,128)(2,1)S(1)}, bf16[152,256]{1,0:T(8,128)(2,1)S(1)}, u32[]{:S(2)}, u32[]{:S(2)}) collective-permute-start(bf16[152,256]{1,0:T(8,128)(2,1)S(1)} %concatenate.11), channel_id=1, source_target_pairs={{0,16},{8,24},{16,32},{24,40},{32,48},{40,56},{48,0},{56,8},{1,17}... | collective-permute-start | bytes 233480 | tf_op jit(solution)/shard_map/ppermute | solution.py:317
  5.7 2.2 %collective-permute-start.2 = (bf16[152,256]{1,0:T(8,128)(2,1)S(1)}, bf16[152,256]{1,0:T(8,128)(2,1)S(1)}, u32[]{:S(2)}, u32[]{:S(2)}) collective-permute-start(bf16[152,256]{1,0:T(8,128)(2,1)S(1)} %concatenate.11), channel_id=1, source_target_pairs={{0,48},{8,56},{16,0},{24,8},{32,16},{40,24},{48,32},{56,40},{1,49}... | collective-permute-start | bytes 233480 | tf_op jit(solution)/shard_map/ppermute | solution.py:317
  10.8 2.8 %collective-permute-start.7 = (bf16[8,8192]{1,0:T(8,128)(2,1)S(1)}, bf16[8,8192]{1,0:T(8,128)(2,1)S(1)}, u32[]{:S(2)}, u32[]{:S(2)}) collective-permute-start(bf16[8,8192]{1,0:T(8,128)(2,1)S(1)} %slice.29), channel_id=1, source_target_pairs={{0,8},{8,16},{16,24},{24,32},{32,40},{40,48},{48,56},{56,64},{64,7... | collective-permute-start | bytes 393224 | tf_op jit(solution)/shard_map/ppermute | solution.py:356
  16.2 10.9 %all-to-all-start = ((bf16[32,1,96,128]{3,2,1,0:T(8,128)(2,1)}), bf16[32,1,96,128]{3,2,1,0:T(8,128)(2,1)S(1)}, u32[]{:S(2)}, u32[]{:S(2)}) async-start(bf16[32,1,96,128]{3,2,1,0:T(8,128)(2,1)} %broadcast_in_dim.82), calls=%async_computation | async-start | bytes 1572864 | tf_op jit(solution)/shard_map/all_to_all | solution.py:297
  28.6 2.4 %collective-permute-start.6 = (bf16[152,256]{1,0:T(8,128)(2,1)S(1)}, bf16[152,256]{1,0:T(8,128)(2,1)S(1)}, u32[]{:S(2)}, u32[]{:S(2)}) collective-permute-start(bf16[152,256]{1,0:T(8,128)(2,1)S(1)} %collective-permute-done.3), channel_id=1, source_target_pairs={{0,16},{8,24},{16,32},{24,40},{32,48},{40,56},{48,0},{56,8},{1,17}... | collective-permute-start | bytes 233480 | tf_op jit(solution)/shard_map/ppermute | solution.py:317
  31.1 2.7 %collective-permute-start.5 = (bf16[152,256]{1,0:T(8,128)(2,1)S(1)}, bf16[152,256]{1,0:T(8,128)(2,1)S(1)}, u32[]{:S(2)}, u32[]{:S(2)}) collective-permute-start(bf16[152,256]{1,0:T(8,128)(2,1)S(1)} %collective-permute-done.3), channel_id=1, source_target_pairs={{0,8},{8,16},{16,24},{24,32},{32,40},{40,48},{48,56},{56,0},{1,9},... | collective-permute-start | bytes 233480 | tf_op jit(solution)/shard_map/ppermute | solution.py:317
  36.3 9.0 %collective-permute-done.4 = bf16[152,256]{1,0:T(8,128)(2,1)S(1)} collective-permute-done((bf16[152,256]{1,0:T(8,128)(2,1)S(1)}, bf16[152,256]{1,0:T(8,128)(2,1)S(1)}, u32[]{:S(2)}, u32[]{:S(2)}) %collective-permute-start.4) | collective-permute-done | bytes 77856 | tf_op jit(solution)/shard_map/ppermute | solution.py:317
  50.7 2.1 %collective-permute-start.14 = (bf16[8,152,256]{2,1,0:T(8,128)(2,1)}, bf16[8,152,256]{2,1,0:T(8,128)(2,1)}, u32[]{:S(2)}, u32[]{:S(2)}) collective-permute-start(bf16[8,152,256]{2,1,0:T(8,128)(2,1)} %bitcast_dynamic-update-slice_fusion.10), channel_id=1, source_target_pairs={{0,192},{64,0},{128,64},{192,128},{1,193},{65,1},{129,65},{193,129... | collective-permute-start | bytes 1867784 | tf_op jit(solution)/shard_map/ppermute | solution.py:317
  54.4 2.8 %collective-permute-start.9 = (bf16[32,80,128]{2,1,0:T(8,128)(2,1)}, bf16[32,80,128]{2,1,0:T(8,128)(2,1)}, u32[]{:S(2)}, u32[]{:S(2)}) collective-permute-start(bf16[32,80,128]{2,1,0:T(8,128)(2,1)} %slice.38), channel_id=1, source_target_pairs={{0,6},{2,0},{4,2},{6,4},{1,7},{3,1},{5,3},{7,5},{8,14},{10,8},{12,... | collective-permute-start | bytes 1966088 | tf_op jit(solution)/shard_map/ppermute | solution.py:317
  57.2 7.6 %conv.1.xc_ref = bf16[128,8192]{1,0:T(8,128)(2,1)} custom-call(bf16[128,8192]{1,0:T(8,128)(2,1)} %ci_ref.1, bf16[8,8192]{1,0:T(8,128)(2,1)} %copy-done.3, bf16[32,16,128]{2,1,0:T(8,128)(2,1)} %slice.39.par_ref), custom_call_target="tpu_custom_call" | custom-call | tf_op jit(solution)/shard_map/conv/pallas_call | solution.py:45
  65.2 1.7 broadcast_in_dim.100
  66.9 1.9 bitcast_dynamic-update-slice_fusion.5
  69.9 3.4 %collective-permute-start.16 = (bf16[4,152,256]{2,1,0:T(8,128)(2,1)S(1)}, bf16[4,152,256]{2,1,0:T(8,128)(2,1)S(1)}, u32[]{:S(2)}, u32[]{:S(2)}) collective-permute-start(bf16[4,152,256]{2,1,0:T(8,128)(2,1)S(1)} %slice.41), channel_id=1, source_target_pairs={{0,192},{64,0},{128,64},{192,128},{1,193},{65,1},{129,65},{193,129... | collective-permute-start | bytes 933896 | tf_op jit(solution)/shard_map/ppermute | solution.py:317
  74.5 2.0 %bitcast_dynamic-update-slice_fusion.4 = bf16[4,8,152,256]{3,2,1,0:T(8,128)(2,1)} fusion(bf16[4,8,152,256]{3,2,1,0:T(8,128)(2,1)} %bitcast_dynamic-update-slice_fusion.5, s32[]{:T(128)S(6)} %select_n.171, bf16[8,152,256]{2,1,0:T(8,128)(2,1)} %collective-permute-done.13), kind=kLoop, calls=%fused_computation.4 | loop fusion | bytes 1245188 | tf_op jit(solution)/shard_map/dynamic_update_slice | solution.py:326
  76.5 2.0 bitcast_dynamic-update-slice_fusion.3
  80.5 3.3 %collective-permute-start.11 = (bf16[16,80,128]{2,1,0:T(8,128)(2,1)S(1)}, bf16[16,80,128]{2,1,0:T(8,128)(2,1)S(1)}, u32[]{:S(2)}, u32[]{:S(2)}) collective-permute-start(bf16[16,80,128]{2,1,0:T(8,128)(2,1)S(1)} %slice.33), channel_id=1, source_target_pairs={{0,6},{2,0},{4,2},{6,4},{1,7},{3,1},{5,3},{7,5},{8,14},{10,8},{12,... | collective-permute-start | bytes 983048 | tf_op jit(solution)/shard_map/ppermute | solution.py:317
  86.9 5.1 %collective-permute-done.10 = bf16[16,80,128]{2,1,0:T(8,128)(2,1)S(1)} collective-permute-done((bf16[16,80,128]{2,1,0:T(8,128)(2,1)S(1)}, bf16[16,80,128]{2,1,0:T(8,128)(2,1)S(1)}, u32[]{:S(2)}, u32[]{:S(2)}) %collective-permute-start.10) | collective-permute-done | bytes 327712 | tf_op jit(solution)/shard_map/ppermute | solution.py:317
  93.5 3.6 %collective-permute-done.12.oth_ref = bf16[4,32,80,128]{3,2,1,0:T(8,128)(2,1)S(1)} collective-permute-done((bf16[4,32,80,128]{3,2,1,0:T(8,128)(2,1)S(1)}, bf16[4,32,80,128]{3,2,1,0:T(8,128)(2,1)S(1)}, u32[]{:S(2)}, u32[]{:S(2)}) %collective-permute-start.12) | collective-permute-done | bytes 2621472 | tf_op jit(solution)/shard_map/ppermute | solution.py:369
  98.7 8.2 %front.1 = (bf16[128,256]{1,0:T(8,128)(2,1)}, f32[4096,128]{1,0:T(8,128)}) custom-call(s32[1]{0:T(128)} %bitcast.core_ref.where_ref, bf16[128,8192]{1,0:T(8,128)(2,1)} %conv.1.xc_ref, bf16[4,32,80,128]{3,2,1,0:T(8,128)(2,1)} %copy-done.1, bf16[4,32,80,128]{3,2,1,0:T(8,128)(2,1)} %copy-done.2, f32[1,256]{1,0:T(1,128)} %bitcast.44), custom_call_target="tpu_custom_call" | custom-call | tf_op jit(solution)/shard_map/front/pallas_call | solution.py:95
  106.9 28.5 %scan.1 = (f32[8,1024,128]{2,1,0:T(8,128)}, f32[8,1024,128]{2,1,0:T(8,128)}, f32[8,128,128]{2,1,0:T(8,128)}, bf16[32,40,128]{2,1,0:T(8,128)(2,1)}) custom-call(s32[1]{0:T(128)} %bitcast.core_ref.where_ref, bf16[128,256]{1,0:T(8,128)(2,1)} %get-tuple-element.30.normed_ref, bf16[128,8192]{1,0:T(8,128)(2,1)} %conv.1.xc_ref, ...), custom_call_target="tpu_custom_call" | custom-call | tf_op jit(solution)/shard_map/scan/pallas_call | solution.py:207
  135.4 23.6 %all_to_all.15.ends_ref = bf16[32,40,128]{2,1,0:T(8,128)(2,1)} all-to-all(bf16[32,40,128]{2,1,0:T(8,128)(2,1)} %get-tuple-element.36), channel_id=1, replica_groups=mesh['y'=4,'z'=8,'x'=4,'core'=2] {'y','z'}, dimensions={0} | all-to-all | bytes 655360 | tf_op jit(solution)/shard_map/all_to_all | solution.py:375
  159.0 1.8 link.1
  160.8 16.8 %all_to_all.16.start_ref = bf16[32,32,128]{2,1,0:T(8,128)(2,1)} all-to-all(bf16[32,32,128]{2,1,0:T(8,128)(2,1)} %link.1), channel_id=1, replica_groups=mesh['y'=4,'z'=8,'x'=4,'core'=2] {'y','z'}, dimensions={0} | all-to-all | bytes 524288 | tf_op jit(solution)/shard_map/all_to_all | solution.py:376
  177.6 18.7 %close.1 = bf16[128,8192]{1,0:T(8,128)(2,1)} custom-call(f32[8,1024,128]{2,1,0:T(8,128)} %get-tuple-element.33.step_ref, f32[8,1024,128]{2,1,0:T(8,128)} %get-tuple-element.34.y_ref, f32[8,128,128]{2,1,0:T(8,128)} %get-tuple-element.35.rate_ref, bf16[32,32,128]{2,1,0:T(8,128)(2,1)} %all_to_all.16.start_ref, f32[4096,128]{1,0:T(8,128)} %get-tuple-element.32.bc_ref.c_ref, ...), custom_call_target="tpu_custom_call" | custom-call | tf_op jit(solution)/shard_map/close/pallas_call | solution.py:276
  (73 shorter events, 29.6 us)
Async XLA Ops:
  0.0 15.2 %copy-start = (bf16[256,288]{0,1:T(8,128)(2,1)S(1)}, bf16[256,288]{0,1:T(8,128)(2,1)}, u32[]{:S(2)}) copy-start(bf16[256,288]{0,1:T(8,128)(2,1)} %param.14) | copy-start | bytes 442372
  2.3 26.3 %collective-permute-start.3 = (bf16[152,256]{1,0:T(8,128)(2,1)S(1)}, bf16[152,256]{1,0:T(8,128)(2,1)S(1)}, u32[]{:S(2)}, u32[]{:S(2)}) collective-permute-start(bf16[152,256]{1,0:T(8,128)(2,1)S(1)} %concatenate.11), channel_id=1, source_target_pairs={{0,16},{8,24},{16,32},{24,40},{32,48},{40,56},{48,0},{56,8},{1,17}... | collective-permute-start | bytes 233480 | tf_op jit(solution)/shard_map/ppermute | solution.py:317
  5.7 23.0 %collective-permute-start.2 = (bf16[152,256]{1,0:T(8,128)(2,1)S(1)}, bf16[152,256]{1,0:T(8,128)(2,1)S(1)}, u32[]{:S(2)}, u32[]{:S(2)}) collective-permute-start(bf16[152,256]{1,0:T(8,128)(2,1)S(1)} %concatenate.11), channel_id=1, source_target_pairs={{0,48},{8,56},{16,0},{24,8},{32,16},{40,24},{48,32},{56,40},{1,49}... | collective-permute-start | bytes 233480 | tf_op jit(solution)/shard_map/ppermute | solution.py:317
  7.9 20.7 %collective-permute-start.1 = (bf16[152,256]{1,0:T(8,128)(2,1)S(1)}, bf16[152,256]{1,0:T(8,128)(2,1)S(1)}, u32[]{:S(2)}, u32[]{:S(2)}) collective-permute-start(bf16[152,256]{1,0:T(8,128)(2,1)S(1)} %concatenate.11), channel_id=1, source_target_pairs={{0,8},{8,16},{16,24},{24,32},{32,40},{40,48},{48,56},{56,0},{1,9},... | collective-permute-start | bytes 233480 | tf_op jit(solution)/shard_map/ppermute | solution.py:317
  8.8 19.8 %collective-permute-start = (bf16[152,256]{1,0:T(8,128)(2,1)S(1)}, bf16[152,256]{1,0:T(8,128)(2,1)S(1)}, u32[]{:S(2)}, u32[]{:S(2)}) collective-permute-start(bf16[152,256]{1,0:T(8,128)(2,1)S(1)} %concatenate.11), channel_id=1, source_target_pairs={{0,56},{8,0},{16,8},{24,16},{32,24},{40,32},{48,40},{56,48},{1,57}... | collective-permute-start | bytes 233480 | tf_op jit(solution)/shard_map/ppermute | solution.py:317
  10.8 39.1 %collective-permute-start.7 = (bf16[8,8192]{1,0:T(8,128)(2,1)S(1)}, bf16[8,8192]{1,0:T(8,128)(2,1)S(1)}, u32[]{:S(2)}, u32[]{:S(2)}) collective-permute-start(bf16[8,8192]{1,0:T(8,128)(2,1)S(1)} %slice.29), channel_id=1, source_target_pairs={{0,8},{8,16},{16,24},{24,32},{32,40},{40,48},{48,56},{56,64},{64,7... | collective-permute-start | bytes 393224 | tf_op jit(solution)/shard_map/ppermute | solution.py:356
  16.2 34.5 %all-to-all-start = ((bf16[32,1,96,128]{3,2,1,0:T(8,128)(2,1)}), bf16[32,1,96,128]{3,2,1,0:T(8,128)(2,1)S(1)}, u32[]{:S(2)}, u32[]{:S(2)}) async-start(bf16[32,1,96,128]{3,2,1,0:T(8,128)(2,1)} %broadcast_in_dim.82), calls=%async_computation | async-start | bytes 1572864 | tf_op jit(solution)/shard_map/all_to_all | solution.py:297
  28.6 20.7 %collective-permute-start.6 = (bf16[152,256]{1,0:T(8,128)(2,1)S(1)}, bf16[152,256]{1,0:T(8,128)(2,1)S(1)}, u32[]{:S(2)}, u32[]{:S(2)}) collective-permute-start(bf16[152,256]{1,0:T(8,128)(2,1)S(1)} %collective-permute-done.3), channel_id=1, source_target_pairs={{0,16},{8,24},{16,32},{24,40},{32,48},{40,56},{48,0},{56,8},{1,17}... | collective-permute-start | bytes 233480 | tf_op jit(solution)/shard_map/ppermute | solution.py:317
  31.1 16.2 %collective-permute-start.5 = (bf16[152,256]{1,0:T(8,128)(2,1)S(1)}, bf16[152,256]{1,0:T(8,128)(2,1)S(1)}, u32[]{:S(2)}, u32[]{:S(2)}) collective-permute-start(bf16[152,256]{1,0:T(8,128)(2,1)S(1)} %collective-permute-done.3), channel_id=1, source_target_pairs={{0,8},{8,16},{16,24},{24,32},{32,40},{40,48},{48,56},{56,0},{1,9},... | collective-permute-start | bytes 233480 | tf_op jit(solution)/shard_map/ppermute | solution.py:317
  33.8 11.5 %collective-permute-start.4 = (bf16[152,256]{1,0:T(8,128)(2,1)S(1)}, bf16[152,256]{1,0:T(8,128)(2,1)S(1)}, u32[]{:S(2)}, u32[]{:S(2)}) collective-permute-start(bf16[152,256]{1,0:T(8,128)(2,1)S(1)} %collective-permute-done.2), channel_id=1, source_target_pairs={{0,56},{8,0},{16,8},{24,16},{32,24},{40,32},{48,40},{56,48},{1,57}... | collective-permute-start | bytes 233480 | tf_op jit(solution)/shard_map/ppermute | solution.py:317
  50.0 7.2 %copy-start.3 = (bf16[8,8192]{1,0:T(8,128)(2,1)}, bf16[8,8192]{1,0:T(8,128)(2,1)S(1)}, u32[]{:S(2)}) copy-start(bf16[8,8192]{1,0:T(8,128)(2,1)S(1)} %collective-permute-done.7.prior_ref) | copy-start | bytes 393220
  50.7 18.2 %collective-permute-start.14 = (bf16[8,152,256]{2,1,0:T(8,128)(2,1)}, bf16[8,152,256]{2,1,0:T(8,128)(2,1)}, u32[]{:S(2)}, u32[]{:S(2)}) collective-permute-start(bf16[8,152,256]{2,1,0:T(8,128)(2,1)} %bitcast_dynamic-update-slice_fusion.10), channel_id=1, source_target_pairs={{0,192},{64,0},{128,64},{192,128},{1,193},{65,1},{129,65},{193,129... | collective-permute-start | bytes 1867784 | tf_op jit(solution)/shard_map/ppermute | solution.py:317
  52.8 20.4 %collective-permute-start.13 = (bf16[8,152,256]{2,1,0:T(8,128)(2,1)}, bf16[8,152,256]{2,1,0:T(8,128)(2,1)}, u32[]{:S(2)}, u32[]{:S(2)}) collective-permute-start(bf16[8,152,256]{2,1,0:T(8,128)(2,1)} %bitcast_dynamic-update-slice_fusion.10), channel_id=1, source_target_pairs={{0,64},{64,128},{128,192},{192,0},{1,65},{65,129},{129,193},{193,1... | collective-permute-start | bytes 1867784 | tf_op jit(solution)/shard_map/ppermute | solution.py:317
  54.4 24.1 %collective-permute-start.9 = (bf16[32,80,128]{2,1,0:T(8,128)(2,1)}, bf16[32,80,128]{2,1,0:T(8,128)(2,1)}, u32[]{:S(2)}, u32[]{:S(2)}) collective-permute-start(bf16[32,80,128]{2,1,0:T(8,128)(2,1)} %slice.38), channel_id=1, source_target_pairs={{0,6},{2,0},{4,2},{6,4},{1,7},{3,1},{5,3},{7,5},{8,14},{10,8},{12,... | collective-permute-start | bytes 1966088 | tf_op jit(solution)/shard_map/ppermute | solution.py:317
  57.2 21.3 %collective-permute-start.8 = (bf16[32,80,128]{2,1,0:T(8,128)(2,1)}, bf16[32,80,128]{2,1,0:T(8,128)(2,1)}, u32[]{:S(2)}, u32[]{:S(2)}) collective-permute-start(bf16[32,80,128]{2,1,0:T(8,128)(2,1)} %slice.38), channel_id=1, source_target_pairs={{0,2},{2,4},{4,6},{6,0},{1,3},{3,5},{5,7},{7,1},{8,10},{10,12},{12... | collective-permute-start | bytes 1966088 | tf_op jit(solution)/shard_map/ppermute | solution.py:317
  69.9 22.4 %collective-permute-start.16 = (bf16[4,152,256]{2,1,0:T(8,128)(2,1)S(1)}, bf16[4,152,256]{2,1,0:T(8,128)(2,1)S(1)}, u32[]{:S(2)}, u32[]{:S(2)}) collective-permute-start(bf16[4,152,256]{2,1,0:T(8,128)(2,1)S(1)} %slice.41), channel_id=1, source_target_pairs={{0,192},{64,0},{128,64},{192,128},{1,193},{65,1},{129,65},{193,129... | collective-permute-start | bytes 933896 | tf_op jit(solution)/shard_map/ppermute | solution.py:317
  74.2 11.9 %collective-permute-start.15 = (bf16[4,152,256]{2,1,0:T(8,128)(2,1)S(1)}, bf16[4,152,256]{2,1,0:T(8,128)(2,1)S(1)}, u32[]{:S(2)}, u32[]{:S(2)}) collective-permute-start(bf16[4,152,256]{2,1,0:T(8,128)(2,1)S(1)} %slice.40), channel_id=1, source_target_pairs={{0,64},{64,128},{128,192},{192,0},{1,65},{65,129},{129,193},{193,1... | collective-permute-start | bytes 933896 | tf_op jit(solution)/shard_map/ppermute | solution.py:317
  80.5 11.6 %collective-permute-start.11 = (bf16[16,80,128]{2,1,0:T(8,128)(2,1)S(1)}, bf16[16,80,128]{2,1,0:T(8,128)(2,1)S(1)}, u32[]{:S(2)}, u32[]{:S(2)}) collective-permute-start(bf16[16,80,128]{2,1,0:T(8,128)(2,1)S(1)} %slice.33), channel_id=1, source_target_pairs={{0,6},{2,0},{4,2},{6,4},{1,7},{3,1},{5,3},{7,5},{8,14},{10,8},{12,... | collective-permute-start | bytes 983048 | tf_op jit(solution)/shard_map/ppermute | solution.py:317
  83.8 8.3 %collective-permute-start.10 = (bf16[16,80,128]{2,1,0:T(8,128)(2,1)S(1)}, bf16[16,80,128]{2,1,0:T(8,128)(2,1)S(1)}, u32[]{:S(2)}, u32[]{:S(2)}) collective-permute-start(bf16[16,80,128]{2,1,0:T(8,128)(2,1)S(1)} %slice.32), channel_id=1, source_target_pairs={{0,2},{2,4},{4,6},{6,0},{1,3},{3,5},{5,7},{7,1},{8,10},{10,12},{12... | collective-permute-start | bytes 983048 | tf_op jit(solution)/shard_map/ppermute | solution.py:317
  92.2 6.6 %copy-start.1 = (bf16[4,32,80,128]{3,2,1,0:T(8,128)(2,1)}, bf16[4,32,80,128]{3,2,1,0:T(8,128)(2,1)S(1)}, u32[]{:S(2)}) copy-start(bf16[4,32,80,128]{3,2,1,0:T(8,128)(2,1)S(1)} %bitcast_dynamic-update-slice_fusion.6.own_ref) | copy-start | bytes 7864324
  92.2 5.0 %collective-permute-start.12 = (bf16[4,32,80,128]{3,2,1,0:T(8,128)(2,1)S(1)}, bf16[4,32,80,128]{3,2,1,0:T(8,128)(2,1)S(1)}, u32[]{:S(2)}, u32[]{:S(2)}) collective-permute-start(bf16[4,32,80,128]{3,2,1,0:T(8,128)(2,1)S(1)} %bitcast_dynamic-update-slice_fusion.6.own_ref), channel_id=1, source_target_pairs={{0,1},{1,0},{2,3},{3,2},{4,5},{5,4},{6,7},{7,6},{8,9},{9,8},{10,11... | collective-permute-start | bytes 7864328 | tf_op jit(solution)/shard_map/ppermute | solution.py:369
  93.2 13.7 %collective-permute-start.17 = (bf16[4,8,152,256]{3,2,1,0:T(8,128)(2,1)}, bf16[4,8,152,256]{3,2,1,0:T(8,128)(2,1)}, u32[]{:S(2)}, u32[]{:S(2)}) collective-permute-start(bf16[4,8,152,256]{3,2,1,0:T(8,128)(2,1)} %bitcast_dynamic-update-slice_fusion.8.own_ref), channel_id=1, source_target_pairs={{0,1},{1,0},{2,3},{3,2},{4,5},{5,4},{6,7},{7,6},{8,9},{9,8},{10,11... | collective-permute-start | bytes 7471112 | tf_op jit(solution)/shard_map/ppermute | solution.py:371
  97.2 1.5 copy-start.2

commit v5 on v4

--- a/solution.py
+++ b/solution.py
@@ -5,6 +5,7 @@
 from jax.experimental.pallas import tpu as pltpu
 from jax.sharding import Mesh, PartitionSpec as P
 
+
 F32 = jnp.float32
 BF16 = jnp.bfloat16
 LOG2E = 1.4426950408889634
@@ -26,83 +27,112 @@
     return high.astype(BF16), (v - high).astype(BF16)
 
 
-def conv_kernel(ci_ref, prior_ref, par_ref, xc_ref, pad_ref):
+def conv_kernel(core_ref, ci_ref, prior_ref, par_ref, xc_ref, lend_ref, pad_ref):
+    core = core_ref[0]
     rows = ci_ref.shape[0]
     taps = 4
     pad_ref[0:8, :] = prior_ref[...].astype(F32)
     pad_ref[8 : 8 + rows, :] = ci_ref[...].astype(F32)
     for s in range(4):
-        par = jnp.concatenate([par_ref[s, 0:8, :], par_ref[s, 8:16, :]], 1).astype(F32)
+        par = par_ref[s, 0].astype(F32)
         lanes = slice(s * SHARD, (s + 1) * SHARD)
         total = jnp.broadcast_to(par[taps : taps + 1, :], (rows, SHARD))
         for k in range(taps):
             total = total + par[k : k + 1, :] * pad_ref[5 + k : 5 + k + rows, lanes]
         xc_ref[:, lanes] = silu(total).astype(BF16)
-
-
-def conv(conv_input, prior, params):
+        at = pl.multiple_of(s * SHARD + (1 - core) * 128, 128)
+        lend_ref[:, s * 128 : (s + 1) * 128] = xc_ref[:, pl.ds(at, 128)]
+
+
+def conv(core, conv_input, prior, params):
     rows, inner = conv_input.shape
     return pl.pallas_call(
         conv_kernel,
         grid=(inner // BLK,),
         in_specs=[
+            pl.BlockSpec(memory_space=pltpu.SMEM),
             pl.BlockSpec((rows, BLK), lambda b: (0, b)),
             pl.BlockSpec((8, BLK), lambda b: (0, b)),
-            pl.BlockSpec((4, 16, 128), lambda b: (b, 0, 0)),
-        ],
-        out_specs=pl.BlockSpec((rows, BLK), lambda b: (0, b)),
-        out_shape=jax.ShapeDtypeStruct((rows, inner), BF16),
+            pl.BlockSpec((4, 1, 8, SHARD), lambda b: (b % 2, b // 2, 0, 0)),
+        ],
+        out_specs=[
+            pl.BlockSpec((rows, BLK), lambda b: (0, b)),
+            pl.BlockSpec((rows, BLK // 2), lambda b: (0, b)),
+        ],
+        out_shape=[
+            jax.ShapeDtypeStruct((rows, inner), BF16),
+            jax.ShapeDtypeStruct((rows, inner // 2), BF16),
+        ],
         scratch_shapes=[pltpu.VMEM((rows + 8, BLK), F32)],
         compiler_params=pltpu.CompilerParams(dimension_semantics=("arbitrary",)),
         name="conv",
-    )(conv_input, prior, params)
+    )(core, conv_input, prior, params)
+
+
+AWAY = (0, -1, 1, -2, 2, -3, 3, 4, 4)
 
 
 def times_rows(left, right):
     return lax.dot_general(left, right, (((1,), (1,)), ((), ())), preferred_element_type=F32)
 
 
-def front_kernel(core_ref, xc_ref, own_ref, oth_ref, gain_ref, normed_ref, bc_ref, acc_ref):
-    core = core_ref[0]
+def project_kernel(where_ref, xc_ref, lent_ref, *refs):
+    blocks, (own_ref, other_ref) = refs[:-2], refs[-2:]
+    core, here = where_ref[0], where_ref[1]
     rows = xc_ref.shape[0]
-    rank = gain_ref.shape[1]
-    acc_ref[...] = jnp.zeros_like(acc_ref)
-
-    def add_shards(group, _):
-        acc = acc_ref[...]
-        for k in range(4):
-            s = group * 4 + k
-            mine = pl.multiple_of(s * SHARD + core * 128, 128)
-            other = pl.multiple_of(s * SHARD + (1 - core) * 128, 128)
-            left = jnp.concatenate([xc_ref[:, pl.ds(mine, 128)], xc_ref[:, pl.ds(other, 128)]], 1)
-            right = [jnp.concatenate([ref[q, s] for q in range(4)], 0) for ref in (own_ref, oth_ref)]
-            acc = acc + times_rows(left, jnp.concatenate(right, 1))
-        acc_ref[...] = acc
-        return 0
-
-    lax.fori_loop(0, own_ref.shape[1] // 4, add_shards, 0)
-    low = acc_ref[:, 0:rank]
+    total = None
+    for k, (away, block) in enumerate(zip(AWAY, blocks)):
+        first = 2 if k == len(AWAY) - 1 else 0
+        z = lax.rem(here + 8 + away, 8)
+        for row in range(0, block.shape[0], 2):
+            left = []
+            for y in (first + row, first + row + 1):
+                mine = pl.multiple_of((y * 8 + z) * SHARD + core * 128, 128)
+                lent = pl.multiple_of((y * 8 + z) * 128, 128)
+                left.append(jnp.concatenate([xc_ref[:, pl.ds(mine, 128)], lent_ref[:, pl.ds(lent, 128)]], 0))
+            right = jnp.concatenate([block[row, 0:288, :], block[row + 1, 0:288, :]], 1)
+            part = times_rows(jnp.concatenate(left, 1), right)
+            total = part if total is None else total + part
+    own_ref[...] = total[:rows]
+    other_ref[...] = total[rows:]
+
+
+def project(where, xc, lent, blocks):
+    rows = xc.shape[0]
+    vmem = pl.BlockSpec(memory_space=pltpu.VMEM)
+    shape = jax.ShapeDtypeStruct((rows, 288), F32)
+    return pl.pallas_call(
+        project_kernel,
+        in_specs=[pl.BlockSpec(memory_space=pltpu.SMEM)] + [vmem] * (2 + len(blocks)),
+        out_specs=[vmem, vmem],
+        out_shape=[shape, shape],
+        name="project",
+    )(where, xc, lent, *blocks)
+
+
+def norm_kernel(own_ref, other_ref, gain_ref, normed_ref, bc_ref):
+    rows, rank = normed_ref.shape
+    proj = own_ref[...] + other_ref[...]
+    low = proj[:, 0:rank]
     scale = lax.rsqrt(jnp.mean(low * low, axis=1, keepdims=True) + 1e-06)
     normed_ref[...] = (low * scale * gain_ref[...]).astype(BF16)
     for m in range(32):
-        col = acc_ref[:, rank + m : rank + m + 1]
-        bc_ref[m * rows : (m + 1) * rows, :] = jnp.broadcast_to(col, (rows, 128))
-
-
-def front(core, xc, x_own, x_oth, gain):
-    rows = xc.shape[0]
+        bc_ref[m * rows : (m + 1) * rows, :] = jnp.broadcast_to(proj[:, rank + m : rank + m + 1], (rows, 128))
+
+
+def norm(own, other, gain):
+    rows = own.shape[0]
     vmem = pl.BlockSpec(memory_space=pltpu.VMEM)
     return pl.pallas_call(
-        front_kernel,
-        in_specs=[pl.BlockSpec(memory_space=pltpu.SMEM), vmem, vmem, vmem, vmem],
+        norm_kernel,
+        in_specs=[vmem, vmem, vmem],
         out_specs=[vmem, vmem],
         out_shape=[
             jax.ShapeDtypeStruct((rows, 256), BF16),
             jax.ShapeDtypeStruct((32 * rows, 128), F32),
         ],
-        scratch_shapes=[pltpu.VMEM((rows, 320), F32)],
-        name="front",
-    )(core, xc, x_own, x_oth, gain)
+        name="norm",
+    )(own, other, gain)
 
 
 def scan_kernel(where_ref, normed_ref, xc_ref, own_ref, oth_ref, bc_ref, step_ref, y_ref, rate_ref, ends_ref, x_scr, par_scr, h_scr):
@@ -297,11 +327,10 @@
     return lax.all_to_all(copies, axis, split_axis=0, concat_axis=0, tiled=True)
 
 
-def pack_x(core, quarter, x_weight, conv_weight, conv_bias):
+def pack_x(core, x_weight, conv_weight, conv_bias):
     half = lax.dynamic_slice_in_dim(x_weight.T, core * 128, 128, 1)
-    part = lax.dynamic_slice_in_dim(jnp.pad(half, ((0, 32), (0, 0))), quarter * 80, 80, 0)
     taps = jnp.concatenate([conv_weight, conv_bias[None, :], jnp.zeros((3, SHARD), BF16)], 0)
-    return jnp.concatenate([part, taps[:, :128], taps[:, 128:]], 0)
+    return jnp.concatenate([half, taps[:, :128], taps[:, 128:]], 0)
 
 
 def pack_d(core, dt_weight, dt_bias, a_log, skip):
@@ -331,46 +360,37 @@
     return lax.optimization_barrier(values)
 
 
-def around_eight(block, axis):
-    near = {k: shifted(block, axis, -k) for k in (1, -1, 2, -2)}
-    near = dict(zip(near, together(*near.values())))
-    far = {3: shifted(near[2], axis, -1), -3: shifted(near[-2], axis, 1), 4: shifted(near[-2], axis, 2)}
-    blocks = {0: block, **near, **far}
-    return placed(list(blocks.values()), [(k, 0) for k in blocks], axis)
-
-
-def halves_on(up, down, axis):
-    half = up.shape[0] // 2
-    return shifted(up[:half], axis, 1), shifted(down[half:], axis, -1)
-
-
-def around_four(block, first, second, axis):
-    half = block.shape[0] // 2
-    return placed([block, *first, *second], [(0, 0), (-1, 0), (1, 0), (2, 0), (2, half)], axis)
-
-
-def local(conv_input, gate_input, conv_weight, conv_bias, x_weight, dt_gain, dt_weight, dt_bias, a_log, skip):
+def both_ways(pair, axis):
+    return shifted(pair[0], axis, 1), shifted(pair[1], axis, -1)
+
+
+def body(conv_input, gate_input, conv_weight, conv_bias, x_weight, dt_gain, dt_weight, dt_bias, a_log, skip):
     core = lax.axis_index("core")
     count = lax.axis_size(SEQ)
     swap = [(0, 1), (1, 0)]
+    where = jnp.stack([core, lax.axis_index("z")]).astype(jnp.int32)
     prior = lax.ppermute(conv_input[conv_input.shape[0] - 8 :], SEQ, [(i, i + 1) for i in range(count - 1)])
-    x_part = from_everyone(pack_x(core, lax.axis_index("x"), x_weight, conv_weight, conv_bias)[None], SEQ)
-    d0 = around_eight(pack_d(core, dt_weight, dt_bias, a_log, skip), "z")
-    x_part, d0, prior = together(x_part, d0, prior)
-    x_part = x_part.reshape(count, 96, 128)
-    x0 = x_part[:, :80]
-    x1 = shifted(x0, "x", 1), shifted(x0, "x", -1)
-    d1 = shifted(d0, "y", 1), shifted(d0, "y", -1)
-    xc = conv(conv_input, prior, x_part[:, 80:])
-    *x1, xc = together(*x1, xc)
-    x2 = halves_on(*x1, "x")
-    d2 = halves_on(*d1, "y")
-    x_own = around_four(x0, x1, x2, "x")
-    x_oth = lax.ppermute(x_own, "core", swap)
-    d_own = around_four(d0, d1, d2, "y")
+    x_piece = pack_x(core, x_weight, conv_weight, conv_bias)
+    x_pieces = [x_piece] + [shifted(x_piece, "y", k) for k in (1, 2, 3)]
+    x0 = placed(x_pieces, [(0, 0), (-1, 0), (-2, 0), (-3, 0)], "y")
+    x1 = both_ways((x0, x0), "z")
+    taps = jnp.concatenate([x0[:, 288:296], x0[:, 296:304]], 2).reshape(32, SHARD)
+    d_msg = jnp.concatenate([pack_d(core, dt_weight, dt_bias, a_log, skip), taps], 0)
+    d_part = from_everyone(d_msg, "z").reshape(8, 184, SHARD)
+    x2 = both_ways(x1, "z")
+    *x2, d_part, prior = together(*x2, d_part, prior)
+    d0 = d_part[:, :152]
+    d1 = both_ways((d0, d0), "y")
+    x3 = both_ways(x2, "z")
+    xc, lend = conv(where, conv_input, prior, d_part[:, 152:].reshape(8, 4, 8, SHARD))
+    lent = lax.ppermute(lend, "core", swap)
+    *x3, xc, up, down = together(*x3, xc, *d1)
+    x4 = both_ways((x3[0][:2], x3[1][2:]), "z")
+    d2 = both_ways((up[:4], down[4:]), "y")
+    d_own = placed([d0, up, down, *d2], [(0, 0), (-1, 0), (1, 0), (2, 0), (2, 4)], "y")
     d_oth = lax.ppermute(d_own, "core", swap)
-    where = core.reshape(1).astype(jnp.int32)
-    normed, bc = front(where, xc, x_own, x_oth, dt_gain[None, :])
+    own, other = project(where, xc, lent, [x0, *x1, *x2, *x3, *x4])
+    normed, bc = norm(own, lax.ppermute(other, "core", swap), dt_gain[None, :])
     step, y, rate, ends = scan(where, normed, xc, d_own, d_oth, bc)
     ends = lax.all_to_all(ends, SEQ, split_axis=0, concat_axis=0, tiled=True)
     start = lax.all_to_all(link(ends, a_log), SEQ, split_axis=0, concat_axis=0, tiled=True)
@@ -381,7 +401,7 @@
     inner = Mesh(mesh.devices.reshape(4, 8, 4, 2), ("y", "z", "x", "core"))
     tokens = P(("x", "core", "y", "z"), None)
     return jax.shard_map(
-        local,
+        body,
         mesh=inner,
         in_specs=(tokens, tokens, P(None, SEQ), P(SEQ), P(SEQ, None), P(), P(None, SEQ), P(SEQ), P(None, SEQ), P(SEQ)),
         out_specs=tokens,

time: 197 us -> 198 us (level)
  waiting for transfers between devices: 21.3 us -> 40 us
  local copies, waits for them, and re-layouts: 28.8 us -> 13 us
  starting transfers between devices: 38.6 us -> 34 us
    ppermute x15, waiting for transfers between devices: 16.9 us -> 34.2 us  [shifted(): lax.ppermute(block, axis, [(i, (i + by) % count) for i in range(count)])]
    dynamic_update_slice x18 -> x8, local copies, waits for them, and re-layouts: 15.2 us -> 2.39 us  [placed(): lax.dynamic_update_slice(out, block[None], ((here + by) % count, row) + (...]
    ppermute x15, starting transfers between devices: 24.5 us -> 20.5 us  [shifted(): lax.ppermute(block, axis, [(i, (i + by) % count) for i in range(count)])]
    broadcast_in_dim x3 -> x2, local copies, waits for them, and re-layouts: 2.95 us -> 0.21 us  [placed(): out = jnp.zeros((count, *first.shape), first.dtype)]
    all_to_all x1, starting transfers between devices: 10.9 us -> 8.57 us  [from_everyone(): return lax.all_to_all(copies, axis, split_axis=0, concat_axis=0, tiled=True)]
    ppermute x3 -> x4, waiting for transfers between devices: 3.64 us -> 5.8 us  [the longest x1 4.16 us: body(): lax.ppermute(conv_input[conv_input.shape[0] - 8:], SEQ, [(i, i + 1) for i...]
    ppermute x3 -> x4, starting transfers between devices: 3.26 us -> 4.91 us  [the longest x1 4.11 us: body(): lax.ppermute(conv_input[conv_input.shape[0] - 8:], SEQ, [(i, i + 1) for i...]
    pallas_call x1 -> x2, Pallas kernels: 8.18 us -> 7.61 us  [the longest x1 4.58 us: project(): pl.pallas_call(project_kernel, in_specs=[pl.BlockSpec(memory_space=pltpu....]
  transfers between devices with their start and end apart: 19 -> 20, of which waited for: 6 -> 9; matrix products, arithmetic and copies ran while one was open for 14% -> 5% of each run, Pallas kernels for 8% -> 8%
where the time goes in v5:
time: 198 us; the launch traced here: 197 us
  Pallas kernels  65.2 us (33%)
  blocking collectives  42.1 us (21%)
  waiting for transfers between devices  40 us (20%)
  starting transfers between devices  34 us (17%)
  local copies, waits for them, and re-layouts  13 us (7%)
  other arithmetic  2.77 us (1%)
    ppermute x15, waiting for transfers between devices, shifted(): lax.ppermute(block, axis, [(i, (i + by) % count) for i in range(count)])  34.2 us
    pallas_call x1, Pallas kernels, scan(): pl.pallas_call(scan_kernel, grid_spec=grid_spec, out_shape=[jax.ShapeDtyp...  29.2 us
    all_to_all x1, blocking collectives, body(): ends = lax.all_to_all(ends, SEQ, split_axis=0, concat_axis=0, tiled=True)  25.3 us
    ppermute x15, starting transfers between devices, shifted(): lax.ppermute(block, axis, [(i, (i + by) % count) for i in range(count)])  20.5 us
    pallas_call x1, Pallas kernels, close(): pl.pallas_call(close_kernel, grid=(inner // BLK,), in_specs=[pl.BlockSpec...  18.7 us
    all_to_all x1, blocking collectives, body(): lax.all_to_all(link(ends, a_log), SEQ, split_axis=0, concat_axis=0, tiled...  16.8 us
    all_to_all x1, starting transfers between devices, from_everyone(): return lax.all_to_all(copies, axis, split_axis=0, concat_axis=0, tiled=True)  8.57 us
    pallas_call x1, Pallas kernels, conv(): pl.pallas_call(conv_kernel, grid=(inner // BLK,), in_specs=[pl.BlockSpec(...  7.94 us
  transfers between devices with their start and end apart: 20, of which 9 were waited for; matrix products, arithmetic and copies ran while one was open for 5% of the time, Pallas kernels for 8%

profile of v5, /device:TPU:32, one launch (start us, length us, event | category | flops | bytes accessed | tf_op | source)
XLA Modules:
  0.0 197.4 jit_solution(13872993170359051206)
XLA Ops:
  1.6 3.3 %collective-permute-start.1 = (bf16[304,128]{1,0:T(8,128)(2,1)S(1)}, bf16[304,128]{1,0:T(8,128)(2,1)S(1)}, u32[]{:S(2)}, u32[]{:S(2)}) collective-permute-start(bf16[304,128]{1,0:T(8,128)(2,1)S(1)} %pad_maximum_fusion), channel_id=1, source_target_pairs={{0,128},{64,192},{128,0},{192,64},{1,129},{65,193},{129,1},{193,65... | collective-permute-start | bytes 233480 | tf_op jit(solution)/shard_map/ppermute | solution.py:346
  5.5 2.6 %collective-permute-start.2 = (bf16[304,128]{1,0:T(8,128)(2,1)S(1)}, bf16[304,128]{1,0:T(8,128)(2,1)S(1)}, u32[]{:S(2)}, u32[]{:S(2)}) collective-permute-start(bf16[304,128]{1,0:T(8,128)(2,1)S(1)} %pad_maximum_fusion), channel_id=1, source_target_pairs={{0,192},{64,0},{128,64},{192,128},{1,193},{65,1},{129,65},{193,129... | collective-permute-start | bytes 233480 | tf_op jit(solution)/shard_map/ppermute | solution.py:346
  11.5 8.6 %all-to-all-start = ((bf16[8,184,256]{2,1,0:T(8,128)(2,1)}), bf16[8,184,256]{2,1,0:T(8,128)(2,1)S(1)}, u32[]{:S(2)}, u32[]{:S(2)}) async-start(bf16[8,184,256]{2,1,0:T(8,128)(2,1)} %broadcast_in_dim.57), calls=%async_computation | async-start | bytes 1507328 | tf_op jit(solution)/shard_map/all_to_all | solution.py:327
  20.1 2.0 %collective-permute-start.3 = (bf16[4,304,128]{2,1,0:T(8,128)(2,1)S(1)}, bf16[4,304,128]{2,1,0:T(8,128)(2,1)S(1)}, u32[]{:S(2)}, u32[]{:S(2)}) collective-permute-start(bf16[4,304,128]{2,1,0:T(8,128)(2,1)S(1)} %bitcast_dynamic-update-slice_fusion.5.refs_0_), channel_id=1, source_target_pairs={{0,8},{8,16},{16,24},{24,32},{32,40},{40,48},{48,56},{56,0},{1,9},... | collective-permute-start | bytes 933896 | tf_op jit(solution)/shard_map/ppermute | solution.py:346
  22.1 21.7 %collective-permute-done.5.refs_2_ = bf16[4,304,128]{2,1,0:T(8,128)(2,1)S(1)} collective-permute-done((bf16[4,304,128]{2,1,0:T(8,128)(2,1)S(1)}, bf16[4,304,128]{2,1,0:T(8,128)(2,1)S(1)}, u32[]{:S(2)}, u32[]{:S(2)}) %collective-permute-start.5) | collective-permute-done | bytes 311328 | tf_op jit(solution)/shard_map/ppermute | solution.py:346
  46.8 4.1 %collective-permute-start.7 = (bf16[8,8192]{1,0:T(8,128)(2,1)S(1)}, bf16[8,8192]{1,0:T(8,128)(2,1)S(1)}, u32[]{:S(2)}, u32[]{:S(2)}) collective-permute-start(bf16[8,8192]{1,0:T(8,128)(2,1)S(1)} %slice.37), channel_id=1, source_target_pairs={{0,8},{8,16},{16,24},{24,32},{32,40},{40,48},{48,56},{56,64},{64,7... | collective-permute-start | bytes 393224 | tf_op jit(solution)/shard_map/ppermute | solution.py:372
  50.9 4.2 %collective-permute-done.7.prior_ref = bf16[8,8192]{1,0:T(8,128)(2,1)S(1)} collective-permute-done((bf16[8,8192]{1,0:T(8,128)(2,1)S(1)}, bf16[8,8192]{1,0:T(8,128)(2,1)S(1)}, u32[]{:S(2)}, u32[]{:S(2)}) %collective-permute-start.7) | collective-permute-done | bytes 131104 | tf_op jit(solution)/shard_map/ppermute | solution.py:372
  56.0 2.3 %collective-permute-start.11 = (bf16[8,152,256]{2,1,0:T(8,128)(2,1)}, bf16[8,152,256]{2,1,0:T(8,128)(2,1)}, u32[]{:S(2)}, u32[]{:S(2)}) collective-permute-start(bf16[8,152,256]{2,1,0:T(8,128)(2,1)} %slice.39), channel_id=1, source_target_pairs={{0,192},{64,0},{128,64},{192,128},{1,193},{65,1},{129,65},{193,129... | collective-permute-start | bytes 1867784 | tf_op jit(solution)/shard_map/ppermute | solution.py:346
  61.7 7.9 %conv.1 = (bf16[128,8192]{1,0:T(8,128)(2,1)}, bf16[128,4096]{1,0:T(8,128)(2,1)}) custom-call(s32[2]{0:T(128)} %pad_add_fusion.core_ref.where_ref, bf16[128,8192]{1,0:T(8,128)(2,1)} %ci_ref.1, bf16[8,8192]{1,0:T(8,128)(2,1)} %copy-done.8, bf16[8,4,8,256]{3,2,1,0:T(8,128)(2,1)} %slice_bitcast_fusion.par_ref), custom_call_target="tpu_custom_call" | custom-call | tf_op jit(solution)/shard_map/conv/pallas_call | solution.py:49
  70.1 3.3 %collective-permute-done.10 = bf16[8,152,256]{2,1,0:T(8,128)(2,1)} collective-permute-done((bf16[8,152,256]{2,1,0:T(8,128)(2,1)}, bf16[8,152,256]{2,1,0:T(8,128)(2,1)}, u32[]{:S(2)}, u32[]{:S(2)}) %collective-permute-start.10) | collective-permute-done | bytes 622624 | tf_op jit(solution)/shard_map/ppermute | solution.py:346
  76.6 3.3 %collective-permute-start.17 = (bf16[4,152,256]{2,1,0:T(8,128)(2,1)S(1)}, bf16[4,152,256]{2,1,0:T(8,128)(2,1)S(1)}, u32[]{:S(2)}, u32[]{:S(2)}) collective-permute-start(bf16[4,152,256]{2,1,0:T(8,128)(2,1)S(1)} %slice.43), channel_id=1, source_target_pairs={{0,192},{64,0},{128,64},{192,128},{1,193},{65,1},{129,65},{193,129... | collective-permute-start | bytes 933896 | tf_op jit(solution)/shard_map/ppermute | solution.py:346
  81.0 1.6 collective-permute-done.16
  82.6 1.7 collective-permute-done.17
  87.1 2.2 %collective-permute-start.14 = (bf16[2,304,128]{2,1,0:T(8,128)(2,1)S(1)}, bf16[2,304,128]{2,1,0:T(8,128)(2,1)S(1)}, u32[]{:S(2)}, u32[]{:S(2)}) collective-permute-start(bf16[2,304,128]{2,1,0:T(8,128)(2,1)S(1)} %slice.41), channel_id=1, source_target_pairs={{0,56},{8,0},{16,8},{24,16},{32,24},{40,32},{48,40},{56,48},{1,57}... | collective-permute-start | bytes 466952 | tf_op jit(solution)/shard_map/ppermute | solution.py:346
  89.2 3.9 %collective-permute-done.14.refs_8_ = bf16[2,304,128]{2,1,0:T(8,128)(2,1)S(1)} collective-permute-done((bf16[2,304,128]{2,1,0:T(8,128)(2,1)S(1)}, bf16[2,304,128]{2,1,0:T(8,128)(2,1)S(1)}, u32[]{:S(2)}, u32[]{:S(2)}) %collective-permute-start.14) | collective-permute-done | bytes 155680 | tf_op jit(solution)/shard_map/ppermute | solution.py:346
  93.1 1.8 collective-permute-done.13.refs_7_
  95.6 4.6 %project.1 = (f32[128,288]{1,0:T(8,128)}, f32[128,288]{1,0:T(8,128)}) custom-call(s32[2]{0:T(128)} %pad_add_fusion.core_ref.where_ref, bf16[128,8192]{1,0:T(8,128)(2,1)} %get-tuple-element.29.xc_ref, bf16[128,4096]{1,0:T(8,128)(2,1)} %collective-permute-done.12.lent_ref, bf16[4,304,128]{2,1,0:T(8,128)(2,1)} %copy-done.2, bf16[4,304,128]{2,1,0:T(8,128)(2,1)} %copy-done.4, ...), custom_call_target="tpu_custom_call" | custom-call | tf_op jit(solution)/shard_map/project/pallas_call | solution.py:104
  100.3 1.6 collective-permute-done.15.other_ref
  102.6 3.0 %norm.1 = (bf16[128,256]{1,0:T(8,128)(2,1)}, f32[4096,128]{1,0:T(8,128)}) custom-call(f32[128,288]{1,0:T(8,128)} %get-tuple-element.33.own_ref, f32[128,288]{1,0:T(8,128)} %copy-done.5, f32[1,256]{1,0:T(1,128)} %bitcast.27), custom_call_target="tpu_custom_call" | custom-call | tf_op jit(solution)/shard_map/norm/pallas_call | solution.py:126
  105.6 29.2 %scan.1 = (f32[8,1024,128]{2,1,0:T(8,128)}, f32[8,1024,128]{2,1,0:T(8,128)}, f32[8,128,128]{2,1,0:T(8,128)}, bf16[32,40,128]{2,1,0:T(8,128)(2,1)}) custom-call(s32[2]{0:T(128)} %pad_add_fusion.core_ref.where_ref, bf16[128,256]{1,0:T(8,128)(2,1)} %get-tuple-element.35.normed_ref, bf16[128,8192]{1,0:T(8,128)(2,1)} %get-tuple-element.29.xc_ref, ...), custom_call_target="tpu_custom_call" | custom-call | tf_op jit(solution)/shard_map/scan/pallas_call | solution.py:237
  134.8 25.3 %all_to_all.15.ends_ref = bf16[32,40,128]{2,1,0:T(8,128)(2,1)} all-to-all(bf16[32,40,128]{2,1,0:T(8,128)(2,1)} %get-tuple-element.42), channel_id=1, replica_groups=mesh['y'=4,'z'=8,'x'=4,'core'=2] {'y','z'}, dimensions={0} | all-to-all | bytes 655360 | tf_op jit(solution)/shard_map/all_to_all | solution.py:395
  160.1 1.8 link.1
  161.9 16.8 %all_to_all.16.start_ref = bf16[32,32,128]{2,1,0:T(8,128)(2,1)} all-to-all(bf16[32,32,128]{2,1,0:T(8,128)(2,1)} %link.1), channel_id=1, replica_groups=mesh['y'=4,'z'=8,'x'=4,'core'=2] {'y','z'}, dimensions={0} | all-to-all | bytes 524288 | tf_op jit(solution)/shard_map/all_to_all | solution.py:396
  178.7 18.7 %close.1 = bf16[128,8192]{1,0:T(8,128)(2,1)} custom-call(f32[8,1024,128]{2,1,0:T(8,128)} %get-tuple-element.39.step_ref, f32[8,1024,128]{2,1,0:T(8,128)} %get-tuple-element.40.y_ref, f32[8,128,128]{2,1,0:T(8,128)} %get-tuple-element.41.rate_ref, bf16[32,32,128]{2,1,0:T(8,128)(2,1)} %all_to_all.16.start_ref, f32[4096,128]{1,0:T(8,128)} %get-tuple-element.38.bc_ref.c_ref, ...), custom_call_target="tpu_custom_call" | custom-call | tf_op jit(solution)/shard_map/close/pallas_call | solution.py:306
  (80 shorter events, 21.8 us)
Async XLA Ops:
  1.6 8.9 %collective-permute-start.1 = (bf16[304,128]{1,0:T(8,128)(2,1)S(1)}, bf16[304,128]{1,0:T(8,128)(2,1)S(1)}, u32[]{:S(2)}, u32[]{:S(2)}) collective-permute-start(bf16[304,128]{1,0:T(8,128)(2,1)S(1)} %pad_maximum_fusion), channel_id=1, source_target_pairs={{0,128},{64,192},{128,0},{192,64},{1,129},{65,193},{129,1},{193,65... | collective-permute-start | bytes 233480 | tf_op jit(solution)/shard_map/ppermute | solution.py:346
  4.8 5.6 %collective-permute-start = (bf16[304,128]{1,0:T(8,128)(2,1)S(1)}, bf16[304,128]{1,0:T(8,128)(2,1)S(1)}, u32[]{:S(2)}, u32[]{:S(2)}) collective-permute-start(bf16[304,128]{1,0:T(8,128)(2,1)S(1)} %pad_maximum_fusion), channel_id=1, source_target_pairs={{0,64},{64,128},{128,192},{192,0},{1,65},{65,129},{129,193},{193,1... | collective-permute-start | bytes 233480 | tf_op jit(solution)/shard_map/ppermute | solution.py:346
  5.5 5.0 %collective-permute-start.2 = (bf16[304,128]{1,0:T(8,128)(2,1)S(1)}, bf16[304,128]{1,0:T(8,128)(2,1)S(1)}, u32[]{:S(2)}, u32[]{:S(2)}) collective-permute-start(bf16[304,128]{1,0:T(8,128)(2,1)S(1)} %pad_maximum_fusion), channel_id=1, source_target_pairs={{0,192},{64,0},{128,64},{192,128},{1,193},{65,1},{129,65},{193,129... | collective-permute-start | bytes 233480 | tf_op jit(solution)/shard_map/ppermute | solution.py:346
  10.5 51.1 %copy-start.2 = (bf16[4,304,128]{2,1,0:T(8,128)(2,1)}, bf16[4,304,128]{2,1,0:T(8,128)(2,1)S(1)}, u32[]{:S(2)}) copy-start(bf16[4,304,128]{2,1,0:T(8,128)(2,1)S(1)} %bitcast_dynamic-update-slice_fusion.5.refs_0_) | copy-start | bytes 933892
  11.5 43.5 %all-to-all-start = ((bf16[8,184,256]{2,1,0:T(8,128)(2,1)}), bf16[8,184,256]{2,1,0:T(8,128)(2,1)S(1)}, u32[]{:S(2)}, u32[]{:S(2)}) async-start(bf16[8,184,256]{2,1,0:T(8,128)(2,1)} %broadcast_in_dim.57), calls=%async_computation | async-start | bytes 1507328 | tf_op jit(solution)/shard_map/all_to_all | solution.py:327
  20.1 23.7 %collective-permute-start.5 = (bf16[4,304,128]{2,1,0:T(8,128)(2,1)S(1)}, bf16[4,304,128]{2,1,0:T(8,128)(2,1)S(1)}, u32[]{:S(2)}, u32[]{:S(2)}) collective-permute-start(bf16[4,304,128]{2,1,0:T(8,128)(2,1)S(1)} %bitcast_dynamic-update-slice_fusion.5.refs_0_), channel_id=1, source_target_pairs={{0,56},{8,0},{16,8},{24,16},{32,24},{40,32},{48,40},{56,48},{1,57}... | collective-permute-start | bytes 933896 | tf_op jit(solution)/shard_map/ppermute | solution.py:346
  20.1 24.3 %collective-permute-start.3 = (bf16[4,304,128]{2,1,0:T(8,128)(2,1)S(1)}, bf16[4,304,128]{2,1,0:T(8,128)(2,1)S(1)}, u32[]{:S(2)}, u32[]{:S(2)}) collective-permute-start(bf16[4,304,128]{2,1,0:T(8,128)(2,1)S(1)} %bitcast_dynamic-update-slice_fusion.5.refs_0_), channel_id=1, source_target_pairs={{0,8},{8,16},{16,24},{24,32},{32,40},{40,48},{48,56},{56,0},{1,9},... | collective-permute-start | bytes 933896 | tf_op jit(solution)/shard_map/ppermute | solution.py:346
  43.8 17.8 %copy-start.3 = (bf16[4,304,128]{2,1,0:T(8,128)(2,1)}, bf16[4,304,128]{2,1,0:T(8,128)(2,1)S(1)}, u32[]{:S(2)}) copy-start(bf16[4,304,128]{2,1,0:T(8,128)(2,1)S(1)} %collective-permute-done.5.refs_2_) | copy-start | bytes 933892
  43.8 11.2 %collective-permute-start.6 = (bf16[4,304,128]{2,1,0:T(8,128)(2,1)S(1)}, bf16[4,304,128]{2,1,0:T(8,128)(2,1)}, u32[]{:S(2)}, u32[]{:S(2)}) collective-permute-start(bf16[4,304,128]{2,1,0:T(8,128)(2,1)S(1)} %collective-permute-done.5.refs_2_), channel_id=1, source_target_pairs={{0,56},{8,0},{16,8},{24,16},{32,24},{40,32},{48,40},{56,48},{1,57}... | collective-permute-start | bytes 933896 | tf_op jit(solution)/shard_map/ppermute | solution.py:346
  44.4 17.2 %copy-start.4 = (bf16[4,304,128]{2,1,0:T(8,128)(2,1)}, bf16[4,304,128]{2,1,0:T(8,128)(2,1)S(1)}, u32[]{:S(2)}) copy-start(bf16[4,304,128]{2,1,0:T(8,128)(2,1)S(1)} %collective-permute-done.3.refs_1_) | copy-start | bytes 933892
  44.4 10.7 %collective-permute-start.4 = (bf16[4,304,128]{2,1,0:T(8,128)(2,1)S(1)}, bf16[4,304,128]{2,1,0:T(8,128)(2,1)}, u32[]{:S(2)}, u32[]{:S(2)}) collective-permute-start(bf16[4,304,128]{2,1,0:T(8,128)(2,1)S(1)} %collective-permute-done.3.refs_1_), channel_id=1, source_target_pairs={{0,8},{8,16},{16,24},{24,32},{32,40},{40,48},{48,56},{56,0},{1,9},... | collective-permute-start | bytes 933896 | tf_op jit(solution)/shard_map/ppermute | solution.py:346
  46.8 8.3 %collective-permute-start.7 = (bf16[8,8192]{1,0:T(8,128)(2,1)S(1)}, bf16[8,8192]{1,0:T(8,128)(2,1)S(1)}, u32[]{:S(2)}, u32[]{:S(2)}) collective-permute-start(bf16[8,8192]{1,0:T(8,128)(2,1)S(1)} %slice.37), channel_id=1, source_target_pairs={{0,8},{8,16},{16,24},{24,32},{32,40},{40,48},{48,56},{56,64},{64,7... | collective-permute-start | bytes 393224 | tf_op jit(solution)/shard_map/ppermute | solution.py:372
  56.0 14.1 %collective-permute-start.11 = (bf16[8,152,256]{2,1,0:T(8,128)(2,1)}, bf16[8,152,256]{2,1,0:T(8,128)(2,1)}, u32[]{:S(2)}, u32[]{:S(2)}) collective-permute-start(bf16[8,152,256]{2,1,0:T(8,128)(2,1)} %slice.39), channel_id=1, source_target_pairs={{0,192},{64,0},{128,64},{192,128},{1,193},{65,1},{129,65},{193,129... | collective-permute-start | bytes 1867784 | tf_op jit(solution)/shard_map/ppermute | solution.py:346
  58.3 15.0 %collective-permute-start.10 = (bf16[8,152,256]{2,1,0:T(8,128)(2,1)}, bf16[8,152,256]{2,1,0:T(8,128)(2,1)}, u32[]{:S(2)}, u32[]{:S(2)}) collective-permute-start(bf16[8,152,256]{2,1,0:T(8,128)(2,1)} %slice.39), channel_id=1, source_target_pairs={{0,64},{64,128},{128,192},{192,0},{1,65},{65,129},{129,193},{193,1... | collective-permute-start | bytes 1867784 | tf_op jit(solution)/shard_map/ppermute | solution.py:346
  58.9 10.9 %collective-permute-start.8 = (bf16[4,304,128]{2,1,0:T(8,128)(2,1)}, bf16[4,304,128]{2,1,0:T(8,128)(2,1)}, u32[]{:S(2)}, u32[]{:S(2)}) collective-permute-start(bf16[4,304,128]{2,1,0:T(8,128)(2,1)} %collective-permute-done.4.refs_3_), channel_id=1, source_target_pairs={{0,8},{8,16},{16,24},{24,32},{32,40},{40,48},{48,56},{56,0},{1,9},... | collective-permute-start | bytes 933896 | tf_op jit(solution)/shard_map/ppermute | solution.py:346
  60.4 9.5 %collective-permute-start.9 = (bf16[4,304,128]{2,1,0:T(8,128)(2,1)}, bf16[4,304,128]{2,1,0:T(8,128)(2,1)}, u32[]{:S(2)}, u32[]{:S(2)}) collective-permute-start(bf16[4,304,128]{2,1,0:T(8,128)(2,1)} %collective-permute-done.6.refs_4_), channel_id=1, source_target_pairs={{0,56},{8,0},{16,8},{24,16},{32,24},{40,32},{48,40},{56,48},{1,57}... | collective-permute-start | bytes 933896 | tf_op jit(solution)/shard_map/ppermute | solution.py:346
  74.4 8.2 %collective-permute-start.16 = (bf16[4,152,256]{2,1,0:T(8,128)(2,1)S(1)}, bf16[4,152,256]{2,1,0:T(8,128)(2,1)S(1)}, u32[]{:S(2)}, u32[]{:S(2)}) collective-permute-start(bf16[4,152,256]{2,1,0:T(8,128)(2,1)S(1)} %slice.42), channel_id=1, source_target_pairs={{0,64},{64,128},{128,192},{192,0},{1,65},{65,129},{129,193},{193,1... | collective-permute-start | bytes 933896 | tf_op jit(solution)/shard_map/ppermute | solution.py:346
  76.6 7.7 %collective-permute-start.17 = (bf16[4,152,256]{2,1,0:T(8,128)(2,1)S(1)}, bf16[4,152,256]{2,1,0:T(8,128)(2,1)S(1)}, u32[]{:S(2)}, u32[]{:S(2)}) collective-permute-start(bf16[4,152,256]{2,1,0:T(8,128)(2,1)S(1)} %slice.43), channel_id=1, source_target_pairs={{0,192},{64,0},{128,64},{192,128},{1,193},{65,1},{129,65},{193,129... | collective-permute-start | bytes 933896 | tf_op jit(solution)/shard_map/ppermute | solution.py:346
  84.4 15.8 %copy-start.1 = (bf16[4,8,152,256]{3,2,1,0:T(8,128)(2,1)}, bf16[4,8,152,256]{3,2,1,0:T(8,128)(2,1)S(1)}, u32[]{:S(2)}) copy-start(bf16[4,8,152,256]{3,2,1,0:T(8,128)(2,1)S(1)} %bitcast_dynamic-update-slice_fusion.3.own_ref) | copy-start | bytes 7471108
  84.4 21.2 %collective-permute-start.18 = (bf16[4,8,152,256]{3,2,1,0:T(8,128)(2,1)S(1)}, bf16[4,8,152,256]{3,2,1,0:T(8,128)(2,1)}, u32[]{:S(2)}, u32[]{:S(2)}) collective-permute-start(bf16[4,8,152,256]{3,2,1,0:T(8,128)(2,1)S(1)} %bitcast_dynamic-update-slice_fusion.3.own_ref), channel_id=1, source_target_pairs={{0,1},{1,0},{2,3},{3,2},{4,5},{5,4},{6,7},{7,6},{8,9},{9,8},{10,11... | collective-permute-start | bytes 7471112 | tf_op jit(solution)/shard_map/ppermute | solution.py:391
  84.7 10.3 %collective-permute-start.12 = (bf16[128,4096]{1,0:T(8,128)(2,1)S(1)}, bf16[128,4096]{1,0:T(8,128)(2,1)}, u32[]{:S(2)}, u32[]{:S(2)}) collective-permute-start(bf16[128,4096]{1,0:T(8,128)(2,1)S(1)} %copy-done.9), channel_id=1, source_target_pairs={{0,1},{1,0},{2,3},{3,2},{4,5},{5,4},{6,7},{7,6},{8,9},{9,8},{10,11... | collective-permute-start | bytes 3145736 | tf_op jit(solution)/shard_map/ppermute | solution.py:386
  87.1 6.1 %collective-permute-start.14 = (bf16[2,304,128]{2,1,0:T(8,128)(2,1)S(1)}, bf16[2,304,128]{2,1,0:T(8,128)(2,1)S(1)}, u32[]{:S(2)}, u32[]{:S(2)}) collective-permute-start(bf16[2,304,128]{2,1,0:T(8,128)(2,1)S(1)} %slice.41), channel_id=1, source_target_pairs={{0,56},{8,0},{16,8},{24,16},{32,24},{40,32},{48,40},{56,48},{1,57}... | collective-permute-start | bytes 466952 | tf_op jit(solution)/shard_map/ppermute | solution.py:346
  89.2 5.7 %collective-permute-start.13 = (bf16[2,304,128]{2,1,0:T(8,128)(2,1)S(1)}, bf16[2,304,128]{2,1,0:T(8,128)(2,1)S(1)}, u32[]{:S(2)}, u32[]{:S(2)}) collective-permute-start(bf16[2,304,128]{2,1,0:T(8,128)(2,1)S(1)} %slice.40), channel_id=1, source_target_pairs={{0,8},{8,16},{16,24},{24,32},{32,40},{40,48},{48,56},{56,0},{1,9},... | collective-permute-start | bytes 466952 | tf_op jit(solution)/shard_map/ppermute | solution.py:346
  100.2 1.7 collective-permute-start.15
  (6 other events, 22.6 us)

commit v6 on v5

--- a/solution.py
+++ b/solution.py
@@ -193,7 +193,7 @@
         return total + now, tuple(fresh)
 
     zero = jnp.zeros((8, 128), F32)
-    total, state = lax.fori_loop(0, rows, advance, (zero, (zero,) * 16), unroll=4)
+    total, state = lax.fori_loop(0, rows, advance, (zero, (zero,) * 16), unroll=8)
     for n in range(16):
         h_scr[8 * n : 8 * n + 8, :] = state[n]
     high = total.astype(BF16).astype(F32)
@@ -291,7 +291,7 @@
         y_scr[pl.ds(at, 8), :] = even + odd
         return total
 
-    lax.fori_loop(0, rows, advance, jnp.zeros((8, 128), F32), unroll=4)
+    lax.fori_loop(0, rows, advance, jnp.zeros((8, 128), F32), unroll=8)
     for j in range(8):
         for i in range(rows // 16):
             low = y_scr[pl.ds(128 * i + j, 8, stride=8), :]
@@ -378,19 +378,20 @@
     d_msg = jnp.concatenate([pack_d(core, dt_weight, dt_bias, a_log, skip), taps], 0)
     d_part = from_everyone(d_msg, "z").reshape(8, 184, SHARD)
     x2 = both_ways(x1, "z")
-    *x2, d_part, prior = together(*x2, d_part, prior)
     d0 = d_part[:, :152]
     d1 = both_ways((d0, d0), "y")
     x3 = both_ways(x2, "z")
     xc, lend = conv(where, conv_input, prior, d_part[:, 152:].reshape(8, 4, 8, SHARD))
+    *x3, xc, lend = together(*x3, xc, lend)
+    up, down = d1
     lent = lax.ppermute(lend, "core", swap)
-    *x3, xc, up, down = together(*x3, xc, *d1)
     x4 = both_ways((x3[0][:2], x3[1][2:]), "z")
     d2 = both_ways((up[:4], down[4:]), "y")
     d_own = placed([d0, up, down, *d2], [(0, 0), (-1, 0), (1, 0), (2, 0), (2, 4)], "y")
     d_oth = lax.ppermute(d_own, "core", swap)
     own, other = project(where, xc, lent, [x0, *x1, *x2, *x3, *x4])
-    normed, bc = norm(own, lax.ppermute(other, "core", swap), dt_gain[None, :])
+    other = lax.ppermute(other, "core", swap)
+    normed, bc = norm(own, other, dt_gain[None, :])
     step, y, rate, ends = scan(where, normed, xc, d_own, d_oth, bc)
     ends = lax.all_to_all(ends, SEQ, split_axis=0, concat_axis=0, tiled=True)
     start = lax.all_to_all(link(ends, a_log), SEQ, split_axis=0, concat_axis=0, tiled=True)

time: 198 us -> 210 us (1.061)
  blocking collectives: 42.1 us -> 70.6 us
  starting transfers between devices: 34 us -> 25.5 us
  waiting for transfers between devices: 40 us -> 33.6 us
  Pallas kernels: 65.2 us -> 62 us
    all_to_all x0 -> x1, blocking collectives: none -> 28.4 us  [from_everyone(): return lax.all_to_all(copies, axis, split_axis=0, concat_axis=0, tiled=True)]
    all_to_all x1 -> x0, starting transfers between devices: 8.57 us -> none  [from_everyone(): return lax.all_to_all(copies, axis, split_axis=0, concat_axis=0, tiled=True)]
    ppermute x1, waiting for transfers between devices: 4.16 us -> 0.01 us  [body(): lax.ppermute(conv_input[conv_input.shape[0] - 8:], SEQ, [(i, i + 1) for i...]
    ppermute x15, waiting for transfers between devices: 34.2 us -> 32 us  [shifted(): lax.ppermute(block, axis, [(i, (i + by) % count) for i in range(count)])]
  transfers between devices with their start and end apart: 20 -> 19, of which waited for: 9 -> 9; matrix products, arithmetic and copies ran while one was open for 5% -> 6% of each run, Pallas kernels for 8% -> 7%
where the time goes in v6:
time: 210 us; the launch traced here: 209 us
  blocking collectives  70.6 us (34%)
  Pallas kernels  62 us (30%)
  waiting for transfers between devices  33.6 us (16%)
  starting transfers between devices  25.5 us (12%)
  local copies, waits for them, and re-layouts  14 us (7%)
  other arithmetic  2.83 us (1%)
    ppermute x15, waiting for transfers between devices, shifted(): lax.ppermute(block, axis, [(i, (i + by) % count) for i in range(count)])  32 us
    all_to_all x1, blocking collectives, from_everyone(): return lax.all_to_all(copies, axis, split_axis=0, concat_axis=0, tiled=True)  28.4 us
    pallas_call x1, Pallas kernels, scan(): pl.pallas_call(scan_kernel, grid_spec=grid_spec, out_shape=[jax.ShapeDtyp...  27.3 us
    all_to_all x1, blocking collectives, body(): ends = lax.all_to_all(ends, SEQ, split_axis=0, concat_axis=0, tiled=True)  25.4 us
    ppermute x15, starting transfers between devices, shifted(): lax.ppermute(block, axis, [(i, (i + by) % count) for i in range(count)])  21.8 us
    pallas_call x1, Pallas kernels, close(): pl.pallas_call(close_kernel, grid=(inner // BLK,), in_specs=[pl.BlockSpec...  17.3 us
    all_to_all x1, blocking collectives, body(): lax.all_to_all(link(ends, a_log), SEQ, split_axis=0, concat_axis=0, tiled...  16.8 us
    pallas_call x1, Pallas kernels, conv(): pl.pallas_call(conv_kernel, grid=(inner // BLK,), in_specs=[pl.BlockSpec(...  7.91 us
  transfers between devices with their start and end apart: 19, of which 9 were waited for; matrix products, arithmetic and copies ran while one was open for 6% of the time, Pallas kernels for 7%

profile of v6, /device:TPU:32, one launch (start us, length us, event | category | flops | bytes accessed | tf_op | source)
XLA Modules:
  0.0 208.7 jit_solution(8550353765464241078)
XLA Ops:
  1.6 3.3 %collective-permute-start.1 = (bf16[304,128]{1,0:T(8,128)(2,1)S(1)}, bf16[304,128]{1,0:T(8,128)(2,1)S(1)}, u32[]{:S(2)}, u32[]{:S(2)}) collective-permute-start(bf16[304,128]{1,0:T(8,128)(2,1)S(1)} %pad_maximum_fusion), channel_id=1, source_target_pairs={{0,128},{64,192},{128,0},{192,64},{1,129},{65,193},{129,1},{193,65... | collective-permute-start | bytes 233480 | tf_op jit(solution)/shard_map/ppermute | solution.py:346
  5.5 2.6 %collective-permute-start.2 = (bf16[304,128]{1,0:T(8,128)(2,1)S(1)}, bf16[304,128]{1,0:T(8,128)(2,1)S(1)}, u32[]{:S(2)}, u32[]{:S(2)}) collective-permute-start(bf16[304,128]{1,0:T(8,128)(2,1)S(1)} %pad_maximum_fusion), channel_id=1, source_target_pairs={{0,192},{64,0},{128,64},{192,128},{1,193},{65,1},{129,65},{193,129... | collective-permute-start | bytes 233480 | tf_op jit(solution)/shard_map/ppermute | solution.py:346
  11.4 28.4 %all_to_all.15 = bf16[8,184,256]{2,1,0:T(8,128)(2,1)S(1)} all-to-all(bf16[8,184,256]{2,1,0:T(8,128)(2,1)S(1)} %broadcast_in_dim.57), channel_id=1, replica_groups=mesh['y'=4,'z'=8,'x'=4,'core'=2] {'z'}, dimensions={0} | all-to-all | bytes 1507328 | tf_op jit(solution)/shard_map/all_to_all | solution.py:327
  41.5 2.4 %collective-permute-start.15 = (bf16[8,152,256]{2,1,0:T(8,128)(2,1)}, bf16[8,152,256]{2,1,0:T(8,128)(2,1)}, u32[]{:S(2)}, u32[]{:S(2)}) collective-permute-start(bf16[8,152,256]{2,1,0:T(8,128)(2,1)} %slice.49), channel_id=1, source_target_pairs={{0,192},{64,0},{128,64},{192,128},{1,193},{65,1},{129,65},{193,129... | collective-permute-start | bytes 1867784 | tf_op jit(solution)/shard_map/ppermute | solution.py:346
  44.2 11.2 %collective-permute-done.14 = bf16[8,152,256]{2,1,0:T(8,128)(2,1)} collective-permute-done((bf16[8,152,256]{2,1,0:T(8,128)(2,1)}, bf16[8,152,256]{2,1,0:T(8,128)(2,1)}, u32[]{:S(2)}, u32[]{:S(2)}) %collective-permute-start.14) | collective-permute-done | bytes 622624 | tf_op jit(solution)/shard_map/ppermute | solution.py:346
  57.4 3.3 %collective-permute-start.17 = (bf16[4,152,256]{2,1,0:T(8,128)(2,1)S(1)}, bf16[4,152,256]{2,1,0:T(8,128)(2,1)S(1)}, u32[]{:S(2)}, u32[]{:S(2)}) collective-permute-start(bf16[4,152,256]{2,1,0:T(8,128)(2,1)S(1)} %slice.51), channel_id=1, source_target_pairs={{0,192},{64,0},{128,64},{192,128},{1,193},{65,1},{129,65},{193,129... | collective-permute-start | bytes 933896 | tf_op jit(solution)/shard_map/ppermute | solution.py:346
  63.0 1.6 collective-permute-done.16
  65.3 1.6 collective-permute-start.6
  67.4 7.8 %collective-permute-done.6.refs_2_ = bf16[4,304,128]{2,1,0:T(8,128)(2,1)} collective-permute-done((bf16[4,304,128]{2,1,0:T(8,128)(2,1)S(1)}, bf16[4,304,128]{2,1,0:T(8,128)(2,1)}, u32[]{:S(2)}, u32[]{:S(2)}) %collective-permute-start.6) | collective-permute-done | bytes 311328 | tf_op jit(solution)/shard_map/ppermute | solution.py:346
  77.2 1.6 slice.35
  78.7 3.5 %collective-permute-start.9 = (bf16[8,8192]{1,0:T(8,128)(2,1)}, bf16[8,8192]{1,0:T(8,128)(2,1)S(1)}, u32[]{:S(2)}, u32[]{:S(2)}) collective-permute-start(bf16[8,8192]{1,0:T(8,128)(2,1)} %slice.35), channel_id=1, source_target_pairs={{0,8},{8,16},{16,24},{24,32},{32,40},{40,48},{48,56},{56,64},{64,7... | collective-permute-start | bytes 393224 | tf_op jit(solution)/shard_map/ppermute | solution.py:372
  82.2 2.1 collective-permute-done.7.refs_4_
  89.4 7.9 %conv.1 = (bf16[128,8192]{1,0:T(8,128)(2,1)}, bf16[128,4096]{1,0:T(8,128)(2,1)}) custom-call(s32[2]{0:T(128)} %pad_add_fusion.core_ref.where_ref, bf16[128,8192]{1,0:T(8,128)(2,1)} %ci_ref.1, bf16[8,8192]{1,0:T(8,128)(2,1)} %copy-done.7, bf16[8,4,8,256]{3,2,1,0:T(8,128)(2,1)} %slice_bitcast_fusion.par_ref), custom_call_target="tpu_custom_call" | custom-call | tf_op jit(solution)/shard_map/conv/pallas_call | solution.py:49
  99.3 2.6 %collective-permute-start.12 = (bf16[2,304,128]{2,1,0:T(8,128)(2,1)S(1)}, bf16[2,304,128]{2,1,0:T(8,128)(2,1)S(1)}, u32[]{:S(2)}, u32[]{:S(2)}) collective-permute-start(bf16[2,304,128]{2,1,0:T(8,128)(2,1)S(1)} %slice.40), channel_id=1, source_target_pairs={{0,56},{8,0},{16,8},{24,16},{32,24},{40,32},{48,40},{56,48},{1,57}... | collective-permute-start | bytes 466952 | tf_op jit(solution)/shard_map/ppermute | solution.py:346
  101.8 4.5 %collective-permute-done.12.refs_8_ = bf16[2,304,128]{2,1,0:T(8,128)(2,1)S(1)} collective-permute-done((bf16[2,304,128]{2,1,0:T(8,128)(2,1)S(1)}, bf16[2,304,128]{2,1,0:T(8,128)(2,1)S(1)}, u32[]{:S(2)}, u32[]{:S(2)}) %collective-permute-start.12) | collective-permute-done | bytes 155680 | tf_op jit(solution)/shard_map/ppermute | solution.py:346
  106.3 3.1 %collective-permute-done.11.refs_7_ = bf16[2,304,128]{2,1,0:T(8,128)(2,1)S(1)} collective-permute-done((bf16[2,304,128]{2,1,0:T(8,128)(2,1)S(1)}, bf16[2,304,128]{2,1,0:T(8,128)(2,1)S(1)}, u32[]{:S(2)}, u32[]{:S(2)}) %collective-permute-start.11) | collective-permute-done | bytes 155680 | tf_op jit(solution)/shard_map/ppermute | solution.py:346
  110.1 4.6 %project.1 = (f32[128,288]{1,0:T(8,128)}, f32[128,288]{1,0:T(8,128)}) custom-call(s32[2]{0:T(128)} %pad_add_fusion.core_ref.where_ref, bf16[128,8192]{1,0:T(8,128)(2,1)} %get-tuple-element.21.xc_ref, bf16[128,4096]{1,0:T(8,128)(2,1)} %collective-permute-done.10.lent_ref, bf16[4,304,128]{2,1,0:T(8,128)(2,1)} %copy-done.2, ...), custom_call_target="tpu_custom_call" | custom-call | tf_op jit(solution)/shard_map/project/pallas_call | solution.py:104
  114.8 1.6 collective-permute-done.13.other_ref
  117.1 3.0 %norm.1 = (bf16[128,256]{1,0:T(8,128)(2,1)}, f32[4096,128]{1,0:T(8,128)}) custom-call(f32[128,288]{1,0:T(8,128)} %get-tuple-element.25.own_ref, f32[128,288]{1,0:T(8,128)} %copy-done.4, f32[1,256]{1,0:T(1,128)} %bitcast.27), custom_call_target="tpu_custom_call" | custom-call | tf_op jit(solution)/shard_map/norm/pallas_call | solution.py:126
  120.1 27.3 %scan.1 = (f32[8,1024,128]{2,1,0:T(8,128)}, f32[8,1024,128]{2,1,0:T(8,128)}, f32[8,128,128]{2,1,0:T(8,128)}, bf16[32,40,128]{2,1,0:T(8,128)(2,1)}) custom-call(s32[2]{0:T(128)} %pad_add_fusion.core_ref.where_ref, bf16[128,256]{1,0:T(8,128)(2,1)} %get-tuple-element.27.normed_ref, bf16[128,8192]{1,0:T(8,128)(2,1)} %get-tuple-element.21.xc_ref, ...), custom_call_target="tpu_custom_call" | custom-call | tf_op jit(solution)/shard_map/scan/pallas_call | solution.py:237
  147.4 25.4 %all_to_all.16.ends_ref = bf16[32,40,128]{2,1,0:T(8,128)(2,1)} all-to-all(bf16[32,40,128]{2,1,0:T(8,128)(2,1)} %get-tuple-element.32), channel_id=1, replica_groups=mesh['y'=4,'z'=8,'x'=4,'core'=2] {'y','z'}, dimensions={0} | all-to-all | bytes 655360 | tf_op jit(solution)/shard_map/all_to_all | solution.py:396
  172.8 1.8 link.1
  174.6 16.8 %all_to_all.17.start_ref = bf16[32,32,128]{2,1,0:T(8,128)(2,1)} all-to-all(bf16[32,32,128]{2,1,0:T(8,128)(2,1)} %link.1), channel_id=1, replica_groups=mesh['y'=4,'z'=8,'x'=4,'core'=2] {'y','z'}, dimensions={0} | all-to-all | bytes 524288 | tf_op jit(solution)/shard_map/all_to_all | solution.py:397
  191.4 17.3 %close.1 = bf16[128,8192]{1,0:T(8,128)(2,1)} custom-call(f32[8,1024,128]{2,1,0:T(8,128)} %get-tuple-element.29.step_ref, f32[8,1024,128]{2,1,0:T(8,128)} %get-tuple-element.30.y_ref, f32[8,128,128]{2,1,0:T(8,128)} %get-tuple-element.31.rate_ref, bf16[32,32,128]{2,1,0:T(8,128)(2,1)} %all_to_all.17.start_ref, f32[4096,128]{1,0:T(8,128)} %get-tuple-element.28.bc_ref.c_ref, ...), custom_call_target="tpu_custom_call" | custom-call | tf_op jit(solution)/shard_map/close/pallas_call | solution.py:306
  (75 shorter events, 23.4 us)
Async XLA Ops:
  0.0 1.5 copy-start
  1.6 8.9 %collective-permute-start.1 = (bf16[304,128]{1,0:T(8,128)(2,1)S(1)}, bf16[304,128]{1,0:T(8,128)(2,1)S(1)}, u32[]{:S(2)}, u32[]{:S(2)}) collective-permute-start(bf16[304,128]{1,0:T(8,128)(2,1)S(1)} %pad_maximum_fusion), channel_id=1, source_target_pairs={{0,128},{64,192},{128,0},{192,64},{1,129},{65,193},{129,1},{193,65... | collective-permute-start | bytes 233480 | tf_op jit(solution)/shard_map/ppermute | solution.py:346
  4.8 5.6 %collective-permute-start = (bf16[304,128]{1,0:T(8,128)(2,1)S(1)}, bf16[304,128]{1,0:T(8,128)(2,1)S(1)}, u32[]{:S(2)}, u32[]{:S(2)}) collective-permute-start(bf16[304,128]{1,0:T(8,128)(2,1)S(1)} %pad_maximum_fusion), channel_id=1, source_target_pairs={{0,64},{64,128},{128,192},{192,0},{1,65},{65,129},{129,193},{193,1... | collective-permute-start | bytes 233480 | tf_op jit(solution)/shard_map/ppermute | solution.py:346
  5.5 5.0 %collective-permute-start.2 = (bf16[304,128]{1,0:T(8,128)(2,1)S(1)}, bf16[304,128]{1,0:T(8,128)(2,1)S(1)}, u32[]{:S(2)}, u32[]{:S(2)}) collective-permute-start(bf16[304,128]{1,0:T(8,128)(2,1)S(1)} %pad_maximum_fusion), channel_id=1, source_target_pairs={{0,192},{64,0},{128,64},{192,128},{1,193},{65,1},{129,65},{193,129... | collective-permute-start | bytes 233480 | tf_op jit(solution)/shard_map/ppermute | solution.py:346
  10.5 0.7 copy-start.2
  40.7 14.7 %collective-permute-start.14 = (bf16[8,152,256]{2,1,0:T(8,128)(2,1)}, bf16[8,152,256]{2,1,0:T(8,128)(2,1)}, u32[]{:S(2)}, u32[]{:S(2)}) collective-permute-start(bf16[8,152,256]{2,1,0:T(8,128)(2,1)} %slice.49), channel_id=1, source_target_pairs={{0,64},{64,128},{128,192},{192,0},{1,65},{65,129},{129,193},{193,1... | collective-permute-start | bytes 1867784 | tf_op jit(solution)/shard_map/ppermute | solution.py:346
  41.5 14.9 %collective-permute-start.15 = (bf16[8,152,256]{2,1,0:T(8,128)(2,1)}, bf16[8,152,256]{2,1,0:T(8,128)(2,1)}, u32[]{:S(2)}, u32[]{:S(2)}) collective-permute-start(bf16[8,152,256]{2,1,0:T(8,128)(2,1)} %slice.49), channel_id=1, source_target_pairs={{0,192},{64,0},{128,64},{192,128},{1,193},{65,1},{129,65},{193,129... | collective-permute-start | bytes 1867784 | tf_op jit(solution)/shard_map/ppermute | solution.py:346
  44.1 21.1 %copy-start.3 = (bf16[4,304,128]{2,1,0:T(8,128)(2,1)S(1)}, bf16[4,304,128]{2,1,0:T(8,128)(2,1)}, u32[]{:S(2)}) copy-start(bf16[4,304,128]{2,1,0:T(8,128)(2,1)} %copy-done.2) | copy-start | bytes 933892
  56.3 8.2 %collective-permute-start.16 = (bf16[4,152,256]{2,1,0:T(8,128)(2,1)S(1)}, bf16[4,152,256]{2,1,0:T(8,128)(2,1)S(1)}, u32[]{:S(2)}, u32[]{:S(2)}) collective-permute-start(bf16[4,152,256]{2,1,0:T(8,128)(2,1)S(1)} %slice.50), channel_id=1, source_target_pairs={{0,64},{64,128},{128,192},{192,0},{1,65},{65,129},{129,193},{193,1... | collective-permute-start | bytes 933896 | tf_op jit(solution)/shard_map/ppermute | solution.py:346
  57.4 7.7 %collective-permute-start.17 = (bf16[4,152,256]{2,1,0:T(8,128)(2,1)S(1)}, bf16[4,152,256]{2,1,0:T(8,128)(2,1)S(1)}, u32[]{:S(2)}, u32[]{:S(2)}) collective-permute-start(bf16[4,152,256]{2,1,0:T(8,128)(2,1)S(1)} %slice.51), channel_id=1, source_target_pairs={{0,192},{64,0},{128,64},{192,128},{1,193},{65,1},{129,65},{193,129... | collective-permute-start | bytes 933896 | tf_op jit(solution)/shard_map/ppermute | solution.py:346
  65.2 49.5 %copy-start.1 = (bf16[4,8,152,256]{3,2,1,0:T(8,128)(2,1)}, bf16[4,8,152,256]{3,2,1,0:T(8,128)(2,1)S(1)}, u32[]{:S(2)}) copy-start(bf16[4,8,152,256]{3,2,1,0:T(8,128)(2,1)S(1)} %bitcast_dynamic-update-slice_fusion.3.own_ref) | copy-start | bytes 7471108
  65.2 54.9 %collective-permute-start.18 = (bf16[4,8,152,256]{3,2,1,0:T(8,128)(2,1)S(1)}, bf16[4,8,152,256]{3,2,1,0:T(8,128)(2,1)}, u32[]{:S(2)}, u32[]{:S(2)}) collective-permute-start(bf16[4,8,152,256]{3,2,1,0:T(8,128)(2,1)S(1)} %bitcast_dynamic-update-slice_fusion.3.own_ref), channel_id=1, source_target_pairs={{0,1},{1,0},{2,3},{3,2},{4,5},{5,4},{6,7},{7,6},{8,9},{9,8},{10,11... | collective-permute-start | bytes 7471112 | tf_op jit(solution)/shard_map/ppermute | solution.py:391
  65.3 9.9 %collective-permute-start.6 = (bf16[4,304,128]{2,1,0:T(8,128)(2,1)S(1)}, bf16[4,304,128]{2,1,0:T(8,128)(2,1)}, u32[]{:S(2)}, u32[]{:S(2)}) collective-permute-start(bf16[4,304,128]{2,1,0:T(8,128)(2,1)S(1)} %copy-done.3), channel_id=1, source_target_pairs={{0,56},{8,0},{16,8},{24,16},{32,24},{40,32},{48,40},{56,48},{1,57}... | collective-permute-start | bytes 933896 | tf_op jit(solution)/shard_map/ppermute | solution.py:346
  66.9 9.8 %collective-permute-start.3 = (bf16[4,304,128]{2,1,0:T(8,128)(2,1)S(1)}, bf16[4,304,128]{2,1,0:T(8,128)(2,1)}, u32[]{:S(2)}, u32[]{:S(2)}) collective-permute-start(bf16[4,304,128]{2,1,0:T(8,128)(2,1)S(1)} %copy-done.3), channel_id=1, source_target_pairs={{0,8},{8,16},{16,24},{24,32},{32,40},{40,48},{48,56},{56,0},{1,9},... | collective-permute-start | bytes 933896 | tf_op jit(solution)/shard_map/ppermute | solution.py:346
  75.1 9.1 %collective-permute-start.7 = (bf16[4,304,128]{2,1,0:T(8,128)(2,1)}, bf16[4,304,128]{2,1,0:T(8,128)(2,1)}, u32[]{:S(2)}, u32[]{:S(2)}) collective-permute-start(bf16[4,304,128]{2,1,0:T(8,128)(2,1)} %collective-permute-done.6.refs_2_), channel_id=1, source_target_pairs={{0,56},{8,0},{16,8},{24,16},{32,24},{40,32},{48,40},{56,48},{1,57}... | collective-permute-start | bytes 933896 | tf_op jit(solution)/shard_map/ppermute | solution.py:346
  76.7 10.3 %collective-permute-start.4 = (bf16[4,304,128]{2,1,0:T(8,128)(2,1)}, bf16[4,304,128]{2,1,0:T(8,128)(2,1)}, u32[]{:S(2)}, u32[]{:S(2)}) collective-permute-start(bf16[4,304,128]{2,1,0:T(8,128)(2,1)} %collective-permute-done.3.refs_1_), channel_id=1, source_target_pairs={{0,8},{8,16},{16,24},{24,32},{32,40},{40,48},{48,56},{56,0},{1,9},... | collective-permute-start | bytes 933896 | tf_op jit(solution)/shard_map/ppermute | solution.py:346
  78.7 10.0 %collective-permute-start.9 = (bf16[8,8192]{1,0:T(8,128)(2,1)}, bf16[8,8192]{1,0:T(8,128)(2,1)S(1)}, u32[]{:S(2)}, u32[]{:S(2)}) collective-permute-start(bf16[8,8192]{1,0:T(8,128)(2,1)} %slice.35), channel_id=1, source_target_pairs={{0,8},{8,16},{16,24},{24,32},{32,40},{40,48},{48,56},{56,64},{64,7... | collective-permute-start | bytes 393224 | tf_op jit(solution)/shard_map/ppermute | solution.py:372
  84.3 13.0 %collective-permute-start.8 = (bf16[4,304,128]{2,1,0:T(8,128)(2,1)}, bf16[4,304,128]{2,1,0:T(8,128)(2,1)}, u32[]{:S(2)}, u32[]{:S(2)}) collective-permute-start(bf16[4,304,128]{2,1,0:T(8,128)(2,1)} %collective-permute-done.7.refs_4_), channel_id=1, source_target_pairs={{0,56},{8,0},{16,8},{24,16},{32,24},{40,32},{48,40},{56,48},{1,57}... | collective-permute-start | bytes 933896 | tf_op jit(solution)/shard_map/ppermute | solution.py:346
  87.0 10.3 %collective-permute-start.5 = (bf16[4,304,128]{2,1,0:T(8,128)(2,1)}, bf16[4,304,128]{2,1,0:T(8,128)(2,1)}, u32[]{:S(2)}, u32[]{:S(2)}) collective-permute-start(bf16[4,304,128]{2,1,0:T(8,128)(2,1)} %collective-permute-done.4.refs_3_), channel_id=1, source_target_pairs={{0,8},{8,16},{16,24},{24,32},{32,40},{40,48},{48,56},{56,0},{1,9},... | collective-permute-start | bytes 933896 | tf_op jit(solution)/shard_map/ppermute | solution.py:346
  97.3 12.2 %collective-permute-start.10 = (bf16[128,4096]{1,0:T(8,128)(2,1)}, bf16[128,4096]{1,0:T(8,128)(2,1)}, u32[]{:S(2)}, u32[]{:S(2)}) collective-permute-start(bf16[128,4096]{1,0:T(8,128)(2,1)} %get-tuple-element.22), channel_id=1, source_target_pairs={{0,1},{1,0},{2,3},{3,2},{4,5},{5,4},{6,7},{7,6},{8,9},{9,8},{10,11... | collective-permute-start | bytes 3145736 | tf_op jit(solution)/shard_map/ppermute | solution.py:387
  99.3 7.1 %collective-permute-start.12 = (bf16[2,304,128]{2,1,0:T(8,128)(2,1)S(1)}, bf16[2,304,128]{2,1,0:T(8,128)(2,1)S(1)}, u32[]{:S(2)}, u32[]{:S(2)}) collective-permute-start(bf16[2,304,128]{2,1,0:T(8,128)(2,1)S(1)} %slice.40), channel_id=1, source_target_pairs={{0,56},{8,0},{16,8},{24,16},{32,24},{40,32},{48,40},{56,48},{1,57}... | collective-permute-start | bytes 466952 | tf_op jit(solution)/shard_map/ppermute | solution.py:346
  101.8 7.6 %collective-permute-start.11 = (bf16[2,304,128]{2,1,0:T(8,128)(2,1)S(1)}, bf16[2,304,128]{2,1,0:T(8,128)(2,1)S(1)}, u32[]{:S(2)}, u32[]{:S(2)}) collective-permute-start(bf16[2,304,128]{2,1,0:T(8,128)(2,1)S(1)} %slice.39), channel_id=1, source_target_pairs={{0,8},{8,16},{16,24},{24,32},{32,40},{40,48},{48,56},{56,0},{1,9},... | collective-permute-start | bytes 466952 | tf_op jit(solution)/shard_map/ppermute | solution.py:346
  106.3 3.1 %copy-start.5 = (bf16[2,304,128]{2,1,0:T(8,128)(2,1)}, bf16[2,304,128]{2,1,0:T(8,128)(2,1)S(1)}, u32[]{:S(2)}) copy-start(bf16[2,304,128]{2,1,0:T(8,128)(2,1)S(1)} %collective-permute-done.12.refs_8_) | copy-start | bytes 466948
  114.7 1.7 collective-permute-start.13
  (3 other events, 2.0 us)

commit v7 on v6

--- a/solution.py
+++ b/solution.py
@@ -34,7 +34,7 @@
     pad_ref[0:8, :] = prior_ref[...].astype(F32)
     pad_ref[8 : 8 + rows, :] = ci_ref[...].astype(F32)
     for s in range(4):
-        par = par_ref[s, 0].astype(F32)
+        par = par_ref[0, s].astype(F32)
         lanes = slice(s * SHARD, (s + 1) * SHARD)
         total = jnp.broadcast_to(par[taps : taps + 1, :], (rows, SHARD))
         for k in range(taps):
@@ -53,7 +53,7 @@
             pl.BlockSpec(memory_space=pltpu.SMEM),
             pl.BlockSpec((rows, BLK), lambda b: (0, b)),
             pl.BlockSpec((8, BLK), lambda b: (0, b)),
-            pl.BlockSpec((4, 1, 8, SHARD), lambda b: (b % 2, b // 2, 0, 0)),
+            pl.BlockSpec((1, 4, 8, SHARD), lambda b: (b // 2, b % 2, 0, 0)),
         ],
         out_specs=[
             pl.BlockSpec((rows, BLK), lambda b: (0, b)),
@@ -110,34 +110,26 @@
     )(where, xc, lent, *blocks)
 
 
-def norm_kernel(own_ref, other_ref, gain_ref, normed_ref, bc_ref):
-    rows, rank = normed_ref.shape
-    proj = own_ref[...] + other_ref[...]
-    low = proj[:, 0:rank]
-    scale = lax.rsqrt(jnp.mean(low * low, axis=1, keepdims=True) + 1e-06)
-    normed_ref[...] = (low * scale * gain_ref[...]).astype(BF16)
-    for m in range(32):
-        bc_ref[m * rows : (m + 1) * rows, :] = jnp.broadcast_to(proj[:, rank + m : rank + m + 1], (rows, 128))
-
-
-def norm(own, other, gain):
-    rows = own.shape[0]
-    vmem = pl.BlockSpec(memory_space=pltpu.VMEM)
-    return pl.pallas_call(
-        norm_kernel,
-        in_specs=[vmem, vmem, vmem],
-        out_specs=[vmem, vmem],
-        out_shape=[
-            jax.ShapeDtypeStruct((rows, 256), BF16),
-            jax.ShapeDtypeStruct((32 * rows, 128), F32),
-        ],
-        name="norm",
-    )(own, other, gain)
-
-
-def scan_kernel(where_ref, normed_ref, xc_ref, own_ref, oth_ref, bc_ref, step_ref, y_ref, rate_ref, ends_ref, x_scr, par_scr, h_scr):
+def spread(proj, first, count, out_ref):
+    rows = proj.shape[0]
+    for m in range(count):
+        out_ref[m * rows : (m + 1) * rows, :] = jnp.broadcast_to(proj[:, first + m : first + m + 1], (rows, 128))
+
+
+def scan_kernel(where_ref, mine_ref, other_ref, gain_ref, xc_ref, own_ref, oth_ref, step_ref, y_ref, rate_ref, ends_ref, *scratch):
+    x_scr, par_scr, h_scr, normed_ref, bc_ref = scratch
     core = where_ref[0]
-    rows = normed_ref.shape[0]
+    rows = xc_ref.shape[0]
+    rank = gain_ref.shape[1]
+
+    @pl.when(pl.program_id(0) == 0)
+    def _():
+        proj = mine_ref[...] + other_ref[...]
+        low = proj[:, 0:rank]
+        scale = lax.rsqrt(jnp.mean(low * low, axis=1, keepdims=True) + 1e-06)
+        normed_ref[...] = (low * scale * gain_ref[...]).astype(BF16)
+        spread(proj, rank, 32, bc_ref)
+
     mine_k = normed_ref[:, pl.ds(pl.multiple_of(core * 128, 128), 128)]
     other_k = normed_ref[:, pl.ds(pl.multiple_of((1 - core) * 128, 128), 128)]
     skips = []
@@ -208,7 +200,7 @@
         ends_ref[jj, 32:40, :] = jnp.concatenate(sums, 0).astype(BF16)
 
 
-def scan(where, normed, xc, d_own, d_oth, bc):
+def scan(where, mine, other, gain, xc, d_own, d_oth):
     rows, inner = xc.shape
     blocks = inner // BLK
     wspec = pl.BlockSpec((1, 4, 152, 256), lambda b, where: (b // 2, b % 2, 0, 0))
@@ -216,11 +208,12 @@
         num_scalar_prefetch=1,
         grid=(blocks,),
         in_specs=[
-            pl.BlockSpec((rows, 256), lambda b, where: (0, 0)),
+            pl.BlockSpec((rows, 288), lambda b, where: (0, 0)),
+            pl.BlockSpec((rows, 288), lambda b, where: (0, 0)),
+            pl.BlockSpec((1, 256), lambda b, where: (0, 0)),
             pl.BlockSpec((rows, BLK), lambda b, where: (0, b)),
             wspec,
             wspec,
-            pl.BlockSpec((32 * rows, 128), lambda b, where: (0, 0)),
         ],
         out_specs=[
             pl.BlockSpec((1, 8 * rows, 128), lambda b, where: (b, 0, 0)),
@@ -232,6 +225,8 @@
             pltpu.VMEM((8 * rows, 128), F32),
             pltpu.VMEM((128, 128), F32),
             pltpu.VMEM((144, 128), F32),
+            pltpu.VMEM((rows, 256), BF16),
+            pltpu.VMEM((32 * rows, 128), F32),
         ],
     )
     return pl.pallas_call(
@@ -245,7 +240,7 @@
         ],
         compiler_params=pltpu.CompilerParams(dimension_semantics=("arbitrary",)),
         name="scan",
-    )(where, normed, xc, d_own, d_oth, bc)
+    )(where, mine, other, gain, xc, d_own, d_oth)
 
 
 def link_kernel(ends_ref, log_ref, start_ref):
@@ -269,8 +264,13 @@
     )(ends, a_log)
 
 
-def close_kernel(step_ref, y_ref, rate_ref, start_ref, c_ref, gate_ref, out_ref, s_scr, y_scr):
+def close_kernel(step_ref, y_ref, rate_ref, start_ref, mine_ref, other_ref, gate_ref, out_ref, s_scr, y_scr, c_ref):
     rows = gate_ref.shape[0]
+
+    @pl.when(pl.program_id(0) == 0)
+    def _():
+        spread(mine_ref[...] + other_ref[...], 272, 16, c_ref)
+
     for j in range(8):
         s_scr[16 * j : 16 * j + 16, :] = start_ref[j // 2, (j % 2) * 16 : (j % 2) * 16 + 16, :].astype(F32)
     starts = [s_scr[pl.ds(n, 8, stride=16), :] for n in range(16)]
@@ -301,7 +301,7 @@
             out_ref[16 * i : 16 * i + 16, j * 128 : (j + 1) * 128] = (y * silu(gate)).astype(BF16)
 
 
-def close(step, y, rate, start, bc, gate):
+def close(step, y, rate, start, mine, other, gate):
     rows, inner = gate.shape
     return pl.pallas_call(
         close_kernel,
@@ -311,15 +311,16 @@
             pl.BlockSpec((1, 8 * rows, 128), lambda b: (b, 0, 0)),
             pl.BlockSpec((1, 128, 128), lambda b: (b, 0, 0)),
             pl.BlockSpec((4, 32, 128), lambda b: (b, 0, 0)),
-            pl.BlockSpec((16 * rows, 128), lambda b: (1, 0)),
+            pl.BlockSpec((rows, 288), lambda b: (0, 0)),
+            pl.BlockSpec((rows, 288), lambda b: (0, 0)),
             pl.BlockSpec((rows, BLK), lambda b: (0, b)),
         ],
         out_specs=pl.BlockSpec((rows, BLK), lambda b: (0, b)),
         out_shape=jax.ShapeDtypeStruct((rows, inner), BF16),
-        scratch_shapes=[pltpu.VMEM((128, 128), F32), pltpu.VMEM((8 * rows, 128), F32)],
+        scratch_shapes=[pltpu.VMEM((128, 128), F32), pltpu.VMEM((8 * rows, 128), F32), pltpu.VMEM((16 * rows, 128), F32)],
         compiler_params=pltpu.CompilerParams(dimension_semantics=("arbitrary",)),
         name="close",
-    )(step, y, rate, start, bc, gate)
+    )(step, y, rate, start, mine, other, gate)
 
 
 def from_everyone(x, axis):
@@ -327,17 +328,16 @@
     return lax.all_to_all(copies, axis, split_axis=0, concat_axis=0, tiled=True)
 
 
-def pack_x(core, x_weight, conv_weight, conv_bias):
-    half = lax.dynamic_slice_in_dim(x_weight.T, core * 128, 128, 1)
-    taps = jnp.concatenate([conv_weight, conv_bias[None, :], jnp.zeros((3, SHARD), BF16)], 0)
-    return jnp.concatenate([half, taps[:, :128], taps[:, 128:]], 0)
-
-
-def pack_d(core, dt_weight, dt_bias, a_log, skip):
+def pack_x(core, x_weight):
+    return lax.dynamic_slice_in_dim(x_weight.T, core * 128, 128, 1)
+
+
+def pack_d(core, dt_weight, dt_bias, a_log, skip, conv_weight, conv_bias):
     half = lax.dynamic_slice_in_dim(dt_weight, core * 128, 128, 0)
     logs = lax.dynamic_slice_in_dim(a_log, core * 8, 8, 0)
     vec = jnp.where(core == 0, dt_bias, skip)[None, :]
     pieces = [half, *two_parts(logs), *two_parts(vec), jnp.zeros((6, SHARD), BF16)]
+    pieces += [conv_weight, conv_bias[None, :], jnp.zeros((3, SHARD), BF16)]
     return jnp.concatenate(pieces, 0)
 
 
@@ -356,10 +356,6 @@
     return out
 
 
-def together(*values):
-    return lax.optimization_barrier(values)
-
-
 def both_ways(pair, axis):
     return shifted(pair[0], axis, 1), shifted(pair[1], axis, -1)
 
@@ -369,33 +365,30 @@
     count = lax.axis_size(SEQ)
     swap = [(0, 1), (1, 0)]
     where = jnp.stack([core, lax.axis_index("z")]).astype(jnp.int32)
-    prior = lax.ppermute(conv_input[conv_input.shape[0] - 8 :], SEQ, [(i, i + 1) for i in range(count - 1)])
-    x_piece = pack_x(core, x_weight, conv_weight, conv_bias)
+    x_piece = pack_x(core, x_weight)
     x_pieces = [x_piece] + [shifted(x_piece, "y", k) for k in (1, 2, 3)]
     x0 = placed(x_pieces, [(0, 0), (-1, 0), (-2, 0), (-3, 0)], "y")
+    d_part = from_everyone(pack_d(core, dt_weight, dt_bias, a_log, skip, conv_weight, conv_bias), "z")
+    d_part = d_part.reshape(8, 160, SHARD)
+    prior = lax.ppermute(conv_input[conv_input.shape[0] - 8 :], SEQ, [(i, i + 1) for i in range(count - 1)])
     x1 = both_ways((x0, x0), "z")
-    taps = jnp.concatenate([x0[:, 288:296], x0[:, 296:304]], 2).reshape(32, SHARD)
-    d_msg = jnp.concatenate([pack_d(core, dt_weight, dt_bias, a_log, skip), taps], 0)
-    d_part = from_everyone(d_msg, "z").reshape(8, 184, SHARD)
+    taps = from_everyone(d_part[:, 152:], "y").reshape(4, 8, 8, SHARD)
     x2 = both_ways(x1, "z")
     d0 = d_part[:, :152]
-    d1 = both_ways((d0, d0), "y")
+    up, down = both_ways((d0, d0), "y")
+    xc, lend = conv(where, conv_input, prior, taps)
     x3 = both_ways(x2, "z")
-    xc, lend = conv(where, conv_input, prior, d_part[:, 152:].reshape(8, 4, 8, SHARD))
-    *x3, xc, lend = together(*x3, xc, lend)
-    up, down = d1
     lent = lax.ppermute(lend, "core", swap)
     x4 = both_ways((x3[0][:2], x3[1][2:]), "z")
     d2 = both_ways((up[:4], down[4:]), "y")
     d_own = placed([d0, up, down, *d2], [(0, 0), (-1, 0), (1, 0), (2, 0), (2, 4)], "y")
     d_oth = lax.ppermute(d_own, "core", swap)
-    own, other = project(where, xc, lent, [x0, *x1, *x2, *x3, *x4])
+    mine, other = project(where, xc, lent, [x0, *x1, *x2, *x3, *x4])
     other = lax.ppermute(other, "core", swap)
-    normed, bc = norm(own, other, dt_gain[None, :])
-    step, y, rate, ends = scan(where, normed, xc, d_own, d_oth, bc)
+    step, y, rate, ends = scan(where, mine, other, dt_gain[None, :], xc, d_own, d_oth)
     ends = lax.all_to_all(ends, SEQ, split_axis=0, concat_axis=0, tiled=True)
     start = lax.all_to_all(link(ends, a_log), SEQ, split_axis=0, concat_axis=0, tiled=True)
-    return close(step, y, rate, start, bc, gate_input)
+    return close(step, y, rate, start, mine, other, gate_input)
 
 
 def solution(mesh):

time: 210 us -> 221 us (1.052)
  waiting for transfers between devices: 33.6 us -> 45.7 us
  starting transfers between devices: 25.5 us -> 30.6 us
  blocking collectives: 70.6 us -> 65.8 us
  Pallas kernels: 62 us -> 59.2 us
    ppermute x15, waiting for transfers between devices: 32 us -> 39.6 us  [shifted(): lax.ppermute(block, axis, [(i, (i + by) % count) for i in range(count)])]
    all_to_all x0 -> x1, waiting for transfers between devices: none -> 4.4 us  [from_everyone(): return lax.all_to_all(copies, axis, split_axis=0, concat_axis=0, tiled=True)]
    dynamic_update_slice x8 -> x9, local copies, waits for them, and re-layouts: 2.39 us -> 6.31 us  [placed(): lax.dynamic_update_slice(out, block[None], ((here + by) % count, row) + (...]
    all_to_all x1, blocking collectives: 25.4 us -> 21.7 us  [body(): ends = lax.all_to_all(ends, SEQ, split_axis=0, concat_axis=0, tiled=True)]
    all_to_all x0 -> x1, starting transfers between devices: none -> 3.32 us  [from_everyone(): return lax.all_to_all(copies, axis, split_axis=0, concat_axis=0, tiled=True)]
    pallas_call x1 -> x0, Pallas kernels: 3.04 us -> none  [norm(): pl.pallas_call(norm_kernel, in_specs=[vmem, vmem, vmem], out_specs=[vmem,...]
    ppermute x15, starting transfers between devices: 21.8 us -> 24.3 us  [shifted(): lax.ppermute(block, axis, [(i, (i + by) % count) for i in range(count)])]
  transfers between devices with their start and end apart: 19 -> 20, of which waited for: 9 -> 13; matrix products, arithmetic and copies ran while one was open for 6% -> 6% of each run, Pallas kernels for 7% -> 6%
where the time goes in v7:
time: 221 us; the launch traced here: 219 us
  blocking collectives  65.8 us (30%)
  Pallas kernels  59.2 us (27%)
  waiting for transfers between devices  45.7 us (21%)
  starting transfers between devices  30.6 us (14%)
  local copies, waits for them, and re-layouts  15.9 us (7%)
    ppermute x15, waiting for transfers between devices, shifted(): lax.ppermute(block, axis, [(i, (i + by) % count) for i in range(count)])  39.6 us
    pallas_call x1, Pallas kernels, scan(): pl.pallas_call(scan_kernel, grid_spec=grid_spec, out_shape=[jax.ShapeDtyp...  27.4 us
    all_to_all x1, blocking collectives, from_everyone(): return lax.all_to_all(copies, axis, split_axis=0, concat_axis=0, tiled=True)  27.2 us
    ppermute x15, starting transfers between devices, shifted(): lax.ppermute(block, axis, [(i, (i + by) % count) for i in range(count)])  24.3 us
    all_to_all x1, blocking collectives, body(): ends = lax.all_to_all(ends, SEQ, split_axis=0, concat_axis=0, tiled=True)  21.7 us
    pallas_call x1, Pallas kernels, close(): pl.pallas_call(close_kernel, grid=(inner // BLK,), in_specs=[pl.BlockSpec...  17.5 us
    all_to_all x1, blocking collectives, body(): lax.all_to_all(link(ends, a_log), SEQ, split_axis=0, concat_axis=0, tiled...  16.8 us
    pallas_call x1, Pallas kernels, conv(): pl.pallas_call(conv_kernel, grid=(inner // BLK,), in_specs=[pl.BlockSpec(...  7.96 us
  transfers between devices with their start and end apart: 20, of which 13 were waited for; matrix products, arithmetic and copies ran while one was open for 6% of the time, Pallas kernels for 6%

profile of v7, /device:TPU:32, one launch (start us, length us, event | category | flops | bytes accessed | tf_op | source)
XLA Modules:
  0.0 219.5 jit_solution(131408699294283333)
XLA Ops:
  2.9 27.2 %all_to_all.20 = bf16[8,160,256]{2,1,0:T(8,128)(2,1)S(1)} all-to-all(bf16[8,160,256]{2,1,0:T(8,128)(2,1)S(1)} %broadcast_in_dim.55), channel_id=1, replica_groups=mesh['y'=4,'z'=8,'x'=4,'core'=2] {'z'}, dimensions={0} | all-to-all | bytes 1310720 | tf_op jit(solution)/shard_map/all_to_all | solution.py:328
  32.6 1.7 collective-permute-start.15
  34.5 11.5 %collective-permute-done.14 = bf16[8,152,256]{2,1,0:T(8,128)(2,1)} collective-permute-done((bf16[8,152,256]{2,1,0:T(8,128)(2,1)}, bf16[8,152,256]{2,1,0:T(8,128)(2,1)}, u32[]{:S(2)}, u32[]{:S(2)}) %collective-permute-start.14) | collective-permute-done | bytes 622624 | tf_op jit(solution)/shard_map/ppermute | solution.py:346
  48.3 3.0 %collective-permute-start.17 = (bf16[4,152,256]{2,1,0:T(8,128)(2,1)S(1)}, bf16[4,152,256]{2,1,0:T(8,128)(2,1)S(1)}, u32[]{:S(2)}, u32[]{:S(2)}) collective-permute-start(bf16[4,152,256]{2,1,0:T(8,128)(2,1)S(1)} %slice.33), channel_id=1, source_target_pairs={{0,192},{64,0},{128,64},{192,128},{1,193},{65,1},{129,65},{193,129... | collective-permute-start | bytes 933896 | tf_op jit(solution)/shard_map/ppermute | solution.py:346
  56.7 2.5 %collective-permute-start.3 = (bf16[288,128]{1,0:T(8,128)(2,1)}, bf16[288,128]{1,0:T(8,128)(2,1)}, u32[]{:S(2)}, u32[]{:S(2)}) collective-permute-start(bf16[288,128]{1,0:T(8,128)(2,1)} %dynamic-slice_bitcast_fusion), channel_id=1, source_target_pairs={{0,128},{64,192},{128,0},{192,64},{1,129},{65,193},{129,1},{193,65... | collective-permute-start | bytes 221192 | tf_op jit(solution)/shard_map/ppermute | solution.py:346
  59.1 2.1 collective-permute-start.2
  63.9 2.8 %collective-permute-start = (bf16[8,8192]{1,0:T(8,128)(2,1)}, bf16[8,8192]{1,0:T(8,128)(2,1)S(1)}, u32[]{:S(2)}, u32[]{:S(2)}) collective-permute-start(bf16[8,8192]{1,0:T(8,128)(2,1)} %slice.21), channel_id=1, source_target_pairs={{0,8},{8,16},{16,24},{24,32},{32,40},{40,48},{48,56},{56,64},{64,7... | collective-permute-start | bytes 393224 | tf_op jit(solution)/shard_map/ppermute | solution.py:373
  69.8 3.3 %all-to-all-start.1 = ((bf16[4,8,8,256]{3,2,1,0:T(8,128)(2,1)}), bf16[4,8,8,256]{3,2,1,0:T(8,128)(2,1)S(1)}, u32[]{:S(2)}, u32[]{:S(2)}) async-start(bf16[4,8,8,256]{3,2,1,0:T(8,128)(2,1)} %broadcast_in_dim.56), calls=%async_computation.1 | async-start | bytes 262144 | tf_op jit(solution)/shard_map/all_to_all | solution.py:328
  74.7 4.4 %all-to-all-done.1.par_ref = bf16[4,8,8,256]{3,2,1,0:T(8,128)(2,1)S(1)} async-done(((bf16[4,8,8,256]{3,2,1,0:T(8,128)(2,1)}), bf16[4,8,8,256]{3,2,1,0:T(8,128)(2,1)S(1)}, u32[]{:S(2)}, u32[]{:S(2)}) %all-to-all-start.1) | async-done | bytes 131104 | tf_op jit(solution)/shard_map/all_to_all | solution.py:328
  79.7 8.0 %conv.1 = (bf16[128,8192]{1,0:T(8,128)(2,1)}, bf16[128,4096]{1,0:T(8,128)(2,1)}) custom-call(s32[2]{0:T(128)} %pad_add_fusion.core_ref.where_ref, bf16[128,8192]{1,0:T(8,128)(2,1)} %ci_ref.1, bf16[8,8192]{1,0:T(8,128)(2,1)} %copy-done.13, bf16[4,8,8,256]{3,2,1,0:T(8,128)(2,1)} %copy-done.6), custom_call_target="tpu_custom_call" | custom-call | tf_op jit(solution)/shard_map/conv/pallas_call | solution.py:49
  91.2 7.6 %collective-permute-done.6.refs_2_ = bf16[4,288,128]{2,1,0:T(8,128)(2,1)S(1)} collective-permute-done((bf16[4,288,128]{2,1,0:T(8,128)(2,1)}, bf16[4,288,128]{2,1,0:T(8,128)(2,1)S(1)}, u32[]{:S(2)}, u32[]{:S(2)}) %collective-permute-start.6) | collective-permute-done | bytes 294944 | tf_op jit(solution)/shard_map/ppermute | solution.py:346
  98.8 2.7 %collective-permute-start.8 = (bf16[4,288,128]{2,1,0:T(8,128)(2,1)S(1)}, bf16[4,288,128]{2,1,0:T(8,128)(2,1)S(1)}, u32[]{:S(2)}, u32[]{:S(2)}) collective-permute-start(bf16[4,288,128]{2,1,0:T(8,128)(2,1)S(1)} %collective-permute-done.6.refs_2_), channel_id=1, source_target_pairs={{0,56},{8,0},{16,8},{24,16},{32,24},{40,32},{48,40},{56,48},{1,57}... | collective-permute-start | bytes 884744 | tf_op jit(solution)/shard_map/ppermute | solution.py:346
  102.0 5.7 %collective-permute-done.8.refs_4_ = bf16[4,288,128]{2,1,0:T(8,128)(2,1)S(1)} collective-permute-done((bf16[4,288,128]{2,1,0:T(8,128)(2,1)S(1)}, bf16[4,288,128]{2,1,0:T(8,128)(2,1)S(1)}, u32[]{:S(2)}, u32[]{:S(2)}) %collective-permute-start.8) | collective-permute-done | bytes 294944 | tf_op jit(solution)/shard_map/ppermute | solution.py:346
  107.7 3.5 %collective-permute-start.10 = (bf16[4,288,128]{2,1,0:T(8,128)(2,1)S(1)}, bf16[4,288,128]{2,1,0:T(8,128)(2,1)S(1)}, u32[]{:S(2)}, u32[]{:S(2)}) collective-permute-start(bf16[4,288,128]{2,1,0:T(8,128)(2,1)S(1)} %collective-permute-done.8.refs_4_), channel_id=1, source_target_pairs={{0,56},{8,0},{16,8},{24,16},{32,24},{40,32},{48,40},{56,48},{1,57}... | collective-permute-start | bytes 884744 | tf_op jit(solution)/shard_map/ppermute | solution.py:346
  111.7 4.9 %collective-permute-done.10.refs_6_ = bf16[4,288,128]{2,1,0:T(8,128)(2,1)S(1)} collective-permute-done((bf16[4,288,128]{2,1,0:T(8,128)(2,1)S(1)}, bf16[4,288,128]{2,1,0:T(8,128)(2,1)S(1)}, u32[]{:S(2)}, u32[]{:S(2)}) %collective-permute-start.10) | collective-permute-done | bytes 294944 | tf_op jit(solution)/shard_map/ppermute | solution.py:346
  116.7 3.6 %collective-permute-start.12 = (bf16[2,288,128]{2,1,0:T(8,128)(2,1)S(1)}, bf16[2,288,128]{2,1,0:T(8,128)(2,1)S(1)}, u32[]{:S(2)}, u32[]{:S(2)}) collective-permute-start(bf16[2,288,128]{2,1,0:T(8,128)(2,1)S(1)} %slice.30), channel_id=1, source_target_pairs={{0,56},{8,0},{16,8},{24,16},{32,24},{40,32},{48,40},{56,48},{1,57}... | collective-permute-start | bytes 442376 | tf_op jit(solution)/shard_map/ppermute | solution.py:346
  121.0 1.9 collective-permute-done.12.refs_8_
  122.9 4.3 %collective-permute-done.11.refs_7_ = bf16[2,288,128]{2,1,0:T(8,128)(2,1)} collective-permute-done((bf16[2,288,128]{2,1,0:T(8,128)(2,1)S(1)}, bf16[2,288,128]{2,1,0:T(8,128)(2,1)}, u32[]{:S(2)}, u32[]{:S(2)}) %collective-permute-start.11) | collective-permute-done | bytes 147488 | tf_op jit(solution)/shard_map/ppermute | solution.py:346
  127.3 4.5 %project.1 = (f32[128,288]{1,0:T(8,128)}, f32[128,288]{1,0:T(8,128)}) custom-call(s32[2]{0:T(128)} %pad_add_fusion.core_ref.where_ref, bf16[128,8192]{1,0:T(8,128)(2,1)} %get-tuple-element.13.xc_ref, bf16[128,4096]{1,0:T(8,128)(2,1)} %collective-permute-done.1.lent_ref, bf16[4,288,128]{2,1,0:T(8,128)(2,1)} %bitcast_dynamic-update-slice_fusion.6.refs_0_, ...), custom_call_target="tpu_custom_call" | custom-call | tf_op jit(solution)/shard_map/project/pallas_call | solution.py:104
  134.2 27.4 %scan.1 = (f32[8,1024,128]{2,1,0:T(8,128)}, f32[8,1024,128]{2,1,0:T(8,128)}, f32[8,128,128]{2,1,0:T(8,128)}, bf16[32,40,128]{2,1,0:T(8,128)(2,1)}) custom-call(s32[2]{0:T(128)} %pad_add_fusion.core_ref.where_ref, f32[128,288]{1,0:T(8,128)} %get-tuple-element.15.mine_ref, f32[128,288]{1,0:T(8,128)} %copy-done.3, f32[1,256]{1,0:T(1,128)} %bitcast.24, ...), custom_call_target="tpu_custom_call" | custom-call | tf_op jit(solution)/shard_map/scan/pallas_call | solution.py:232
  161.6 21.7 %all_to_all.21.ends_ref = bf16[32,40,128]{2,1,0:T(8,128)(2,1)} all-to-all(bf16[32,40,128]{2,1,0:T(8,128)(2,1)} %get-tuple-element.20), channel_id=1, replica_groups=mesh['y'=4,'z'=8,'x'=4,'core'=2] {'y','z'}, dimensions={0} | all-to-all | bytes 655360 | tf_op jit(solution)/shard_map/all_to_all | solution.py:389
  183.4 1.8 link.1
  185.2 16.8 %all_to_all.22.start_ref = bf16[32,32,128]{2,1,0:T(8,128)(2,1)} all-to-all(bf16[32,32,128]{2,1,0:T(8,128)(2,1)} %link.1), channel_id=1, replica_groups=mesh['y'=4,'z'=8,'x'=4,'core'=2] {'y','z'}, dimensions={0} | all-to-all | bytes 524288 | tf_op jit(solution)/shard_map/all_to_all | solution.py:390
  202.0 17.5 %close.1 = bf16[128,8192]{1,0:T(8,128)(2,1)} custom-call(f32[8,1024,128]{2,1,0:T(8,128)} %get-tuple-element.17.step_ref, f32[8,1024,128]{2,1,0:T(8,128)} %get-tuple-element.18.y_ref, f32[8,128,128]{2,1,0:T(8,128)} %get-tuple-element.19.rate_ref, bf16[32,32,128]{2,1,0:T(8,128)(2,1)} %all_to_all.22.start_ref, f32[128,288]{1,0:T(8,128)} %get-tuple-element.15.mine_ref, ...), custom_call_target="tpu_custom_call" | custom-call | tf_op jit(solution)/shard_map/close/pallas_call | solution.py:306
  (83 shorter events, 28.6 us)
Async XLA Ops:
  31.0 14.9 %collective-permute-start.14 = (bf16[8,152,256]{2,1,0:T(8,128)(2,1)}, bf16[8,152,256]{2,1,0:T(8,128)(2,1)}, u32[]{:S(2)}, u32[]{:S(2)}) collective-permute-start(bf16[8,152,256]{2,1,0:T(8,128)(2,1)} %slice.31), channel_id=1, source_target_pairs={{0,64},{64,128},{128,192},{192,0},{1,65},{65,129},{129,193},{193,1... | collective-permute-start | bytes 1867784 | tf_op jit(solution)/shard_map/ppermute | solution.py:346
  32.6 14.7 %collective-permute-start.15 = (bf16[8,152,256]{2,1,0:T(8,128)(2,1)}, bf16[8,152,256]{2,1,0:T(8,128)(2,1)}, u32[]{:S(2)}, u32[]{:S(2)}) collective-permute-start(bf16[8,152,256]{2,1,0:T(8,128)(2,1)} %slice.31), channel_id=1, source_target_pairs={{0,192},{64,0},{128,64},{192,128},{1,193},{65,1},{129,65},{193,129... | collective-permute-start | bytes 1867784 | tf_op jit(solution)/shard_map/ppermute | solution.py:346
  34.5 21.4 %copy-start.12 = (bf16[256,288]{0,1:T(8,128)(2,1)S(1)}, bf16[256,288]{0,1:T(8,128)(2,1)}, u32[]{:S(2)}) copy-start(bf16[256,288]{0,1:T(8,128)(2,1)} %param.14) | copy-start | bytes 442372
  46.9 8.2 %collective-permute-start.16 = (bf16[4,152,256]{2,1,0:T(8,128)(2,1)S(1)}, bf16[4,152,256]{2,1,0:T(8,128)(2,1)S(1)}, u32[]{:S(2)}, u32[]{:S(2)}) collective-permute-start(bf16[4,152,256]{2,1,0:T(8,128)(2,1)S(1)} %slice.32), channel_id=1, source_target_pairs={{0,64},{64,128},{128,192},{192,0},{1,65},{65,129},{129,193},{193,1... | collective-permute-start | bytes 933896 | tf_op jit(solution)/shard_map/ppermute | solution.py:346
  48.3 7.4 %collective-permute-start.17 = (bf16[4,152,256]{2,1,0:T(8,128)(2,1)S(1)}, bf16[4,152,256]{2,1,0:T(8,128)(2,1)S(1)}, u32[]{:S(2)}, u32[]{:S(2)}) collective-permute-start(bf16[4,152,256]{2,1,0:T(8,128)(2,1)S(1)} %slice.33), channel_id=1, source_target_pairs={{0,192},{64,0},{128,64},{192,128},{1,193},{65,1},{129,65},{193,129... | collective-permute-start | bytes 933896 | tf_op jit(solution)/shard_map/ppermute | solution.py:346
  55.8 76.1 %copy-start.1 = (bf16[4,8,152,256]{3,2,1,0:T(8,128)(2,1)}, bf16[4,8,152,256]{3,2,1,0:T(8,128)(2,1)S(1)}, u32[]{:S(2)}) copy-start(bf16[4,8,152,256]{3,2,1,0:T(8,128)(2,1)S(1)} %bitcast_dynamic-update-slice_fusion.3.own_ref) | copy-start | bytes 7471108
  55.8 77.8 %collective-permute-start.18 = (bf16[4,8,152,256]{3,2,1,0:T(8,128)(2,1)S(1)}, bf16[4,8,152,256]{3,2,1,0:T(8,128)(2,1)}, u32[]{:S(2)}, u32[]{:S(2)}) collective-permute-start(bf16[4,8,152,256]{3,2,1,0:T(8,128)(2,1)S(1)} %bitcast_dynamic-update-slice_fusion.3.own_ref), channel_id=1, source_target_pairs={{0,1},{1,0},{2,3},{3,2},{4,5},{5,4},{6,7},{7,6},{8,9},{9,8},{10,11... | collective-permute-start | bytes 7471112 | tf_op jit(solution)/shard_map/ppermute | solution.py:385
  56.7 16.5 %collective-permute-start.3 = (bf16[288,128]{1,0:T(8,128)(2,1)}, bf16[288,128]{1,0:T(8,128)(2,1)}, u32[]{:S(2)}, u32[]{:S(2)}) collective-permute-start(bf16[288,128]{1,0:T(8,128)(2,1)} %dynamic-slice_bitcast_fusion), channel_id=1, source_target_pairs={{0,128},{64,192},{128,0},{192,64},{1,129},{65,193},{129,1},{193,65... | collective-permute-start | bytes 221192 | tf_op jit(solution)/shard_map/ppermute | solution.py:346
  59.1 8.4 %collective-permute-start.2 = (bf16[288,128]{1,0:T(8,128)(2,1)}, bf16[288,128]{1,0:T(8,128)(2,1)}, u32[]{:S(2)}, u32[]{:S(2)}) collective-permute-start(bf16[288,128]{1,0:T(8,128)(2,1)} %dynamic-slice_bitcast_fusion), channel_id=1, source_target_pairs={{0,64},{64,128},{128,192},{192,0},{1,65},{65,129},{129,193},{193,1... | collective-permute-start | bytes 221192 | tf_op jit(solution)/shard_map/ppermute | solution.py:346
  61.2 26.5 %collective-permute-start.4 = (bf16[288,128]{1,0:T(8,128)(2,1)}, bf16[288,128]{1,0:T(8,128)(2,1)}, u32[]{:S(2)}, u32[]{:S(2)}) collective-permute-start(bf16[288,128]{1,0:T(8,128)(2,1)} %dynamic-slice_bitcast_fusion), channel_id=1, source_target_pairs={{0,192},{64,0},{128,64},{192,128},{1,193},{65,1},{129,65},{193,129... | collective-permute-start | bytes 221192 | tf_op jit(solution)/shard_map/ppermute | solution.py:346
  63.9 10.7 %collective-permute-start = (bf16[8,8192]{1,0:T(8,128)(2,1)}, bf16[8,8192]{1,0:T(8,128)(2,1)S(1)}, u32[]{:S(2)}, u32[]{:S(2)}) collective-permute-start(bf16[8,8192]{1,0:T(8,128)(2,1)} %slice.21), channel_id=1, source_target_pairs={{0,8},{8,16},{16,24},{24,32},{32,40},{40,48},{48,56},{56,64},{64,7... | collective-permute-start | bytes 393224 | tf_op jit(solution)/shard_map/ppermute | solution.py:373
  69.8 9.3 %all-to-all-start.1 = ((bf16[4,8,8,256]{3,2,1,0:T(8,128)(2,1)}), bf16[4,8,8,256]{3,2,1,0:T(8,128)(2,1)S(1)}, u32[]{:S(2)}, u32[]{:S(2)}) async-start(bf16[4,8,8,256]{3,2,1,0:T(8,128)(2,1)} %broadcast_in_dim.56), calls=%async_computation.1 | async-start | bytes 262144 | tf_op jit(solution)/shard_map/all_to_all | solution.py:328
  87.7 39.6 %collective-permute-start.1 = (bf16[128,4096]{1,0:T(8,128)(2,1)}, bf16[128,4096]{1,0:T(8,128)(2,1)}, u32[]{:S(2)}, u32[]{:S(2)}) collective-permute-start(bf16[128,4096]{1,0:T(8,128)(2,1)} %get-tuple-element.14), channel_id=1, source_target_pairs={{0,1},{1,0},{2,3},{3,2},{4,5},{5,4},{6,7},{7,6},{8,9},{9,8},{10,11... | collective-permute-start | bytes 3145736 | tf_op jit(solution)/shard_map/ppermute | solution.py:381
  89.2 9.6 %collective-permute-start.6 = (bf16[4,288,128]{2,1,0:T(8,128)(2,1)}, bf16[4,288,128]{2,1,0:T(8,128)(2,1)S(1)}, u32[]{:S(2)}, u32[]{:S(2)}) collective-permute-start(bf16[4,288,128]{2,1,0:T(8,128)(2,1)} %bitcast_dynamic-update-slice_fusion.6.refs_0_), channel_id=1, source_target_pairs={{0,56},{8,0},{16,8},{24,16},{32,24},{40,32},{48,40},{56,48},{1,57}... | collective-permute-start | bytes 884744 | tf_op jit(solution)/shard_map/ppermute | solution.py:346
  90.3 11.6 %collective-permute-start.5 = (bf16[4,288,128]{2,1,0:T(8,128)(2,1)}, bf16[4,288,128]{2,1,0:T(8,128)(2,1)S(1)}, u32[]{:S(2)}, u32[]{:S(2)}) collective-permute-start(bf16[4,288,128]{2,1,0:T(8,128)(2,1)} %bitcast_dynamic-update-slice_fusion.6.refs_0_), channel_id=1, source_target_pairs={{0,8},{8,16},{16,24},{24,32},{32,40},{40,48},{48,56},{56,0},{1,9},... | collective-permute-start | bytes 884744 | tf_op jit(solution)/shard_map/ppermute | solution.py:346
  98.8 8.9 %collective-permute-start.8 = (bf16[4,288,128]{2,1,0:T(8,128)(2,1)S(1)}, bf16[4,288,128]{2,1,0:T(8,128)(2,1)S(1)}, u32[]{:S(2)}, u32[]{:S(2)}) collective-permute-start(bf16[4,288,128]{2,1,0:T(8,128)(2,1)S(1)} %collective-permute-done.6.refs_2_), channel_id=1, source_target_pairs={{0,56},{8,0},{16,8},{24,16},{32,24},{40,32},{48,40},{56,48},{1,57}... | collective-permute-start | bytes 884744 | tf_op jit(solution)/shard_map/ppermute | solution.py:346
  102.0 9.3 %copy-start.8 = (bf16[4,288,128]{2,1,0:T(8,128)(2,1)}, bf16[4,288,128]{2,1,0:T(8,128)(2,1)S(1)}, u32[]{:S(2)}) copy-start(bf16[4,288,128]{2,1,0:T(8,128)(2,1)S(1)} %collective-permute-done.5.refs_1_) | copy-start | bytes 884740
  102.0 9.7 %collective-permute-start.7 = (bf16[4,288,128]{2,1,0:T(8,128)(2,1)S(1)}, bf16[4,288,128]{2,1,0:T(8,128)(2,1)S(1)}, u32[]{:S(2)}, u32[]{:S(2)}) collective-permute-start(bf16[4,288,128]{2,1,0:T(8,128)(2,1)S(1)} %collective-permute-done.5.refs_1_), channel_id=1, source_target_pairs={{0,8},{8,16},{16,24},{24,32},{32,40},{40,48},{48,56},{56,0},{1,9},... | collective-permute-start | bytes 884744 | tf_op jit(solution)/shard_map/ppermute | solution.py:346
  107.7 8.9 %collective-permute-start.10 = (bf16[4,288,128]{2,1,0:T(8,128)(2,1)S(1)}, bf16[4,288,128]{2,1,0:T(8,128)(2,1)S(1)}, u32[]{:S(2)}, u32[]{:S(2)}) collective-permute-start(bf16[4,288,128]{2,1,0:T(8,128)(2,1)S(1)} %collective-permute-done.8.refs_4_), channel_id=1, source_target_pairs={{0,56},{8,0},{16,8},{24,16},{32,24},{40,32},{48,40},{56,48},{1,57}... | collective-permute-start | bytes 884744 | tf_op jit(solution)/shard_map/ppermute | solution.py:346
  111.7 9.2 %collective-permute-start.9 = (bf16[4,288,128]{2,1,0:T(8,128)(2,1)S(1)}, bf16[4,288,128]{2,1,0:T(8,128)(2,1)S(1)}, u32[]{:S(2)}, u32[]{:S(2)}) collective-permute-start(bf16[4,288,128]{2,1,0:T(8,128)(2,1)S(1)} %collective-permute-done.7.refs_3_), channel_id=1, source_target_pairs={{0,8},{8,16},{16,24},{24,32},{32,40},{40,48},{48,56},{56,0},{1,9},... | collective-permute-start | bytes 884744 | tf_op jit(solution)/shard_map/ppermute | solution.py:346
  116.6 10.6 %copy-start.4 = (bf16[4,288,128]{2,1,0:T(8,128)(2,1)}, bf16[4,288,128]{2,1,0:T(8,128)(2,1)S(1)}, u32[]{:S(2)}) copy-start(bf16[4,288,128]{2,1,0:T(8,128)(2,1)S(1)} %collective-permute-done.10.refs_6_) | copy-start | bytes 884740
  116.7 6.3 %collective-permute-start.12 = (bf16[2,288,128]{2,1,0:T(8,128)(2,1)S(1)}, bf16[2,288,128]{2,1,0:T(8,128)(2,1)S(1)}, u32[]{:S(2)}, u32[]{:S(2)}) collective-permute-start(bf16[2,288,128]{2,1,0:T(8,128)(2,1)S(1)} %slice.30), channel_id=1, source_target_pairs={{0,56},{8,0},{16,8},{24,16},{32,24},{40,32},{48,40},{56,48},{1,57}... | collective-permute-start | bytes 442376 | tf_op jit(solution)/shard_map/ppermute | solution.py:346
  120.9 6.4 %collective-permute-start.11 = (bf16[2,288,128]{2,1,0:T(8,128)(2,1)S(1)}, bf16[2,288,128]{2,1,0:T(8,128)(2,1)}, u32[]{:S(2)}, u32[]{:S(2)}) collective-permute-start(bf16[2,288,128]{2,1,0:T(8,128)(2,1)S(1)} %slice.29), channel_id=1, source_target_pairs={{0,8},{8,16},{16,24},{24,32},{32,40},{40,48},{48,56},{56,0},{1,9},... | collective-permute-start | bytes 442376 | tf_op jit(solution)/shard_map/ppermute | solution.py:346
  131.8 1.7 collective-permute-start.13
  (10 other events, 35.6 us)

commit v8 on v7

--- a/solution.py
+++ b/solution.py
@@ -69,45 +69,40 @@
     )(core, conv_input, prior, params)
 
 
-AWAY = (0, -1, 1, -2, 2, -3, 3, 4, 4)
-
-
 def times_rows(left, right):
     return lax.dot_general(left, right, (((1,), (1,)), ((), ())), preferred_element_type=F32)
 
 
-def project_kernel(where_ref, xc_ref, lent_ref, *refs):
-    blocks, (own_ref, other_ref) = refs[:-2], refs[-2:]
-    core, here = where_ref[0], where_ref[1]
+def project_kernel(where_ref, xc_ref, lent_ref, weight_ref, own_ref, other_ref):
+    core = where_ref[0]
     rows = xc_ref.shape[0]
+    depth, width = weight_ref.shape[:2]
     total = None
-    for k, (away, block) in enumerate(zip(AWAY, blocks)):
-        first = 2 if k == len(AWAY) - 1 else 0
-        z = lax.rem(here + 8 + away, 8)
-        for row in range(0, block.shape[0], 2):
+    for z in range(depth):
+        for y in range(0, width, 2):
             left = []
-            for y in (first + row, first + row + 1):
-                mine = pl.multiple_of((y * 8 + z) * SHARD + core * 128, 128)
-                lent = pl.multiple_of((y * 8 + z) * 128, 128)
-                left.append(jnp.concatenate([xc_ref[:, pl.ds(mine, 128)], lent_ref[:, pl.ds(lent, 128)]], 0))
-            right = jnp.concatenate([block[row, 0:288, :], block[row + 1, 0:288, :]], 1)
+            for shard in (y * depth + z, (y + 1) * depth + z):
+                mine = pl.multiple_of(shard * SHARD + core * 128, 128)
+                both = [xc_ref[:, pl.ds(mine, 128)], lent_ref[:, shard * 128 : (shard + 1) * 128]]
+                left.append(jnp.concatenate(both, 0))
+            right = jnp.concatenate([weight_ref[z, y], weight_ref[z, y + 1]], 1)
             part = times_rows(jnp.concatenate(left, 1), right)
             total = part if total is None else total + part
     own_ref[...] = total[:rows]
     other_ref[...] = total[rows:]
 
 
-def project(where, xc, lent, blocks):
+def project(where, xc, lent, weight):
     rows = xc.shape[0]
     vmem = pl.BlockSpec(memory_space=pltpu.VMEM)
     shape = jax.ShapeDtypeStruct((rows, 288), F32)
     return pl.pallas_call(
         project_kernel,
-        in_specs=[pl.BlockSpec(memory_space=pltpu.SMEM)] + [vmem] * (2 + len(blocks)),
+        in_specs=[pl.BlockSpec(memory_space=pltpu.SMEM), vmem, vmem, vmem],
         out_specs=[vmem, vmem],
         out_shape=[shape, shape],
         name="project",
-    )(where, xc, lent, *blocks)
+    )(where, xc, lent, weight)
 
 
 def spread(proj, first, count, out_ref):
@@ -371,19 +366,16 @@
     d_part = from_everyone(pack_d(core, dt_weight, dt_bias, a_log, skip, conv_weight, conv_bias), "z")
     d_part = d_part.reshape(8, 160, SHARD)
     prior = lax.ppermute(conv_input[conv_input.shape[0] - 8 :], SEQ, [(i, i + 1) for i in range(count - 1)])
-    x1 = both_ways((x0, x0), "z")
+    x_own = lax.all_gather(x0, "z", axis=0)
     taps = from_everyone(d_part[:, 152:], "y").reshape(4, 8, 8, SHARD)
-    x2 = both_ways(x1, "z")
     d0 = d_part[:, :152]
     up, down = both_ways((d0, d0), "y")
     xc, lend = conv(where, conv_input, prior, taps)
-    x3 = both_ways(x2, "z")
     lent = lax.ppermute(lend, "core", swap)
-    x4 = both_ways((x3[0][:2], x3[1][2:]), "z")
     d2 = both_ways((up[:4], down[4:]), "y")
     d_own = placed([d0, up, down, *d2], [(0, 0), (-1, 0), (1, 0), (2, 0), (2, 4)], "y")
     d_oth = lax.ppermute(d_own, "core", swap)
-    mine, other = project(where, xc, lent, [x0, *x1, *x2, *x3, *x4])
+    mine, other = project(where, xc, lent, x_own)
     other = lax.ppermute(other, "core", swap)
     step, y, rate, ends = scan(where, mine, other, dt_gain[None, :], xc, d_own, d_oth)
     ends = lax.all_to_all(ends, SEQ, split_axis=0, concat_axis=0, tiled=True)

time: 221 us -> 194 us (0.88)
  blocking collectives: 65.8 us -> 41.6 us
  between operations: 0.27 us -> 13.6 us
  waiting for transfers between devices: 45.7 us -> 34.8 us
  local copies, waits for them, and re-layouts: 15.9 us -> 12.5 us
    all_to_all x1 -> x0, blocking collectives: 27.2 us -> none  [from_everyone(): return lax.all_to_all(copies, axis, split_axis=0, concat_axis=0, tiled=True)]
    ppermute x15 -> x7, waiting for transfers between devices: 39.6 us -> 16.6 us  [shifted(): lax.ppermute(block, axis, [(i, (i + by) % count) for i in range(count)])]
    ppermute x15 -> x7, starting transfers between devices: 24.3 us -> 13.1 us  [shifted(): lax.ppermute(block, axis, [(i, (i + by) % count) for i in range(count)])]
    all_to_all x1 -> x2, starting transfers between devices: 3.32 us -> 13.5 us  [from_everyone(): return lax.all_to_all(copies, axis, split_axis=0, concat_axis=0, tiled=True)]
    all_to_all x1 -> x2, waiting for transfers between devices: 4.4 us -> 12 us  [from_everyone(): return lax.all_to_all(copies, axis, split_axis=0, concat_axis=0, tiled=True)]
    dynamic_update_slice x9, local copies, waits for them, and re-layouts: 6.31 us -> 2.43 us  [placed(): lax.dynamic_update_slice(out, block[None], ((here + by) % count, row) + (...]
    all_to_all x1, blocking collectives: 21.7 us -> 24.8 us  [body(): ends = lax.all_to_all(ends, SEQ, split_axis=0, concat_axis=0, tiled=True)]
    ppermute x1, waiting for transfers between devices: 0.01 us -> 3 us  [body(): lent = lax.ppermute(lend, 'core', swap)]
  transfers between devices with their start and end apart: 20 -> 14, of which waited for: 13 -> 9; matrix products, arithmetic and copies ran while one was open for 6% -> 5% of each run, Pallas kernels for 6% -> 6%
where the time goes in v8:
time: 194 us; the launch traced here: 192 us
  Pallas kernels  59.2 us (31%)
  blocking collectives  41.6 us (21%)
  waiting for transfers between devices  34.8 us (18%)
  starting transfers between devices  28.7 us (15%)
  between operations  13.6 us (7%)
  local copies, waits for them, and re-layouts  12.5 us (6%)
  other arithmetic  2.02 us (1%)
    pallas_call x1, Pallas kernels, scan(): pl.pallas_call(scan_kernel, grid_spec=grid_spec, out_shape=[jax.ShapeDtyp...  27.4 us
    all_to_all x1, blocking collectives, body(): ends = lax.all_to_all(ends, SEQ, split_axis=0, concat_axis=0, tiled=True)  24.8 us
    pallas_call x1, Pallas kernels, close(): pl.pallas_call(close_kernel, grid=(inner // BLK,), in_specs=[pl.BlockSpec...  17.5 us
    all_to_all x1, blocking collectives, body(): lax.all_to_all(link(ends, a_log), SEQ, split_axis=0, concat_axis=0, tiled...  16.8 us
    ppermute x7, waiting for transfers between devices, shifted(): lax.ppermute(block, axis, [(i, (i + by) % count) for i in range(count)])  16.6 us
    all_to_all x2, starting transfers between devices, from_everyone(): return lax.all_to_all(copies, axis, split_axis=0, concat_axis=0, tiled=True)  13.5 us
    ppermute x7, starting transfers between devices, shifted(): lax.ppermute(block, axis, [(i, (i + by) % count) for i in range(count)])  13.1 us
    all_to_all x2, waiting for transfers between devices, from_everyone(): return lax.all_to_all(copies, axis, split_axis=0, concat_axis=0, tiled=True)  12 us
  transfers between devices with their start and end apart: 14, of which 9 were waited for; matrix products, arithmetic and copies ran while one was open for 5% of the time, Pallas kernels for 6%

profile of v8, /device:TPU:32, one launch (start us, length us, event | category | flops | bytes accessed | tf_op | source)
XLA Modules:
  0.0 192.4 jit_solution(11421211577497133815)
XLA Ops:
  10.3 8.6 %all-to-all-start = ((bf16[8,160,256]{2,1,0:T(8,128)(2,1)}), bf16[8,160,256]{2,1,0:T(8,128)(2,1)S(1)}, u32[]{:S(2)}, u32[]{:S(2)}) async-start(bf16[8,160,256]{2,1,0:T(8,128)(2,1)} %broadcast_in_dim.45), calls=%async_computation | async-start | bytes 1310720 | tf_op jit(solution)/shard_map/all_to_all | solution.py:323
  19.8 3.2 %collective-permute-start.3 = (bf16[288,128]{1,0:T(8,128)(2,1)S(1)}, bf16[288,128]{1,0:T(8,128)(2,1)S(1)}, u32[]{:S(2)}, u32[]{:S(2)}) collective-permute-start(bf16[288,128]{1,0:T(8,128)(2,1)S(1)} %dynamic-slice_bitcast_fusion), channel_id=1, source_target_pairs={{0,128},{64,192},{128,0},{192,64},{1,129},{65,193},{129,1},{193,65... | collective-permute-start | bytes 221192 | tf_op jit(solution)/shard_map/ppermute | solution.py:341
  23.6 2.6 %collective-permute-start.4 = (bf16[288,128]{1,0:T(8,128)(2,1)S(1)}, bf16[288,128]{1,0:T(8,128)(2,1)S(1)}, u32[]{:S(2)}, u32[]{:S(2)}) collective-permute-start(bf16[288,128]{1,0:T(8,128)(2,1)S(1)} %dynamic-slice_bitcast_fusion), channel_id=1, source_target_pairs={{0,192},{64,0},{128,64},{192,128},{1,193},{65,1},{129,65},{193,129... | collective-permute-start | bytes 221192 | tf_op jit(solution)/shard_map/ppermute | solution.py:341
  26.3 2.2 %collective-permute-done.2 = bf16[288,128]{1,0:T(8,128)(2,1)S(1)} collective-permute-done((bf16[288,128]{1,0:T(8,128)(2,1)S(1)}, bf16[288,128]{1,0:T(8,128)(2,1)S(1)}, u32[]{:S(2)}, u32[]{:S(2)}) %collective-permute-start.2) | collective-permute-done | bytes 73760 | tf_op jit(solution)/shard_map/ppermute | solution.py:341
  29.4 8.3 %all-to-all-done = bf16[8,160,256]{2,1,0:T(8,128)(2,1)S(1)} async-done(((bf16[8,160,256]{2,1,0:T(8,128)(2,1)}), bf16[8,160,256]{2,1,0:T(8,128)(2,1)S(1)}, u32[]{:S(2)}, u32[]{:S(2)}) %all-to-all-start) | async-done | bytes 655392 | tf_op jit(solution)/shard_map/all_to_all | solution.py:323
  38.6 1.6 collective-permute-start.6
  40.1 1.7 collective-permute-start.7
  42.0 12.2 %collective-permute-done.6 = bf16[8,152,256]{2,1,0:T(8,128)(2,1)} collective-permute-done((bf16[8,152,256]{2,1,0:T(8,128)(2,1)}, bf16[8,152,256]{2,1,0:T(8,128)(2,1)}, u32[]{:S(2)}, u32[]{:S(2)}) %collective-permute-start.6) | collective-permute-done | bytes 622624 | tf_op jit(solution)/shard_map/ppermute | solution.py:341
  56.6 3.0 %collective-permute-start.9 = (bf16[4,152,256]{2,1,0:T(8,128)(2,1)S(1)}, bf16[4,152,256]{2,1,0:T(8,128)(2,1)S(1)}, u32[]{:S(2)}, u32[]{:S(2)}) collective-permute-start(bf16[4,152,256]{2,1,0:T(8,128)(2,1)S(1)} %slice.23), channel_id=1, source_target_pairs={{0,192},{64,0},{128,64},{192,128},{1,193},{65,1},{129,65},{193,129... | collective-permute-start | bytes 933896 | tf_op jit(solution)/shard_map/ppermute | solution.py:341
  60.7 1.1 bitcast_dynamic-update-slice_fusion
  61.9 1.5 collective-permute-done.8
  65.3 1.9 collective-permute-start
  67.9 5.0 %all-to-all-start.1 = ((bf16[4,8,8,256]{3,2,1,0:T(8,128)(2,1)}), bf16[4,8,8,256]{3,2,1,0:T(8,128)(2,1)S(1)}, u32[]{:S(2)}, u32[]{:S(2)}) async-start(bf16[4,8,8,256]{3,2,1,0:T(8,128)(2,1)} %broadcast_in_dim.46), calls=%async_computation.1 | async-start | bytes 262144 | tf_op jit(solution)/shard_map/all_to_all | solution.py:323
  73.4 1.8 collective-permute-done.prior_ref
  75.2 3.6 %all-to-all-done.1.par_ref = bf16[4,8,8,256]{3,2,1,0:T(8,128)(2,1)S(1)} async-done(((bf16[4,8,8,256]{3,2,1,0:T(8,128)(2,1)}), bf16[4,8,8,256]{3,2,1,0:T(8,128)(2,1)S(1)}, u32[]{:S(2)}, u32[]{:S(2)}) %all-to-all-start.1) | async-done | bytes 131104 | tf_op jit(solution)/shard_map/all_to_all | solution.py:323
  79.5 7.9 %conv.1 = (bf16[128,8192]{1,0:T(8,128)(2,1)}, bf16[128,4096]{1,0:T(8,128)(2,1)}) custom-call(s32[2]{0:T(128)} %pad_add_fusion.core_ref.where_ref, bf16[128,8192]{1,0:T(8,128)(2,1)} %ci_ref.1, bf16[8,8192]{1,0:T(8,128)(2,1)} %copy-done.6, bf16[4,8,8,256]{3,2,1,0:T(8,128)(2,1)} %copy-done.4), custom_call_target="tpu_custom_call" | custom-call | tf_op jit(solution)/shard_map/conv/pallas_call | solution.py:49
  87.3 3.0 %collective-permute-done.1.lent_ref = bf16[128,4096]{1,0:T(8,128)(2,1)} collective-permute-done((bf16[128,4096]{1,0:T(8,128)(2,1)}, bf16[128,4096]{1,0:T(8,128)(2,1)}, u32[]{:S(2)}, u32[]{:S(2)}) %collective-permute-start.1) | collective-permute-done | bytes 1048608 | tf_op jit(solution)/shard_map/ppermute | solution.py:374
  90.3 4.6 %project.1 = (f32[128,288]{1,0:T(8,128)}, f32[128,288]{1,0:T(8,128)}) custom-call(s32[2]{0:T(128)} %pad_add_fusion.core_ref.where_ref, bf16[128,8192]{1,0:T(8,128)(2,1)} %get-tuple-element.13.xc_ref, bf16[128,4096]{1,0:T(8,128)(2,1)} %collective-permute-done.1.lent_ref, bf16[8,4,288,128]{3,2,1,0:T(8,128)(2,1)} %all-gather.2.cloned.1.call-done.weight_ref), custom_call_target="tpu_custom_call" | custom-call | tf_op jit(solution)/shard_map/project/pallas_call | solution.py:99
  95.1 1.5 collective-permute-done.5.other_ref
  97.3 27.4 %scan.1 = (f32[8,1024,128]{2,1,0:T(8,128)}, f32[8,1024,128]{2,1,0:T(8,128)}, f32[8,128,128]{2,1,0:T(8,128)}, bf16[32,40,128]{2,1,0:T(8,128)(2,1)}) custom-call(s32[2]{0:T(128)} %pad_add_fusion.core_ref.where_ref, f32[128,288]{1,0:T(8,128)} %get-tuple-element.15.mine_ref, f32[128,288]{1,0:T(8,128)} %copy-done.3, f32[1,256]{1,0:T(1,128)} %bitcast.24, ...), custom_call_target="tpu_custom_call" | custom-call | tf_op jit(solution)/shard_map/scan/pallas_call | solution.py:227
  124.7 24.8 %all_to_all.20.ends_ref = bf16[32,40,128]{2,1,0:T(8,128)(2,1)} all-to-all(bf16[32,40,128]{2,1,0:T(8,128)(2,1)} %get-tuple-element.20), channel_id=1, replica_groups=mesh['y'=4,'z'=8,'x'=4,'core'=2] {'y','z'}, dimensions={0} | all-to-all | bytes 655360 | tf_op jit(solution)/shard_map/all_to_all | solution.py:381
  149.5 1.8 link.1
  151.3 16.8 %all_to_all.21.start_ref = bf16[32,32,128]{2,1,0:T(8,128)(2,1)} all-to-all(bf16[32,32,128]{2,1,0:T(8,128)(2,1)} %link.1), channel_id=1, replica_groups=mesh['y'=4,'z'=8,'x'=4,'core'=2] {'y','z'}, dimensions={0} | all-to-all | bytes 524288 | tf_op jit(solution)/shard_map/all_to_all | solution.py:382
  168.1 17.5 %close.1 = bf16[128,8192]{1,0:T(8,128)(2,1)} custom-call(f32[8,1024,128]{2,1,0:T(8,128)} %get-tuple-element.17.step_ref, f32[8,1024,128]{2,1,0:T(8,128)} %get-tuple-element.18.y_ref, f32[8,128,128]{2,1,0:T(8,128)} %get-tuple-element.19.rate_ref, bf16[32,32,128]{2,1,0:T(8,128)(2,1)} %all_to_all.21.start_ref, f32[128,288]{1,0:T(8,128)} %get-tuple-element.15.mine_ref, ...), custom_call_target="tpu_custom_call" | custom-call | tf_op jit(solution)/shard_map/close/pallas_call | solution.py:301
  (55 shorter events, 15.3 us)
Async XLA Ops:
  6.5 2.1 %copy-start = (bf16[256,256]{1,0:T(8,128)(2,1)S(1)}, bf16[256,256]{1,0:T(8,128)(2,1)}, u32[]{:S(2)}) copy-start(bf16[256,256]{1,0:T(8,128)(2,1)} %param.16) | copy-start | bytes 393220
  6.5 19.7 %copy-start.5 = (bf16[256,288]{0,1:T(8,128)(2,1)S(1)}, bf16[256,288]{0,1:T(8,128)(2,1)}, u32[]{:S(2)}) copy-start(bf16[256,288]{0,1:T(8,128)(2,1)} %param.14) | copy-start | bytes 442372
  10.3 27.4 %all-to-all-start = ((bf16[8,160,256]{2,1,0:T(8,128)(2,1)}), bf16[8,160,256]{2,1,0:T(8,128)(2,1)S(1)}, u32[]{:S(2)}, u32[]{:S(2)}) async-start(bf16[8,160,256]{2,1,0:T(8,128)(2,1)} %broadcast_in_dim.45), calls=%async_computation | async-start | bytes 1310720 | tf_op jit(solution)/shard_map/all_to_all | solution.py:323
  18.9 71.5 %all-gather.2.cloned.1.call-start = ((), (), s32[]{:S(2)}) async-start(), calls=%async_computation.4 | async-start | bytes 2654208 | tf_op jit(solution)/shard_map/all_gather | solution.py:369
  19.8 8.8 %collective-permute-start.3 = (bf16[288,128]{1,0:T(8,128)(2,1)S(1)}, bf16[288,128]{1,0:T(8,128)(2,1)S(1)}, u32[]{:S(2)}, u32[]{:S(2)}) collective-permute-start(bf16[288,128]{1,0:T(8,128)(2,1)S(1)} %dynamic-slice_bitcast_fusion), channel_id=1, source_target_pairs={{0,128},{64,192},{128,0},{192,64},{1,129},{65,193},{129,1},{193,65... | collective-permute-start | bytes 221192 | tf_op jit(solution)/shard_map/ppermute | solution.py:341
  23.0 5.6 %collective-permute-start.2 = (bf16[288,128]{1,0:T(8,128)(2,1)S(1)}, bf16[288,128]{1,0:T(8,128)(2,1)S(1)}, u32[]{:S(2)}, u32[]{:S(2)}) collective-permute-start(bf16[288,128]{1,0:T(8,128)(2,1)S(1)} %dynamic-slice_bitcast_fusion), channel_id=1, source_target_pairs={{0,64},{64,128},{128,192},{192,0},{1,65},{65,129},{129,193},{193,1... | collective-permute-start | bytes 221192 | tf_op jit(solution)/shard_map/ppermute | solution.py:341
  23.6 4.9 %collective-permute-start.4 = (bf16[288,128]{1,0:T(8,128)(2,1)S(1)}, bf16[288,128]{1,0:T(8,128)(2,1)S(1)}, u32[]{:S(2)}, u32[]{:S(2)}) collective-permute-start(bf16[288,128]{1,0:T(8,128)(2,1)S(1)} %dynamic-slice_bitcast_fusion), channel_id=1, source_target_pairs={{0,192},{64,0},{128,64},{192,128},{1,193},{65,1},{129,65},{193,129... | collective-permute-start | bytes 221192 | tf_op jit(solution)/shard_map/ppermute | solution.py:341
  28.6 0.7 copy-start.2
  38.6 15.7 %collective-permute-start.6 = (bf16[8,152,256]{2,1,0:T(8,128)(2,1)}, bf16[8,152,256]{2,1,0:T(8,128)(2,1)}, u32[]{:S(2)}, u32[]{:S(2)}) collective-permute-start(bf16[8,152,256]{2,1,0:T(8,128)(2,1)} %slice.21), channel_id=1, source_target_pairs={{0,64},{64,128},{128,192},{192,0},{1,65},{65,129},{129,193},{193,1... | collective-permute-start | bytes 1867784 | tf_op jit(solution)/shard_map/ppermute | solution.py:341
  40.1 15.5 %collective-permute-start.7 = (bf16[8,152,256]{2,1,0:T(8,128)(2,1)}, bf16[8,152,256]{2,1,0:T(8,128)(2,1)}, u32[]{:S(2)}, u32[]{:S(2)}) collective-permute-start(bf16[8,152,256]{2,1,0:T(8,128)(2,1)} %slice.21), channel_id=1, source_target_pairs={{0,192},{64,0},{128,64},{192,128},{1,193},{65,1},{129,65},{193,129... | collective-permute-start | bytes 1867784 | tf_op jit(solution)/shard_map/ppermute | solution.py:341
  55.2 8.2 %collective-permute-start.8 = (bf16[4,152,256]{2,1,0:T(8,128)(2,1)S(1)}, bf16[4,152,256]{2,1,0:T(8,128)(2,1)S(1)}, u32[]{:S(2)}, u32[]{:S(2)}) collective-permute-start(bf16[4,152,256]{2,1,0:T(8,128)(2,1)S(1)} %slice.22), channel_id=1, source_target_pairs={{0,64},{64,128},{128,192},{192,0},{1,65},{65,129},{129,193},{193,1... | collective-permute-start | bytes 933896 | tf_op jit(solution)/shard_map/ppermute | solution.py:341
  56.6 7.4 %collective-permute-start.9 = (bf16[4,152,256]{2,1,0:T(8,128)(2,1)S(1)}, bf16[4,152,256]{2,1,0:T(8,128)(2,1)S(1)}, u32[]{:S(2)}, u32[]{:S(2)}) collective-permute-start(bf16[4,152,256]{2,1,0:T(8,128)(2,1)S(1)} %slice.23), channel_id=1, source_target_pairs={{0,192},{64,0},{128,64},{192,128},{1,193},{65,1},{129,65},{193,129... | collective-permute-start | bytes 933896 | tf_op jit(solution)/shard_map/ppermute | solution.py:341
  64.1 30.9 %copy-start.1 = (bf16[4,8,152,256]{3,2,1,0:T(8,128)(2,1)}, bf16[4,8,152,256]{3,2,1,0:T(8,128)(2,1)S(1)}, u32[]{:S(2)}) copy-start(bf16[4,8,152,256]{3,2,1,0:T(8,128)(2,1)S(1)} %bitcast_dynamic-update-slice_fusion.3.own_ref) | copy-start | bytes 7471108
  64.1 32.6 %collective-permute-start.10 = (bf16[4,8,152,256]{3,2,1,0:T(8,128)(2,1)S(1)}, bf16[4,8,152,256]{3,2,1,0:T(8,128)(2,1)}, u32[]{:S(2)}, u32[]{:S(2)}) collective-permute-start(bf16[4,8,152,256]{3,2,1,0:T(8,128)(2,1)S(1)} %bitcast_dynamic-update-slice_fusion.3.own_ref), channel_id=1, source_target_pairs={{0,1},{1,0},{2,3},{3,2},{4,5},{5,4},{6,7},{7,6},{8,9},{9,8},{10,11... | collective-permute-start | bytes 7471112 | tf_op jit(solution)/shard_map/ppermute | solution.py:377
  65.3 9.9 %collective-permute-start = (bf16[8,8192]{1,0:T(8,128)(2,1)S(1)}, bf16[8,8192]{1,0:T(8,128)(2,1)S(1)}, u32[]{:S(2)}, u32[]{:S(2)}) collective-permute-start(bf16[8,8192]{1,0:T(8,128)(2,1)S(1)} %slice.15), channel_id=1, source_target_pairs={{0,8},{8,16},{16,24},{24,32},{32,40},{40,48},{48,56},{56,64},{64,7... | collective-permute-start | bytes 393224 | tf_op jit(solution)/shard_map/ppermute | solution.py:368
  67.9 10.9 %all-to-all-start.1 = ((bf16[4,8,8,256]{3,2,1,0:T(8,128)(2,1)}), bf16[4,8,8,256]{3,2,1,0:T(8,128)(2,1)S(1)}, u32[]{:S(2)}, u32[]{:S(2)}) async-start(bf16[4,8,8,256]{3,2,1,0:T(8,128)(2,1)} %broadcast_in_dim.46), calls=%async_computation.1 | async-start | bytes 262144 | tf_op jit(solution)/shard_map/all_to_all | solution.py:323
  75.2 3.6 %copy-start.6 = (bf16[8,8192]{1,0:T(8,128)(2,1)}, bf16[8,8192]{1,0:T(8,128)(2,1)S(1)}, u32[]{:S(2)}) copy-start(bf16[8,8192]{1,0:T(8,128)(2,1)S(1)} %collective-permute-done.prior_ref) | copy-start | bytes 393220
  78.8 0.7 copy-start.4
  87.3 3.0 %collective-permute-start.1 = (bf16[128,4096]{1,0:T(8,128)(2,1)}, bf16[128,4096]{1,0:T(8,128)(2,1)}, u32[]{:S(2)}, u32[]{:S(2)}) collective-permute-start(bf16[128,4096]{1,0:T(8,128)(2,1)} %get-tuple-element.14), channel_id=1, source_target_pairs={{0,1},{1,0},{2,3},{3,2},{4,5},{5,4},{6,7},{7,6},{8,9},{9,8},{10,11... | collective-permute-start | bytes 3145736 | tf_op jit(solution)/shard_map/ppermute | solution.py:374
  95.0 1.7 collective-permute-start.5
  96.6 0.7 copy-start.3
Sparse Core Ops, SparseCore 0:
  29.5 42.1 all-gather.1

commit v9 on v7

--- a/solution.py
+++ b/solution.py
@@ -69,7 +69,7 @@
     )(core, conv_input, prior, params)
 
 
-AWAY = (0, -1, 1, -2, 2, -3, 3, 4, 4)
+AWAY = (0, -1, 1, -2, 2, -3, 3, 4)
 
 
 def times_rows(left, right):
@@ -81,12 +81,11 @@
     core, here = where_ref[0], where_ref[1]
     rows = xc_ref.shape[0]
     total = None
-    for k, (away, block) in enumerate(zip(AWAY, blocks)):
-        first = 2 if k == len(AWAY) - 1 else 0
+    for away, block in zip(AWAY, blocks):
         z = lax.rem(here + 8 + away, 8)
         for row in range(0, block.shape[0], 2):
             left = []
-            for y in (first + row, first + row + 1):
+            for y in (row, row + 1):
                 mine = pl.multiple_of((y * 8 + z) * SHARD + core * 128, 128)
                 lent = pl.multiple_of((y * 8 + z) * 128, 128)
                 left.append(jnp.concatenate([xc_ref[:, pl.ds(mine, 128)], lent_ref[:, pl.ds(lent, 128)]], 0))
@@ -356,6 +355,12 @@
     return out
 
 
+def from_opposite(core, up, down, axis):
+    count = lax.axis_size(axis)
+    pairs = [(2 * i + c, 2 * ((i + 1 - 2 * c) % count) + c) for i in range(count) for c in range(2)]
+    return lax.ppermute(jnp.where(core == 0, up, down), (axis, "core"), pairs)
+
+
 def both_ways(pair, axis):
     return shifted(pair[0], axis, 1), shifted(pair[1], axis, -1)
 
@@ -379,11 +384,11 @@
     xc, lend = conv(where, conv_input, prior, taps)
     x3 = both_ways(x2, "z")
     lent = lax.ppermute(lend, "core", swap)
-    x4 = both_ways((x3[0][:2], x3[1][2:]), "z")
-    d2 = both_ways((up[:4], down[4:]), "y")
-    d_own = placed([d0, up, down, *d2], [(0, 0), (-1, 0), (1, 0), (2, 0), (2, 4)], "y")
+    x4 = from_opposite(core, *x3, "z")
+    d2 = from_opposite(core, up, down, "y")
+    d_own = placed([d0, up, down, d2], [(0, 0), (-1, 0), (1, 0), (2, 0)], "y")
     d_oth = lax.ppermute(d_own, "core", swap)
-    mine, other = project(where, xc, lent, [x0, *x1, *x2, *x3, *x4])
+    mine, other = project(where, xc, lent, [x0, *x1, *x2, *x3, x4])
     other = lax.ppermute(other, "core", swap)
     step, y, rate, ends = scan(where, mine, other, dt_gain[None, :], xc, d_own, d_oth)
     ends = lax.all_to_all(ends, SEQ, split_axis=0, concat_axis=0, tiled=True)

time: 221 us -> 215 us (0.973)
  starting transfers between devices: 30.6 us -> 23.1 us
  waiting for transfers between devices: 45.7 us -> 50.3 us
  local copies, waits for them, and re-layouts: 15.9 us -> 12.7 us
    ppermute x0 -> x2, waiting for transfers between devices: none -> 16.2 us  [from_opposite(): return lax.ppermute(jnp.where(core == 0, up, down), (axis, 'core'), pairs)]
    ppermute x15 -> x11, waiting for transfers between devices: 39.6 us -> 27.2 us  [shifted(): lax.ppermute(block, axis, [(i, (i + by) % count) for i in range(count)])]
    ppermute x15 -> x11, starting transfers between devices: 24.3 us -> 15.5 us  [shifted(): lax.ppermute(block, axis, [(i, (i + by) % count) for i in range(count)])]
    dynamic_update_slice x9 -> x8, local copies, waits for them, and re-layouts: 6.31 us -> 5.35 us  [placed(): lax.dynamic_update_slice(out, block[None], ((here + by) % count, row) + (...]
  transfers between devices with their start and end apart: 20 -> 18, of which waited for: 13 -> 10; matrix products, arithmetic and copies ran while one was open for 6% -> 4% of each run, Pallas kernels for 6% -> 6%
where the time goes in v9:
time: 215 us; the launch traced here: 214 us
  blocking collectives  66.3 us (31%)
  Pallas kernels  59.1 us (27%)
  waiting for transfers between devices  50.3 us (23%)
  starting transfers between devices  23.1 us (11%)
  local copies, waits for them, and re-layouts  12.7 us (6%)
    pallas_call x1, Pallas kernels, scan(): pl.pallas_call(scan_kernel, grid_spec=grid_spec, out_shape=[jax.ShapeDtyp...  27.4 us
    all_to_all x1, blocking collectives, from_everyone(): return lax.all_to_all(copies, axis, split_axis=0, concat_axis=0, tiled=True)  27.2 us
    ppermute x11, waiting for transfers between devices, shifted(): lax.ppermute(block, axis, [(i, (i + by) % count) for i in range(count)])  27.2 us
    all_to_all x1, blocking collectives, body(): ends = lax.all_to_all(ends, SEQ, split_axis=0, concat_axis=0, tiled=True)  22.3 us
    pallas_call x1, Pallas kernels, close(): pl.pallas_call(close_kernel, grid=(inner // BLK,), in_specs=[pl.BlockSpec...  17.5 us
    all_to_all x1, blocking collectives, body(): lax.all_to_all(link(ends, a_log), SEQ, split_axis=0, concat_axis=0, tiled...  16.8 us
    ppermute x2, waiting for transfers between devices, from_opposite(): return lax.ppermute(jnp.where(core == 0, up, down), (axis, 'core'), pairs)  16.2 us
    ppermute x11, starting transfers between devices, shifted(): lax.ppermute(block, axis, [(i, (i + by) % count) for i in range(count)])  15.5 us
  transfers between devices with their start and end apart: 18, of which 10 were waited for; matrix products, arithmetic and copies ran while one was open for 4% of the time, Pallas kernels for 6%

profile of v9, /device:TPU:32, one launch (start us, length us, event | category | flops | bytes accessed | tf_op | source)
XLA Modules:
  0.0 213.9 jit_solution(9054264031395307609)
XLA Ops:
  2.9 27.2 %all_to_all.20 = bf16[8,160,256]{2,1,0:T(8,128)(2,1)S(1)} all-to-all(bf16[8,160,256]{2,1,0:T(8,128)(2,1)S(1)} %broadcast_in_dim.52), channel_id=1, replica_groups=mesh['y'=4,'z'=8,'x'=4,'core'=2] {'z'}, dimensions={0} | all-to-all | bytes 1310720 | tf_op jit(solution)/shard_map/all_to_all | solution.py:327
  31.8 1.7 collective-permute-start.14
  33.5 11.4 %collective-permute-done.13 = bf16[8,152,256]{2,1,0:T(8,128)(2,1)S(1)} collective-permute-done((bf16[8,152,256]{2,1,0:T(8,128)(2,1)S(1)}, bf16[8,152,256]{2,1,0:T(8,128)(2,1)S(1)}, u32[]{:S(2)}, u32[]{:S(2)}) %collective-permute-start.13) | collective-permute-done | bytes 622624 | tf_op jit(solution)/shard_map/ppermute | solution.py:345
  45.9 1.7 collective-permute-start.15
  48.9 8.4 %collective-permute-done.15 = bf16[8,152,256]{2,1,0:T(8,128)(2,1)S(1)} collective-permute-done((bf16[8,152,256]{2,1,0:T(8,128)(2,1)S(1)}, bf16[8,152,256]{2,1,0:T(8,128)(2,1)S(1)}, u32[]{:S(2)}, u32[]{:S(2)}) %collective-permute-start.15) | collective-permute-done | bytes 622624 | tf_op jit(solution)/shard_map/ppermute | solution.py:361
  57.6 1.9 collective-permute-start.3
  60.1 2.6 %collective-permute-start.4 = (bf16[288,128]{1,0:T(8,128)(2,1)S(1)}, bf16[288,128]{1,0:T(8,128)(2,1)}, u32[]{:S(2)}, u32[]{:S(2)}) collective-permute-start(bf16[288,128]{1,0:T(8,128)(2,1)S(1)} %dynamic-slice_bitcast_fusion), channel_id=1, source_target_pairs={{0,192},{64,0},{128,64},{192,128},{1,193},{65,1},{129,65},{193,129... | collective-permute-start | bytes 221192 | tf_op jit(solution)/shard_map/ppermute | solution.py:345
  70.1 2.4 %collective-permute-start.6 = (bf16[4,288,128]{2,1,0:T(8,128)(2,1)}, bf16[4,288,128]{2,1,0:T(8,128)(2,1)}, u32[]{:S(2)}, u32[]{:S(2)}) collective-permute-start(bf16[4,288,128]{2,1,0:T(8,128)(2,1)} %bitcast_dynamic-update-slice_fusion.5.refs_0_), channel_id=1, source_target_pairs={{0,56},{8,0},{16,8},{24,16},{32,24},{40,32},{48,40},{56,48},{1,57}... | collective-permute-start | bytes 884744 | tf_op jit(solution)/shard_map/ppermute | solution.py:345
  73.4 2.4 %collective-permute-start = (bf16[8,8192]{1,0:T(8,128)(2,1)S(1)}, bf16[8,8192]{1,0:T(8,128)(2,1)S(1)}, u32[]{:S(2)}, u32[]{:S(2)}) collective-permute-start(bf16[8,8192]{1,0:T(8,128)(2,1)S(1)} %slice.9), channel_id=1, source_target_pairs={{0,8},{8,16},{16,24},{24,32},{32,40},{40,48},{48,56},{56,64},{64,7... | collective-permute-start | bytes 393224 | tf_op jit(solution)/shard_map/ppermute | solution.py:378
  75.8 3.2 %collective-permute-done.6.refs_2_ = bf16[4,288,128]{2,1,0:T(8,128)(2,1)} collective-permute-done((bf16[4,288,128]{2,1,0:T(8,128)(2,1)}, bf16[4,288,128]{2,1,0:T(8,128)(2,1)}, u32[]{:S(2)}, u32[]{:S(2)}) %collective-permute-start.6) | collective-permute-done | bytes 294944 | tf_op jit(solution)/shard_map/ppermute | solution.py:345
  79.1 2.5 %collective-permute-start.8 = (bf16[4,288,128]{2,1,0:T(8,128)(2,1)}, bf16[4,288,128]{2,1,0:T(8,128)(2,1)}, u32[]{:S(2)}, u32[]{:S(2)}) collective-permute-start(bf16[4,288,128]{2,1,0:T(8,128)(2,1)} %collective-permute-done.6.refs_2_), channel_id=1, source_target_pairs={{0,56},{8,0},{16,8},{24,16},{32,24},{40,32},{48,40},{56,48},{1,57}... | collective-permute-start | bytes 884744 | tf_op jit(solution)/shard_map/ppermute | solution.py:345
  83.4 3.3 %all-to-all-start.1 = ((bf16[4,8,8,256]{3,2,1,0:T(8,128)(2,1)}), bf16[4,8,8,256]{3,2,1,0:T(8,128)(2,1)S(1)}, u32[]{:S(2)}, u32[]{:S(2)}) async-start(bf16[4,8,8,256]{3,2,1,0:T(8,128)(2,1)} %broadcast_in_dim.53), calls=%async_computation.1 | async-start | bytes 262144 | tf_op jit(solution)/shard_map/all_to_all | solution.py:327
  87.4 5.3 %all-to-all-done.1.par_ref = bf16[4,8,8,256]{3,2,1,0:T(8,128)(2,1)S(1)} async-done(((bf16[4,8,8,256]{3,2,1,0:T(8,128)(2,1)}), bf16[4,8,8,256]{3,2,1,0:T(8,128)(2,1)S(1)}, u32[]{:S(2)}, u32[]{:S(2)}) %all-to-all-start.1) | async-done | bytes 131104 | tf_op jit(solution)/shard_map/all_to_all | solution.py:327
  93.3 7.9 %conv.1 = (bf16[128,8192]{1,0:T(8,128)(2,1)}, bf16[128,4096]{1,0:T(8,128)(2,1)}) custom-call(s32[2]{0:T(128)} %pad_add_fusion.core_ref.where_ref, bf16[128,8192]{1,0:T(8,128)(2,1)} %ci_ref.1, bf16[8,8192]{1,0:T(8,128)(2,1)} %copy-done.11, bf16[4,8,8,256]{3,2,1,0:T(8,128)(2,1)} %copy-done.9), custom_call_target="tpu_custom_call" | custom-call | tf_op jit(solution)/shard_map/conv/pallas_call | solution.py:49
  101.3 2.0 collective-permute-start.10
  103.4 7.5 %collective-permute-done.10.refs_6_ = bf16[4,288,128]{2,1,0:T(8,128)(2,1)S(1)} collective-permute-done((bf16[4,288,128]{2,1,0:T(8,128)(2,1)}, bf16[4,288,128]{2,1,0:T(8,128)(2,1)S(1)}, u32[]{:S(2)}, u32[]{:S(2)}) %collective-permute-start.10) | collective-permute-done | bytes 294944 | tf_op jit(solution)/shard_map/ppermute | solution.py:345
  110.9 2.4 %collective-permute-done.9.refs_5_ = bf16[4,288,128]{2,1,0:T(8,128)(2,1)S(1)} collective-permute-done((bf16[4,288,128]{2,1,0:T(8,128)(2,1)}, bf16[4,288,128]{2,1,0:T(8,128)(2,1)S(1)}, u32[]{:S(2)}, u32[]{:S(2)}) %collective-permute-start.9) | collective-permute-done | bytes 294944 | tf_op jit(solution)/shard_map/ppermute | solution.py:345
  113.5 7.7 %collective-permute-done.11.refs_7_ = bf16[4,288,128]{2,1,0:T(8,128)(2,1)} collective-permute-done((bf16[4,288,128]{2,1,0:T(8,128)(2,1)S(1)}, bf16[4,288,128]{2,1,0:T(8,128)(2,1)}, u32[]{:S(2)}, u32[]{:S(2)}) %collective-permute-start.11) | collective-permute-done | bytes 294944 | tf_op jit(solution)/shard_map/ppermute | solution.py:361
  121.2 4.5 %project.1 = (f32[128,288]{1,0:T(8,128)}, f32[128,288]{1,0:T(8,128)}) custom-call(s32[2]{0:T(128)} %pad_add_fusion.core_ref.where_ref, bf16[128,8192]{1,0:T(8,128)(2,1)} %get-tuple-element.13.xc_ref, bf16[128,4096]{1,0:T(8,128)(2,1)} %collective-permute-done.1.lent_ref, bf16[4,288,128]{2,1,0:T(8,128)(2,1)} %bitcast_dynamic-update-slice_fusion.5.refs_0_, ...), custom_call_target="tpu_custom_call" | custom-call | tf_op jit(solution)/shard_map/project/pallas_call | solution.py:103
  128.1 27.4 %scan.1 = (f32[8,1024,128]{2,1,0:T(8,128)}, f32[8,1024,128]{2,1,0:T(8,128)}, f32[8,128,128]{2,1,0:T(8,128)}, bf16[32,40,128]{2,1,0:T(8,128)(2,1)}) custom-call(s32[2]{0:T(128)} %pad_add_fusion.core_ref.where_ref, f32[128,288]{1,0:T(8,128)} %get-tuple-element.15.mine_ref, f32[128,288]{1,0:T(8,128)} %copy-done.8, f32[1,256]{1,0:T(1,128)} %bitcast.22, ...), custom_call_target="tpu_custom_call" | custom-call | tf_op jit(solution)/shard_map/scan/pallas_call | solution.py:231
  155.5 22.3 %all_to_all.21.ends_ref = bf16[32,40,128]{2,1,0:T(8,128)(2,1)} all-to-all(bf16[32,40,128]{2,1,0:T(8,128)(2,1)} %get-tuple-element.20), channel_id=1, replica_groups=mesh['y'=4,'z'=8,'x'=4,'core'=2] {'y','z'}, dimensions={0} | all-to-all | bytes 655360 | tf_op jit(solution)/shard_map/all_to_all | solution.py:394
  177.8 1.8 link.1
  179.6 16.8 %all_to_all.22.start_ref = bf16[32,32,128]{2,1,0:T(8,128)(2,1)} all-to-all(bf16[32,32,128]{2,1,0:T(8,128)(2,1)} %link.1), channel_id=1, replica_groups=mesh['y'=4,'z'=8,'x'=4,'core'=2] {'y','z'}, dimensions={0} | all-to-all | bytes 524288 | tf_op jit(solution)/shard_map/all_to_all | solution.py:395
  196.4 17.5 %close.1 = bf16[128,8192]{1,0:T(8,128)(2,1)} custom-call(f32[8,1024,128]{2,1,0:T(8,128)} %get-tuple-element.17.step_ref, f32[8,1024,128]{2,1,0:T(8,128)} %get-tuple-element.18.y_ref, f32[8,128,128]{2,1,0:T(8,128)} %get-tuple-element.19.rate_ref, bf16[32,32,128]{2,1,0:T(8,128)(2,1)} %all_to_all.22.start_ref, f32[128,288]{1,0:T(8,128)} %get-tuple-element.15.mine_ref, ...), custom_call_target="tpu_custom_call" | custom-call | tf_op jit(solution)/shard_map/close/pallas_call | solution.py:305
  (72 shorter events, 21.8 us)
Async XLA Ops:
  0.0 2.1 copy-start
  30.2 14.7 %collective-permute-start.13 = (bf16[8,152,256]{2,1,0:T(8,128)(2,1)S(1)}, bf16[8,152,256]{2,1,0:T(8,128)(2,1)S(1)}, u32[]{:S(2)}, u32[]{:S(2)}) collective-permute-start(bf16[8,152,256]{2,1,0:T(8,128)(2,1)S(1)} %slice.13), channel_id=1, source_target_pairs={{0,64},{64,128},{128,192},{192,0},{1,65},{65,129},{129,193},{193,1... | collective-permute-start | bytes 1867784 | tf_op jit(solution)/shard_map/ppermute | solution.py:345
  31.8 13.1 %collective-permute-start.14 = (bf16[8,152,256]{2,1,0:T(8,128)(2,1)S(1)}, bf16[8,152,256]{2,1,0:T(8,128)(2,1)S(1)}, u32[]{:S(2)}, u32[]{:S(2)}) collective-permute-start(bf16[8,152,256]{2,1,0:T(8,128)(2,1)S(1)} %slice.13), channel_id=1, source_target_pairs={{0,192},{64,0},{128,64},{192,128},{1,193},{65,1},{129,65},{193,129... | collective-permute-start | bytes 1867784 | tf_op jit(solution)/shard_map/ppermute | solution.py:345
  45.9 11.4 %collective-permute-start.15 = (bf16[8,152,256]{2,1,0:T(8,128)(2,1)S(1)}, bf16[8,152,256]{2,1,0:T(8,128)(2,1)S(1)}, u32[]{:S(2)}, u32[]{:S(2)}) collective-permute-start(bf16[8,152,256]{2,1,0:T(8,128)(2,1)S(1)} %broadcast_select_fusion), channel_id=1, source_target_pairs={{0,64},{1,193},{64,128},{65,1},{128,192},{129,65},{192,0},{193,129... | collective-permute-start | bytes 1867784 | tf_op jit(solution)/shard_map/ppermute | solution.py:361
  47.8 9.7 %copy-start.10 = (bf16[256,288]{0,1:T(8,128)(2,1)S(1)}, bf16[256,288]{0,1:T(8,128)(2,1)}, u32[]{:S(2)}) copy-start(bf16[256,288]{0,1:T(8,128)(2,1)} %param.14) | copy-start | bytes 442372
  57.4 55.9 %copy-start.1 = (bf16[4,8,152,256]{3,2,1,0:T(8,128)(2,1)}, bf16[4,8,152,256]{3,2,1,0:T(8,128)(2,1)S(1)}, u32[]{:S(2)}) copy-start(bf16[4,8,152,256]{3,2,1,0:T(8,128)(2,1)S(1)} %bitcast_dynamic-update-slice_fusion.own_ref) | copy-start | bytes 7471108
  57.4 70.0 %collective-permute-start.16 = (bf16[4,8,152,256]{3,2,1,0:T(8,128)(2,1)S(1)}, bf16[4,8,152,256]{3,2,1,0:T(8,128)(2,1)}, u32[]{:S(2)}, u32[]{:S(2)}) collective-permute-start(bf16[4,8,152,256]{3,2,1,0:T(8,128)(2,1)S(1)} %bitcast_dynamic-update-slice_fusion.own_ref), channel_id=1, source_target_pairs={{0,1},{1,0},{2,3},{3,2},{4,5},{5,4},{6,7},{7,6},{8,9},{9,8},{10,11... | collective-permute-start | bytes 7471112 | tf_op jit(solution)/shard_map/ppermute | solution.py:390
  57.6 9.5 %collective-permute-start.3 = (bf16[288,128]{1,0:T(8,128)(2,1)S(1)}, bf16[288,128]{1,0:T(8,128)(2,1)}, u32[]{:S(2)}, u32[]{:S(2)}) collective-permute-start(bf16[288,128]{1,0:T(8,128)(2,1)S(1)} %dynamic-slice_bitcast_fusion), channel_id=1, source_target_pairs={{0,128},{64,192},{128,0},{192,64},{1,129},{65,193},{129,1},{193,65... | collective-permute-start | bytes 221192 | tf_op jit(solution)/shard_map/ppermute | solution.py:345
  59.4 6.1 %collective-permute-start.2 = (bf16[288,128]{1,0:T(8,128)(2,1)S(1)}, bf16[288,128]{1,0:T(8,128)(2,1)}, u32[]{:S(2)}, u32[]{:S(2)}) collective-permute-start(bf16[288,128]{1,0:T(8,128)(2,1)S(1)} %dynamic-slice_bitcast_fusion), channel_id=1, source_target_pairs={{0,64},{64,128},{128,192},{192,0},{1,65},{65,129},{129,193},{193,1... | collective-permute-start | bytes 221192 | tf_op jit(solution)/shard_map/ppermute | solution.py:345
  60.1 8.5 %collective-permute-start.4 = (bf16[288,128]{1,0:T(8,128)(2,1)S(1)}, bf16[288,128]{1,0:T(8,128)(2,1)}, u32[]{:S(2)}, u32[]{:S(2)}) collective-permute-start(bf16[288,128]{1,0:T(8,128)(2,1)S(1)} %dynamic-slice_bitcast_fusion), channel_id=1, source_target_pairs={{0,192},{64,0},{128,64},{192,128},{1,193},{65,1},{129,65},{193,129... | collective-permute-start | bytes 221192 | tf_op jit(solution)/shard_map/ppermute | solution.py:345
  70.1 9.0 %collective-permute-start.6 = (bf16[4,288,128]{2,1,0:T(8,128)(2,1)}, bf16[4,288,128]{2,1,0:T(8,128)(2,1)}, u32[]{:S(2)}, u32[]{:S(2)}) collective-permute-start(bf16[4,288,128]{2,1,0:T(8,128)(2,1)} %bitcast_dynamic-update-slice_fusion.5.refs_0_), channel_id=1, source_target_pairs={{0,56},{8,0},{16,8},{24,16},{32,24},{40,32},{48,40},{56,48},{1,57}... | collective-permute-start | bytes 884744 | tf_op jit(solution)/shard_map/ppermute | solution.py:345
  72.5 10.2 %collective-permute-start.5 = (bf16[4,288,128]{2,1,0:T(8,128)(2,1)}, bf16[4,288,128]{2,1,0:T(8,128)(2,1)}, u32[]{:S(2)}, u32[]{:S(2)}) collective-permute-start(bf16[4,288,128]{2,1,0:T(8,128)(2,1)} %bitcast_dynamic-update-slice_fusion.5.refs_0_), channel_id=1, source_target_pairs={{0,8},{8,16},{16,24},{24,32},{32,40},{40,48},{48,56},{56,0},{1,9},... | collective-permute-start | bytes 884744 | tf_op jit(solution)/shard_map/ppermute | solution.py:345
  73.4 14.0 %collective-permute-start = (bf16[8,8192]{1,0:T(8,128)(2,1)S(1)}, bf16[8,8192]{1,0:T(8,128)(2,1)S(1)}, u32[]{:S(2)}, u32[]{:S(2)}) collective-permute-start(bf16[8,8192]{1,0:T(8,128)(2,1)S(1)} %slice.9), channel_id=1, source_target_pairs={{0,8},{8,16},{16,24},{24,32},{32,40},{40,48},{48,56},{56,64},{64,7... | collective-permute-start | bytes 393224 | tf_op jit(solution)/shard_map/ppermute | solution.py:378
  79.1 22.2 %collective-permute-start.8 = (bf16[4,288,128]{2,1,0:T(8,128)(2,1)}, bf16[4,288,128]{2,1,0:T(8,128)(2,1)}, u32[]{:S(2)}, u32[]{:S(2)}) collective-permute-start(bf16[4,288,128]{2,1,0:T(8,128)(2,1)} %collective-permute-done.6.refs_2_), channel_id=1, source_target_pairs={{0,56},{8,0},{16,8},{24,16},{32,24},{40,32},{48,40},{56,48},{1,57}... | collective-permute-start | bytes 884744 | tf_op jit(solution)/shard_map/ppermute | solution.py:345
  82.7 20.6 %collective-permute-start.7 = (bf16[4,288,128]{2,1,0:T(8,128)(2,1)}, bf16[4,288,128]{2,1,0:T(8,128)(2,1)}, u32[]{:S(2)}, u32[]{:S(2)}) collective-permute-start(bf16[4,288,128]{2,1,0:T(8,128)(2,1)} %collective-permute-done.5.refs_1_), channel_id=1, source_target_pairs={{0,8},{8,16},{16,24},{24,32},{32,40},{40,48},{48,56},{56,0},{1,9},... | collective-permute-start | bytes 884744 | tf_op jit(solution)/shard_map/ppermute | solution.py:345
  83.4 9.3 %all-to-all-start.1 = ((bf16[4,8,8,256]{3,2,1,0:T(8,128)(2,1)}), bf16[4,8,8,256]{3,2,1,0:T(8,128)(2,1)S(1)}, u32[]{:S(2)}, u32[]{:S(2)}) async-start(bf16[4,8,8,256]{3,2,1,0:T(8,128)(2,1)} %broadcast_in_dim.53), calls=%async_computation.1 | async-start | bytes 262144 | tf_op jit(solution)/shard_map/all_to_all | solution.py:327
  87.4 5.3 %copy-start.11 = (bf16[8,8192]{1,0:T(8,128)(2,1)}, bf16[8,8192]{1,0:T(8,128)(2,1)S(1)}, u32[]{:S(2)}) copy-start(bf16[8,8192]{1,0:T(8,128)(2,1)S(1)} %collective-permute-done.prior_ref) | copy-start | bytes 393220
  101.3 19.9 %collective-permute-start.1 = (bf16[128,4096]{1,0:T(8,128)(2,1)}, bf16[128,4096]{1,0:T(8,128)(2,1)}, u32[]{:S(2)}, u32[]{:S(2)}) collective-permute-start(bf16[128,4096]{1,0:T(8,128)(2,1)} %get-tuple-element.14), channel_id=1, source_target_pairs={{0,1},{1,0},{2,3},{3,2},{4,5},{5,4},{6,7},{7,6},{8,9},{9,8},{10,11... | collective-permute-start | bytes 3145736 | tf_op jit(solution)/shard_map/ppermute | solution.py:386
  101.3 9.6 %collective-permute-start.10 = (bf16[4,288,128]{2,1,0:T(8,128)(2,1)}, bf16[4,288,128]{2,1,0:T(8,128)(2,1)S(1)}, u32[]{:S(2)}, u32[]{:S(2)}) collective-permute-start(bf16[4,288,128]{2,1,0:T(8,128)(2,1)} %collective-permute-done.8.refs_4_), channel_id=1, source_target_pairs={{0,56},{8,0},{16,8},{24,16},{32,24},{40,32},{48,40},{56,48},{1,57}... | collective-permute-start | bytes 884744 | tf_op jit(solution)/shard_map/ppermute | solution.py:345
  103.3 10.0 %collective-permute-start.9 = (bf16[4,288,128]{2,1,0:T(8,128)(2,1)}, bf16[4,288,128]{2,1,0:T(8,128)(2,1)S(1)}, u32[]{:S(2)}, u32[]{:S(2)}) collective-permute-start(bf16[4,288,128]{2,1,0:T(8,128)(2,1)} %collective-permute-done.7.refs_3_), channel_id=1, source_target_pairs={{0,8},{8,16},{16,24},{24,32},{32,40},{40,48},{48,56},{56,0},{1,9},... | collective-permute-start | bytes 884744 | tf_op jit(solution)/shard_map/ppermute | solution.py:345
  110.9 10.3 %copy-start.6 = (bf16[4,288,128]{2,1,0:T(8,128)(2,1)}, bf16[4,288,128]{2,1,0:T(8,128)(2,1)S(1)}, u32[]{:S(2)}) copy-start(bf16[4,288,128]{2,1,0:T(8,128)(2,1)S(1)} %collective-permute-done.10.refs_6_) | copy-start | bytes 884740
  113.3 7.9 %copy-start.7 = (bf16[4,288,128]{2,1,0:T(8,128)(2,1)}, bf16[4,288,128]{2,1,0:T(8,128)(2,1)S(1)}, u32[]{:S(2)}) copy-start(bf16[4,288,128]{2,1,0:T(8,128)(2,1)S(1)} %collective-permute-done.9.refs_5_) | copy-start | bytes 884740
  113.4 7.8 %collective-permute-start.11 = (bf16[4,288,128]{2,1,0:T(8,128)(2,1)S(1)}, bf16[4,288,128]{2,1,0:T(8,128)(2,1)}, u32[]{:S(2)}, u32[]{:S(2)}) collective-permute-start(bf16[4,288,128]{2,1,0:T(8,128)(2,1)S(1)} %broadcast_select_fusion.1), channel_id=1, source_target_pairs={{0,8},{1,57},{8,16},{9,1},{16,24},{17,9},{24,32},{25,17},{32,40},{... | collective-permute-start | bytes 884744 | tf_op jit(solution)/shard_map/ppermute | solution.py:361
  125.8 1.7 collective-permute-start.12
  (6 other events, 5.5 us)

commit v10 on v9

--- a/solution.py
+++ b/solution.py
@@ -115,6 +115,15 @@
         out_ref[m * rows : (m + 1) * rows, :] = jnp.broadcast_to(proj[:, first + m : first + m + 1], (rows, 128))
 
 
+def joined(ref, s):
+    return jnp.concatenate([ref[0, q, s, 0:32, :] for q in range(4)], 0)
+
+
+def extras(ref, s):
+    parts = [ref[0, q, s, 32:40, :].astype(F32) for q in range(4)]
+    return jnp.concatenate([p[0:2] + p[2:4] for p in parts], 0), parts[0][4:5] + parts[0][5:6]
+
+
 def scan_kernel(where_ref, mine_ref, other_ref, gain_ref, xc_ref, own_ref, oth_ref, step_ref, y_ref, rate_ref, ends_ref, *scratch):
     x_scr, par_scr, h_scr, normed_ref, bc_ref = scratch
     core = where_ref[0]
@@ -133,14 +142,10 @@
     other_k = normed_ref[:, pl.ds(pl.multiple_of((1 - core) * 128, 128), 128)]
     skips = []
     for s in range(4):
-        raw = jnp.dot(mine_k, own_ref[0, s, 0:128, :], preferred_element_type=F32)
-        raw = raw + jnp.dot(other_k, oth_ref[0, s, 0:128, :], preferred_element_type=F32)
-        mine = own_ref[0, s, 128:152, :].astype(F32)
-        other = oth_ref[0, s, 128:152, :].astype(F32)
-        mine_log = mine[0:8] + mine[8:16]
-        other_log = other[0:8] + other[8:16]
-        mine_vec = mine[16:17] + mine[17:18]
-        other_vec = other[16:17] + other[17:18]
+        raw = jnp.dot(mine_k, joined(own_ref, s), preferred_element_type=F32)
+        raw = raw + jnp.dot(other_k, joined(oth_ref, s), preferred_element_type=F32)
+        mine_log, mine_vec = extras(own_ref, s)
+        other_log, other_vec = extras(oth_ref, s)
         bias = jnp.where(core == 0, mine_vec, other_vec)
         skip = jnp.where(core == 0, other_vec, mine_vec)
         raw = raw + bias
@@ -202,7 +207,7 @@
 def scan(where, mine, other, gain, xc, d_own, d_oth):
     rows, inner = xc.shape
     blocks = inner // BLK
-    wspec = pl.BlockSpec((1, 4, 152, 256), lambda b, where: (b // 2, b % 2, 0, 0))
+    wspec = pl.BlockSpec((1, 4, 4, 40, 256), lambda b, where: (b // 2, 0, b % 2, 0, 0))
     grid_spec = pltpu.PrefetchScalarGridSpec(
         num_scalar_prefetch=1,
         grid=(blocks,),
@@ -331,11 +336,11 @@
     return lax.dynamic_slice_in_dim(x_weight.T, core * 128, 128, 1)
 
 
-def pack_d(core, dt_weight, dt_bias, a_log, skip, conv_weight, conv_bias):
-    half = lax.dynamic_slice_in_dim(dt_weight, core * 128, 128, 0)
-    logs = lax.dynamic_slice_in_dim(a_log, core * 8, 8, 0)
+def pack_d(core, quarter, dt_weight, dt_bias, a_log, skip, conv_weight, conv_bias):
+    part = lax.dynamic_slice_in_dim(dt_weight, core * 128 + quarter * 32, 32, 0)
+    logs = lax.dynamic_slice_in_dim(a_log, core * 8 + quarter * 2, 2, 0)
     vec = jnp.where(core == 0, dt_bias, skip)[None, :]
-    pieces = [half, *two_parts(logs), *two_parts(vec), jnp.zeros((6, SHARD), BF16)]
+    pieces = [part, *two_parts(logs), *two_parts(vec), jnp.zeros((2, SHARD), BF16)]
     pieces += [conv_weight, conv_bias[None, :], jnp.zeros((3, SHARD), BF16)]
     return jnp.concatenate(pieces, 0)
 
@@ -373,13 +378,14 @@
     x_piece = pack_x(core, x_weight)
     x_pieces = [x_piece] + [shifted(x_piece, "y", k) for k in (1, 2, 3)]
     x0 = placed(x_pieces, [(0, 0), (-1, 0), (-2, 0), (-3, 0)], "y")
-    d_part = from_everyone(pack_d(core, dt_weight, dt_bias, a_log, skip, conv_weight, conv_bias), "z")
-    d_part = d_part.reshape(8, 160, SHARD)
+    quarter = lax.axis_index("x")
+    d_part = from_everyone(pack_d(core, quarter, dt_weight, dt_bias, a_log, skip, conv_weight, conv_bias), "z")
+    d_part = d_part.reshape(8, 48, SHARD)
     prior = lax.ppermute(conv_input[conv_input.shape[0] - 8 :], SEQ, [(i, i + 1) for i in range(count - 1)])
     x1 = both_ways((x0, x0), "z")
-    taps = from_everyone(d_part[:, 152:], "y").reshape(4, 8, 8, SHARD)
+    taps = from_everyone(d_part[:, 40:], "y").reshape(4, 8, 8, SHARD)
     x2 = both_ways(x1, "z")
-    d0 = d_part[:, :152]
+    d0 = from_everyone(d_part[:, :40], "x").reshape(4, 8, 40, SHARD)
     up, down = both_ways((d0, d0), "y")
     xc, lend = conv(where, conv_input, prior, taps)
     x3 = both_ways(x2, "z")

time: 215 us -> 212 us (0.986)
  blocking collectives: 66.3 us -> 70.4 us
  waiting for transfers between devices: 50.3 us -> 47.3 us
  local copies, waits for them, and re-layouts: 12.7 us -> 9.94 us
    dynamic_update_slice x8, local copies, waits for them, and re-layouts: 5.35 us -> 1.15 us  [placed(): lax.dynamic_update_slice(out, block[None], ((here + by) % count, row) + (...]
    all_to_all x1, waiting for transfers between devices: 5.29 us -> 1.95 us  [from_everyone(): return lax.all_to_all(copies, axis, split_axis=0, concat_axis=0, tiled=True)]
    all_to_all x1 -> x2, blocking collectives: 27.2 us -> 30.3 us  [from_everyone(): return lax.all_to_all(copies, axis, split_axis=0, concat_axis=0, tiled=True)]
  transfers between devices with their start and end apart: 18 -> 18, of which waited for: 10 -> 10; matrix products, arithmetic and copies ran while one was open for 4% -> 2% of each run, Pallas kernels for 6% -> 6%
where the time goes in v10:
time: 212 us; the launch traced here: 211 us
  blocking collectives  70.4 us (33%)
  Pallas kernels  59.2 us (28%)
  waiting for transfers between devices  47.3 us (22%)
  starting transfers between devices  21.9 us (10%)
  local copies, waits for them, and re-layouts  9.94 us (5%)
  other arithmetic  2.15 us (1%)
    all_to_all x2, blocking collectives, from_everyone(): return lax.all_to_all(copies, axis, split_axis=0, concat_axis=0, tiled=True)  30.3 us
    pallas_call x1, Pallas kernels, scan(): pl.pallas_call(scan_kernel, grid_spec=grid_spec, out_shape=[jax.ShapeDtyp...  27.5 us
    ppermute x11, waiting for transfers between devices, shifted(): lax.ppermute(block, axis, [(i, (i + by) % count) for i in range(count)])  26.3 us
    all_to_all x1, blocking collectives, body(): ends = lax.all_to_all(ends, SEQ, split_axis=0, concat_axis=0, tiled=True)  23.3 us
    pallas_call x1, Pallas kernels, close(): pl.pallas_call(close_kernel, grid=(inner // BLK,), in_specs=[pl.BlockSpec...  17.5 us
    ppermute x2, waiting for transfers between devices, from_opposite(): return lax.ppermute(jnp.where(core == 0, up, down), (axis, 'core'), pairs)  17.4 us
    all_to_all x1, blocking collectives, body(): lax.all_to_all(link(ends, a_log), SEQ, split_axis=0, concat_axis=0, tiled...  16.8 us
    ppermute x11, starting transfers between devices, shifted(): lax.ppermute(block, axis, [(i, (i + by) % count) for i in range(count)])  15 us
  transfers between devices with their start and end apart: 18, of which 10 were waited for; matrix products, arithmetic and copies ran while one was open for 2% of the time, Pallas kernels for 6%

profile of v10, /device:TPU:32, one launch (start us, length us, event | category | flops | bytes accessed | tf_op | source)
XLA Modules:
  0.0 211.1 jit_solution(6307824893034150097)
XLA Ops:
  2.9 17.4 %all_to_all.25 = bf16[8,48,256]{2,1,0:T(8,128)(2,1)S(1)} all-to-all(bf16[8,48,256]{2,1,0:T(8,128)(2,1)S(1)} %broadcast_in_dim.55), channel_id=1, replica_groups=mesh['y'=4,'z'=8,'x'=4,'core'=2] {'z'}, dimensions={0} | all-to-all | bytes 393216 | tf_op jit(solution)/shard_map/all_to_all | solution.py:332
  21.0 12.9 %all_to_all.26 = bf16[4,8,40,256]{3,2,1,0:T(8,128)(2,1)S(1)} all-to-all(bf16[4,8,40,256]{3,2,1,0:T(8,128)(2,1)S(1)} %broadcast_in_dim.64), channel_id=1, replica_groups=mesh['y'=4,'z'=8,'x'=4,'core'=2] {'x'}, dimensions={0} | all-to-all | bytes 1310720 | tf_op jit(solution)/shard_map/all_to_all | solution.py:332
  33.9 3.0 %collective-permute-start.14 = (bf16[4,8,40,256]{3,2,1,0:T(8,128)(2,1)S(1)}, bf16[4,8,40,256]{3,2,1,0:T(8,128)(2,1)S(1)}, u32[]{:S(2)}, u32[]{:S(2)}) collective-permute-start(bf16[4,8,40,256]{3,2,1,0:T(8,128)(2,1)S(1)} %all_to_all.26), channel_id=1, source_target_pairs={{0,192},{64,0},{128,64},{192,128},{1,193},{65,1},{129,65},{193,129... | collective-permute-start | bytes 1966088 | tf_op jit(solution)/shard_map/ppermute | solution.py:350
  36.9 10.5 %collective-permute-done.14 = bf16[4,8,40,256]{3,2,1,0:T(8,128)(2,1)S(1)} collective-permute-done((bf16[4,8,40,256]{3,2,1,0:T(8,128)(2,1)S(1)}, bf16[4,8,40,256]{3,2,1,0:T(8,128)(2,1)S(1)}, u32[]{:S(2)}, u32[]{:S(2)}) %collective-permute-start.14) | collective-permute-done | bytes 655392 | tf_op jit(solution)/shard_map/ppermute | solution.py:350
  47.4 3.4 %collective-permute-done.13 = bf16[4,8,40,256]{3,2,1,0:T(8,128)(2,1)S(1)} collective-permute-done((bf16[4,8,40,256]{3,2,1,0:T(8,128)(2,1)S(1)}, bf16[4,8,40,256]{3,2,1,0:T(8,128)(2,1)S(1)}, u32[]{:S(2)}, u32[]{:S(2)}) %collective-permute-start.13) | collective-permute-done | bytes 655392 | tf_op jit(solution)/shard_map/ppermute | solution.py:350
  53.1 10.4 %collective-permute-done.15 = bf16[4,8,40,256]{3,2,1,0:T(8,128)(2,1)S(1)} collective-permute-done((bf16[4,8,40,256]{3,2,1,0:T(8,128)(2,1)S(1)}, bf16[4,8,40,256]{3,2,1,0:T(8,128)(2,1)S(1)}, u32[]{:S(2)}, u32[]{:S(2)}) %collective-permute-start.15) | collective-permute-done | bytes 655392 | tf_op jit(solution)/shard_map/ppermute | solution.py:366
  65.0 2.9 %collective-permute-start.4 = (bf16[288,128]{1,0:T(8,128)(2,1)S(1)}, bf16[288,128]{1,0:T(8,128)(2,1)S(1)}, u32[]{:S(2)}, u32[]{:S(2)}) collective-permute-start(bf16[288,128]{1,0:T(8,128)(2,1)S(1)} %dynamic-slice_bitcast_fusion), channel_id=1, source_target_pairs={{0,192},{64,0},{128,64},{192,128},{1,193},{65,1},{129,65},{193,129... | collective-permute-start | bytes 221192 | tf_op jit(solution)/shard_map/ppermute | solution.py:350
  68.9 3.2 %collective-permute-done.2 = bf16[288,128]{1,0:T(8,128)(2,1)S(1)} collective-permute-done((bf16[288,128]{1,0:T(8,128)(2,1)S(1)}, bf16[288,128]{1,0:T(8,128)(2,1)S(1)}, u32[]{:S(2)}, u32[]{:S(2)}) %collective-permute-start.2) | collective-permute-done | bytes 73760 | tf_op jit(solution)/shard_map/ppermute | solution.py:350
  72.2 2.2 %collective-permute-start.6 = (bf16[4,288,128]{2,1,0:T(8,128)(2,1)S(1)}, bf16[4,288,128]{2,1,0:T(8,128)(2,1)}, u32[]{:S(2)}, u32[]{:S(2)}) collective-permute-start(bf16[4,288,128]{2,1,0:T(8,128)(2,1)S(1)} %bitcast_dynamic-update-slice_fusion.5.refs_0_), channel_id=1, source_target_pairs={{0,56},{8,0},{16,8},{24,16},{32,24},{40,32},{48,40},{56,48},{1,57}... | collective-permute-start | bytes 884744 | tf_op jit(solution)/shard_map/ppermute | solution.py:350
  75.9 2.7 %collective-permute-start = (bf16[8,8192]{1,0:T(8,128)(2,1)}, bf16[8,8192]{1,0:T(8,128)(2,1)S(1)}, u32[]{:S(2)}, u32[]{:S(2)}) collective-permute-start(bf16[8,8192]{1,0:T(8,128)(2,1)} %slice.9), channel_id=1, source_target_pairs={{0,8},{8,16},{16,24},{24,32},{32,40},{40,48},{48,56},{56,64},{64,7... | collective-permute-start | bytes 393224 | tf_op jit(solution)/shard_map/ppermute | solution.py:384
  79.3 3.3 %all-to-all-start.1 = ((bf16[4,8,8,256]{3,2,1,0:T(8,128)(2,1)}), bf16[4,8,8,256]{3,2,1,0:T(8,128)(2,1)S(1)}, u32[]{:S(2)}, u32[]{:S(2)}) async-start(bf16[4,8,8,256]{3,2,1,0:T(8,128)(2,1)} %broadcast_in_dim.56), calls=%async_computation.1 | async-start | bytes 262144 | tf_op jit(solution)/shard_map/all_to_all | solution.py:332
  84.3 1.6 collective-permute-start.7
  86.6 1.9 all-to-all-done.1.par_ref
  89.2 7.9 %conv.1 = (bf16[128,8192]{1,0:T(8,128)(2,1)}, bf16[128,4096]{1,0:T(8,128)(2,1)}) custom-call(s32[2]{0:T(128)} %pad_add_fusion.core_ref.where_ref, bf16[128,8192]{1,0:T(8,128)(2,1)} %ci_ref.1, bf16[8,8192]{1,0:T(8,128)(2,1)} %copy-done.12, bf16[4,8,8,256]{3,2,1,0:T(8,128)(2,1)} %copy-done.11), custom_call_target="tpu_custom_call" | custom-call | tf_op jit(solution)/shard_map/conv/pallas_call | solution.py:49
  98.4 2.2 %collective-permute-start.9 = (bf16[4,288,128]{2,1,0:T(8,128)(2,1)}, bf16[4,288,128]{2,1,0:T(8,128)(2,1)S(1)}, u32[]{:S(2)}, u32[]{:S(2)}) collective-permute-start(bf16[4,288,128]{2,1,0:T(8,128)(2,1)} %collective-permute-done.7.refs_3_), channel_id=1, source_target_pairs={{0,8},{8,16},{16,24},{24,32},{32,40},{40,48},{48,56},{56,0},{1,9},... | collective-permute-start | bytes 884744 | tf_op jit(solution)/shard_map/ppermute | solution.py:350
  100.6 7.5 %collective-permute-done.10.refs_6_ = bf16[4,288,128]{2,1,0:T(8,128)(2,1)S(1)} collective-permute-done((bf16[4,288,128]{2,1,0:T(8,128)(2,1)}, bf16[4,288,128]{2,1,0:T(8,128)(2,1)S(1)}, u32[]{:S(2)}, u32[]{:S(2)}) %collective-permute-start.10) | collective-permute-done | bytes 294944 | tf_op jit(solution)/shard_map/ppermute | solution.py:350
  110.3 7.1 %collective-permute-done.11.refs_7_ = bf16[4,288,128]{2,1,0:T(8,128)(2,1)} collective-permute-done((bf16[4,288,128]{2,1,0:T(8,128)(2,1)S(1)}, bf16[4,288,128]{2,1,0:T(8,128)(2,1)}, u32[]{:S(2)}, u32[]{:S(2)}) %collective-permute-start.11) | collective-permute-done | bytes 294944 | tf_op jit(solution)/shard_map/ppermute | solution.py:366
  117.3 4.5 %project.1 = (f32[128,288]{1,0:T(8,128)}, f32[128,288]{1,0:T(8,128)}) custom-call(s32[2]{0:T(128)} %pad_add_fusion.core_ref.where_ref, bf16[128,8192]{1,0:T(8,128)(2,1)} %get-tuple-element.13.xc_ref, bf16[128,4096]{1,0:T(8,128)(2,1)} %collective-permute-done.1.lent_ref, bf16[4,288,128]{2,1,0:T(8,128)(2,1)} %copy-done.8, ...), custom_call_target="tpu_custom_call" | custom-call | tf_op jit(solution)/shard_map/project/pallas_call | solution.py:103
  121.9 1.6 collective-permute-done.12.other_ref
  124.2 27.5 %scan.1 = (f32[8,1024,128]{2,1,0:T(8,128)}, f32[8,1024,128]{2,1,0:T(8,128)}, f32[8,128,128]{2,1,0:T(8,128)}, bf16[32,40,128]{2,1,0:T(8,128)(2,1)}) custom-call(s32[2]{0:T(128)} %pad_add_fusion.core_ref.where_ref, f32[128,288]{1,0:T(8,128)} %get-tuple-element.15.mine_ref, f32[128,288]{1,0:T(8,128)} %copy-done.10, f32[1,256]{1,0:T(1,128)} %bitcast.22, ...), custom_call_target="tpu_custom_call" | custom-call | tf_op jit(solution)/shard_map/scan/pallas_call | solution.py:236
  151.7 23.3 %all_to_all.27.ends_ref = bf16[32,40,128]{2,1,0:T(8,128)(2,1)} all-to-all(bf16[32,40,128]{2,1,0:T(8,128)(2,1)} %get-tuple-element.20), channel_id=1, replica_groups=mesh['y'=4,'z'=8,'x'=4,'core'=2] {'y','z'}, dimensions={0} | all-to-all | bytes 655360 | tf_op jit(solution)/shard_map/all_to_all | solution.py:400
  175.0 1.8 link.1
  176.8 16.8 %all_to_all.28.start_ref = bf16[32,32,128]{2,1,0:T(8,128)(2,1)} all-to-all(bf16[32,32,128]{2,1,0:T(8,128)(2,1)} %link.1), channel_id=1, replica_groups=mesh['y'=4,'z'=8,'x'=4,'core'=2] {'y','z'}, dimensions={0} | all-to-all | bytes 524288 | tf_op jit(solution)/shard_map/all_to_all | solution.py:401
  193.6 17.5 %close.1 = bf16[128,8192]{1,0:T(8,128)(2,1)} custom-call(f32[8,1024,128]{2,1,0:T(8,128)} %get-tuple-element.17.step_ref, f32[8,1024,128]{2,1,0:T(8,128)} %get-tuple-element.18.y_ref, f32[8,128,128]{2,1,0:T(8,128)} %get-tuple-element.19.rate_ref, bf16[32,32,128]{2,1,0:T(8,128)(2,1)} %all_to_all.28.start_ref, f32[128,288]{1,0:T(8,128)} %get-tuple-element.15.mine_ref, ...), custom_call_target="tpu_custom_call" | custom-call | tf_op jit(solution)/shard_map/close/pallas_call | solution.py:310
  (77 shorter events, 17.8 us)
Async XLA Ops:
  33.9 17.0 %copy-start.2 = (bf16[4,8,40,256]{3,2,1,0:T(8,128)(2,1)}, bf16[4,8,40,256]{3,2,1,0:T(8,128)(2,1)S(1)}, u32[]{:S(2)}) copy-start(bf16[4,8,40,256]{3,2,1,0:T(8,128)(2,1)S(1)} %all_to_all.26) | copy-start | bytes 1966084
  33.9 13.5 %collective-permute-start.14 = (bf16[4,8,40,256]{3,2,1,0:T(8,128)(2,1)S(1)}, bf16[4,8,40,256]{3,2,1,0:T(8,128)(2,1)S(1)}, u32[]{:S(2)}, u32[]{:S(2)}) collective-permute-start(bf16[4,8,40,256]{3,2,1,0:T(8,128)(2,1)S(1)} %all_to_all.26), channel_id=1, source_target_pairs={{0,192},{64,0},{128,64},{192,128},{1,193},{65,1},{129,65},{193,129... | collective-permute-start | bytes 1966088 | tf_op jit(solution)/shard_map/ppermute | solution.py:350
  36.9 13.9 %collective-permute-start.13 = (bf16[4,8,40,256]{3,2,1,0:T(8,128)(2,1)S(1)}, bf16[4,8,40,256]{3,2,1,0:T(8,128)(2,1)S(1)}, u32[]{:S(2)}, u32[]{:S(2)}) collective-permute-start(bf16[4,8,40,256]{3,2,1,0:T(8,128)(2,1)S(1)} %all_to_all.26), channel_id=1, source_target_pairs={{0,64},{64,128},{128,192},{192,0},{1,65},{65,129},{129,193},{193,1... | collective-permute-start | bytes 1966088 | tf_op jit(solution)/shard_map/ppermute | solution.py:350
  51.7 11.8 %collective-permute-start.15 = (bf16[4,8,40,256]{3,2,1,0:T(8,128)(2,1)S(1)}, bf16[4,8,40,256]{3,2,1,0:T(8,128)(2,1)S(1)}, u32[]{:S(2)}, u32[]{:S(2)}) collective-permute-start(bf16[4,8,40,256]{3,2,1,0:T(8,128)(2,1)S(1)} %broadcast_select_fusion), channel_id=1, source_target_pairs={{0,64},{1,193},{64,128},{65,1},{128,192},{129,65},{192,0},{193,129... | collective-permute-start | bytes 1966088 | tf_op jit(solution)/shard_map/ppermute | solution.py:366
  53.0 25.6 %slice-start = ((bf16[8,48,256]{2,1,0:T(8,128)(2,1)}), bf16[8,8,256]{2,1,0:T(8,128)(2,1)S(1)}, s32[]{:S(2)}) async-start(bf16[8,48,256]{2,1,0:T(8,128)(2,1)} %copy-done.9), calls=%async_computation.5 | async-start | bytes 65536 | tf_op jit(solution)/shard_map/slice | solution.py:386
  63.5 58.3 %copy-start.1 = (bf16[4,4,8,40,256]{4,3,2,1,0:T(8,128)(2,1)}, bf16[4,4,8,40,256]{4,3,2,1,0:T(8,128)(2,1)S(1)}, u32[]{:S(2)}) copy-start(bf16[4,4,8,40,256]{4,3,2,1,0:T(8,128)(2,1)S(1)} %bitcast_dynamic-update-slice_fusion.own_ref) | copy-start | bytes 7864324
  63.5 60.0 %collective-permute-start.16 = (bf16[4,4,8,40,256]{4,3,2,1,0:T(8,128)(2,1)S(1)}, bf16[4,4,8,40,256]{4,3,2,1,0:T(8,128)(2,1)}, u32[]{:S(2)}, u32[]{:S(2)}) collective-permute-start(bf16[4,4,8,40,256]{4,3,2,1,0:T(8,128)(2,1)S(1)} %bitcast_dynamic-update-slice_fusion.own_ref), channel_id=1, source_target_pairs={{0,1},{1,0},{2,3},{3,2},{4,5},{5,4},{6,7},{7,6},{8,9},{9,8},{10,11... | collective-permute-start | bytes 7864328 | tf_op jit(solution)/shard_map/ppermute | solution.py:396
  64.6 7.5 %collective-permute-start.3 = (bf16[288,128]{1,0:T(8,128)(2,1)S(1)}, bf16[288,128]{1,0:T(8,128)(2,1)S(1)}, u32[]{:S(2)}, u32[]{:S(2)}) collective-permute-start(bf16[288,128]{1,0:T(8,128)(2,1)S(1)} %dynamic-slice_bitcast_fusion), channel_id=1, source_target_pairs={{0,128},{64,192},{128,0},{192,64},{1,129},{65,193},{129,1},{193,65... | collective-permute-start | bytes 221192 | tf_op jit(solution)/shard_map/ppermute | solution.py:350
  64.6 7.4 %collective-permute-start.2 = (bf16[288,128]{1,0:T(8,128)(2,1)S(1)}, bf16[288,128]{1,0:T(8,128)(2,1)S(1)}, u32[]{:S(2)}, u32[]{:S(2)}) collective-permute-start(bf16[288,128]{1,0:T(8,128)(2,1)S(1)} %dynamic-slice_bitcast_fusion), channel_id=1, source_target_pairs={{0,64},{64,128},{128,192},{192,0},{1,65},{65,129},{129,193},{193,1... | collective-permute-start | bytes 221192 | tf_op jit(solution)/shard_map/ppermute | solution.py:350
  65.0 7.1 %collective-permute-start.4 = (bf16[288,128]{1,0:T(8,128)(2,1)S(1)}, bf16[288,128]{1,0:T(8,128)(2,1)S(1)}, u32[]{:S(2)}, u32[]{:S(2)}) collective-permute-start(bf16[288,128]{1,0:T(8,128)(2,1)S(1)} %dynamic-slice_bitcast_fusion), channel_id=1, source_target_pairs={{0,192},{64,0},{128,64},{192,128},{1,193},{65,1},{129,65},{193,129... | collective-permute-start | bytes 221192 | tf_op jit(solution)/shard_map/ppermute | solution.py:350
  72.1 24.9 %copy-start.8 = (bf16[4,288,128]{2,1,0:T(8,128)(2,1)}, bf16[4,288,128]{2,1,0:T(8,128)(2,1)S(1)}, u32[]{:S(2)}) copy-start(bf16[4,288,128]{2,1,0:T(8,128)(2,1)S(1)} %bitcast_dynamic-update-slice_fusion.5.refs_0_) | copy-start | bytes 884740
  72.2 10.4 %collective-permute-start.6 = (bf16[4,288,128]{2,1,0:T(8,128)(2,1)S(1)}, bf16[4,288,128]{2,1,0:T(8,128)(2,1)}, u32[]{:S(2)}, u32[]{:S(2)}) collective-permute-start(bf16[4,288,128]{2,1,0:T(8,128)(2,1)S(1)} %bitcast_dynamic-update-slice_fusion.5.refs_0_), channel_id=1, source_target_pairs={{0,56},{8,0},{16,8},{24,16},{32,24},{40,32},{48,40},{56,48},{1,57}... | collective-permute-start | bytes 884744 | tf_op jit(solution)/shard_map/ppermute | solution.py:350
  74.3 9.9 %collective-permute-start.5 = (bf16[4,288,128]{2,1,0:T(8,128)(2,1)S(1)}, bf16[4,288,128]{2,1,0:T(8,128)(2,1)}, u32[]{:S(2)}, u32[]{:S(2)}) collective-permute-start(bf16[4,288,128]{2,1,0:T(8,128)(2,1)S(1)} %bitcast_dynamic-update-slice_fusion.5.refs_0_), channel_id=1, source_target_pairs={{0,8},{8,16},{16,24},{24,32},{32,40},{40,48},{48,56},{56,0},{1,9},... | collective-permute-start | bytes 884744 | tf_op jit(solution)/shard_map/ppermute | solution.py:350
  75.9 10.7 %collective-permute-start = (bf16[8,8192]{1,0:T(8,128)(2,1)}, bf16[8,8192]{1,0:T(8,128)(2,1)S(1)}, u32[]{:S(2)}, u32[]{:S(2)}) collective-permute-start(bf16[8,8192]{1,0:T(8,128)(2,1)} %slice.9), channel_id=1, source_target_pairs={{0,8},{8,16},{16,24},{24,32},{32,40},{40,48},{48,56},{56,64},{64,7... | collective-permute-start | bytes 393224 | tf_op jit(solution)/shard_map/ppermute | solution.py:384
  79.3 9.3 %all-to-all-start.1 = ((bf16[4,8,8,256]{3,2,1,0:T(8,128)(2,1)}), bf16[4,8,8,256]{3,2,1,0:T(8,128)(2,1)S(1)}, u32[]{:S(2)}, u32[]{:S(2)}) async-start(bf16[4,8,8,256]{3,2,1,0:T(8,128)(2,1)} %broadcast_in_dim.56), calls=%async_computation.1 | async-start | bytes 262144 | tf_op jit(solution)/shard_map/all_to_all | solution.py:332
  82.6 14.5 %collective-permute-start.8 = (bf16[4,288,128]{2,1,0:T(8,128)(2,1)}, bf16[4,288,128]{2,1,0:T(8,128)(2,1)}, u32[]{:S(2)}, u32[]{:S(2)}) collective-permute-start(bf16[4,288,128]{2,1,0:T(8,128)(2,1)} %collective-permute-done.6.refs_2_), channel_id=1, source_target_pairs={{0,56},{8,0},{16,8},{24,16},{32,24},{40,32},{48,40},{56,48},{1,57}... | collective-permute-start | bytes 884744 | tf_op jit(solution)/shard_map/ppermute | solution.py:350
  84.3 14.2 %collective-permute-start.7 = (bf16[4,288,128]{2,1,0:T(8,128)(2,1)}, bf16[4,288,128]{2,1,0:T(8,128)(2,1)}, u32[]{:S(2)}, u32[]{:S(2)}) collective-permute-start(bf16[4,288,128]{2,1,0:T(8,128)(2,1)} %collective-permute-done.5.refs_1_), channel_id=1, source_target_pairs={{0,8},{8,16},{16,24},{24,32},{32,40},{40,48},{48,56},{56,0},{1,9},... | collective-permute-start | bytes 884744 | tf_op jit(solution)/shard_map/ppermute | solution.py:350
  97.1 20.2 %collective-permute-start.1 = (bf16[128,4096]{1,0:T(8,128)(2,1)}, bf16[128,4096]{1,0:T(8,128)(2,1)}, u32[]{:S(2)}, u32[]{:S(2)}) collective-permute-start(bf16[128,4096]{1,0:T(8,128)(2,1)} %get-tuple-element.14), channel_id=1, source_target_pairs={{0,1},{1,0},{2,3},{3,2},{4,5},{5,4},{6,7},{7,6},{8,9},{9,8},{10,11... | collective-permute-start | bytes 3145736 | tf_op jit(solution)/shard_map/ppermute | solution.py:392
  97.1 11.0 %collective-permute-start.10 = (bf16[4,288,128]{2,1,0:T(8,128)(2,1)}, bf16[4,288,128]{2,1,0:T(8,128)(2,1)S(1)}, u32[]{:S(2)}, u32[]{:S(2)}) collective-permute-start(bf16[4,288,128]{2,1,0:T(8,128)(2,1)} %collective-permute-done.8.refs_4_), channel_id=1, source_target_pairs={{0,56},{8,0},{16,8},{24,16},{32,24},{40,32},{48,40},{56,48},{1,57}... | collective-permute-start | bytes 884744 | tf_op jit(solution)/shard_map/ppermute | solution.py:350
  98.4 11.0 %collective-permute-start.9 = (bf16[4,288,128]{2,1,0:T(8,128)(2,1)}, bf16[4,288,128]{2,1,0:T(8,128)(2,1)S(1)}, u32[]{:S(2)}, u32[]{:S(2)}) collective-permute-start(bf16[4,288,128]{2,1,0:T(8,128)(2,1)} %collective-permute-done.7.refs_3_), channel_id=1, source_target_pairs={{0,8},{8,16},{16,24},{24,32},{32,40},{40,48},{48,56},{56,0},{1,9},... | collective-permute-start | bytes 884744 | tf_op jit(solution)/shard_map/ppermute | solution.py:350
  108.1 9.2 %copy-start.6 = (bf16[4,288,128]{2,1,0:T(8,128)(2,1)}, bf16[4,288,128]{2,1,0:T(8,128)(2,1)S(1)}, u32[]{:S(2)}) copy-start(bf16[4,288,128]{2,1,0:T(8,128)(2,1)S(1)} %collective-permute-done.10.refs_6_) | copy-start | bytes 884740
  109.4 7.9 %copy-start.7 = (bf16[4,288,128]{2,1,0:T(8,128)(2,1)}, bf16[4,288,128]{2,1,0:T(8,128)(2,1)S(1)}, u32[]{:S(2)}) copy-start(bf16[4,288,128]{2,1,0:T(8,128)(2,1)S(1)} %collective-permute-done.9.refs_5_) | copy-start | bytes 884740
  109.5 7.8 %collective-permute-start.11 = (bf16[4,288,128]{2,1,0:T(8,128)(2,1)S(1)}, bf16[4,288,128]{2,1,0:T(8,128)(2,1)}, u32[]{:S(2)}, u32[]{:S(2)}) collective-permute-start(bf16[4,288,128]{2,1,0:T(8,128)(2,1)S(1)} %broadcast_select_fusion.1), channel_id=1, source_target_pairs={{0,8},{1,57},{8,16},{9,1},{16,24},{17,9},{24,32},{25,17},{32,40},{... | collective-permute-start | bytes 884744 | tf_op jit(solution)/shard_map/ppermute | solution.py:366
  121.9 1.7 collective-permute-start.12
  (8 other events, 9.3 us)
